TPU v7x, 32 devices: a whole 2x2x4 slice. The times are simulated.
32 devices in a mesh: seq: 8 (over y, x, core), head: 4 (over z).
Axes of the slice: x: 2, y: 2, z: 4, core: 2. Of those that a mesh axis runs over, the one named last changes fastest.
Arguments:
- queries: bfloat16 [2048, 2048], P('seq', 'head'), may hold values from -24 to 24
- key_vectors: bfloat16 [2048, 512], P('seq', 'head'), may hold values from -4 to 4
- values: bfloat16 [2048, 512], P('seq', 'head'), may hold values from -6 to 6
- out_proj: bfloat16 [2048, 4096], P('head'), may hold values from -0.125 to 0.125
- grad_out: bfloat16 [2048, 4096], P('seq', 'head'), may hold values from -6 to 6
- windows: int32 [16], P('head'), may hold values from 512 to 1024, as said below
- slab_order: int32 [8], replicated, may hold values from 0 to 7, as said below
Outputs:
- layer_out: bfloat16 [2048, 4096], P('seq', 'head')
- grad_queries: bfloat16 [2048, 2048], P('seq', 'head')
- grad_keys: bfloat16 [2048, 512], P('seq', 'head')
- grad_values: bfloat16 [2048, 512], P('seq', 'head')
Inputs may be any that keep to these rules, and one draw needn't show every extreme that they name: `windows`: some head's window is exactly 1024. slab_order[d] = (d + c) mod 8 for one c with 0 <= c < 8.
All inputs are finite; a program needn't handle non-finite values.
Results may differ from a plain program's by a relative error of at most 0.019.
Values may be sent and summed in bfloat16 or wider, within the bound.
No kernel may reach another device: no remote copies, remote signals or barrier semaphores. Data moves between devices by JAX's collectives and lax.ppermute only.
A program may use at most 128 MiB of HBM per device.

v0:
```python
import jax
import jax.numpy as jnp
from jax import lax
from jax.sharding import PartitionSpec as P

HEAD_DIM = 128


LOWEST = -1e30


def shifted(block, axis, distance):
    devices = range(lax.axis_size(axis))
    route = [((i - distance) % len(devices), i) for i in devices]
    return lax.ppermute(block, axis, route)


def head_scores(block_query, block_key, groups):
    query_heads = block_query.reshape(block_query.shape[0], groups, -1, HEAD_DIM)
    key_heads = block_key.reshape(block_key.shape[0], groups, HEAD_DIM)
    return jnp.einsum(
        "igrd,jgd->grij", query_heads, key_heads, preferred_element_type=jnp.float32
    ) * HEAD_DIM ** (-0.5)


def allowed(query_place, key_place, spans):
    distance = query_place[:, None] - key_place[None, :]
    return (distance >= 0) & (distance < spans[:, :, None, None])


def block_stats(scores, mask):
    peak = jnp.max(jnp.where(mask, scores, LOWEST), -1)
    total = jnp.sum(jnp.exp(jnp.where(mask, scores - peak[..., None], LOWEST)), -1)
    return (peak, total)


def merge_stats(peak, total, new_peak, new_total):
    upper = jnp.maximum(peak, new_peak)
    return (upper, total * jnp.exp(peak - upper) + new_total * jnp.exp(new_peak - upper))


def probabilities(scores, mask, log_norm):
    return jnp.exp(jnp.where(mask, scores - log_norm[..., None], LOWEST))


def weighted_values(probs, block_value, groups):
    value_heads = block_value.reshape(block_value.shape[0], groups, HEAD_DIM)
    mixed = jnp.einsum(
        "grij,jgd->igrd",
        probs.astype(jnp.bfloat16),
        value_heads,
        preferred_element_type=jnp.float32,
    )
    return mixed.reshape(mixed.shape[0], -1)


def row_delta(grad_attn, attention, groups):
    rows = attention.shape[0]
    product = grad_attn.astype(jnp.float32).reshape(rows, groups, -1, HEAD_DIM) * attention.astype(
        jnp.float32
    ).reshape(rows, groups, -1, HEAD_DIM)
    return jnp.transpose(jnp.sum(product, -1), (1, 2, 0))


def block_grads(block_query, block_grad, block_key, block_value, mask, log_norm, delta, groups):
    rows = block_query.shape[0]
    count = block_key.shape[0]
    probs = probabilities(head_scores(block_query, block_key, groups), mask, log_norm)
    query_heads = block_query.reshape(rows, groups, -1, HEAD_DIM)
    grad_heads = block_grad.reshape(rows, groups, -1, HEAD_DIM)
    key_heads = block_key.reshape(count, groups, HEAD_DIM)
    value_heads = block_value.reshape(count, groups, HEAD_DIM)
    grad_prob = jnp.einsum(
        "igrd,jgd->grij", grad_heads, value_heads, preferred_element_type=jnp.float32
    )
    grad_score = (probs * (grad_prob - delta[..., None]) * HEAD_DIM ** (-0.5)).astype(jnp.bfloat16)
    grad_q = jnp.einsum(
        "grij,jgd->igrd", grad_score, key_heads, preferred_element_type=jnp.float32
    ).reshape(rows, -1)
    grad_k = jnp.einsum(
        "grij,igrd->jgd", grad_score, query_heads, preferred_element_type=jnp.float32
    ).reshape(count, -1)
    grad_v = jnp.einsum(
        "grij,igrd->jgd", probs.astype(jnp.bfloat16), grad_heads, preferred_element_type=jnp.float32
    ).reshape(count, -1)
    return (grad_q, grad_k, grad_v)


def body(queries, key_vectors, values, out_proj, grad_out, windows, slab_order):
    rows = queries.shape[0]
    groups = key_vectors.shape[1] // HEAD_DIM
    spans = windows.reshape(groups, -1)
    ratio = spans.shape[1]
    devices = lax.axis_size("seq")
    reach = min(8, devices // 2)
    here = lax.axis_index("seq")
    offsets = jnp.arange(rows, dtype=jnp.int32)

    def place(device):
        return slab_order[jnp.mod(device, devices)] * rows + offsets

    own = place(here)
    grad_attn = lax.dot_general(
        lax.all_gather(grad_out, "head", axis=1, tiled=True),
        out_proj,
        (((1,), (1,)), ((), ())),
        preferred_element_type=jnp.float32,
    ).astype(jnp.bfloat16)
    blocks = [(key_vectors, values, own)]
    for step in range(1, reach + 1):
        near_key, near_value = shifted((key_vectors, values), "seq", step)
        blocks.append((near_key, near_value, place(here - step)))
    masks = [allowed(own, entry[2], spans) for entry in blocks]
    peak = jnp.full((groups, ratio, rows), LOWEST, jnp.float32)
    total = jnp.zeros((groups, ratio, rows), jnp.float32)
    for index in range(reach + 1):
        part_peak, part_total = block_stats(
            head_scores(queries, blocks[index][0], groups), masks[index]
        )
        peak, total = merge_stats(peak, total, part_peak, part_total)
    log_norm = peak + jnp.log(total)
    mixed = jnp.zeros((rows, queries.shape[1]), jnp.float32)
    for index in range(reach + 1):
        probs = probabilities(
            head_scores(queries, blocks[index][0], groups), masks[index], log_norm
        )
        mixed = mixed + weighted_values(probs, blocks[index][1], groups)
    attention = mixed.astype(jnp.bfloat16)
    delta = row_delta(grad_attn, attention, groups)
    grad_q = jnp.zeros((rows, queries.shape[1]), jnp.float32)
    for index in range(reach + 1):
        part_q, part_k, part_v = block_grads(
            queries,
            grad_attn,
            blocks[index][0],
            blocks[index][1],
            masks[index],
            log_norm,
            delta,
            groups,
        )
        grad_q = grad_q + part_q
        if index == 0:
            grad_k, grad_v = (part_k, part_v)
        else:
            back_k, back_v = (
                shifted(part_k.astype(jnp.bfloat16), "seq", -index).astype(part_k.dtype),
                shifted(part_v.astype(jnp.bfloat16), "seq", -index).astype(part_v.dtype),
            )
            grad_k = grad_k + back_k
            grad_v = grad_v + back_v
    share = jnp.dot(attention, out_proj, preferred_element_type=jnp.float32)
    layer_out = lax.psum_scatter(
        share.astype(jnp.bfloat16), "head", scatter_dimension=1, tiled=True
    )
    return (
        layer_out,
        grad_q.astype(jnp.bfloat16),
        grad_k.astype(jnp.bfloat16),
        grad_v.astype(jnp.bfloat16),
    )


def solution(mesh):
    in_specs = (
        P("seq", "head"),
        P("seq", "head"),
        P("seq", "head"),
        P("head", None),
        P("seq", "head"),
        P("head"),
        P(),
    )
    out_specs = (P("seq", "head"), P("seq", "head"), P("seq", "head"), P("seq", "head"))
    return jax.shard_map(body, mesh=mesh, in_specs=in_specs, out_specs=out_specs, check_vma=False)
```

profile of v0, /device:TPU:0, one launch (start us, length us, event | category | flops | bytes accessed | tf_op | source)
XLA Modules:
  0.0 128.7 jit_solution(16631710933322051)
XLA Ops:
  7.2 1.6 %copy.18 = bf16[256,128]{0,1:T(8,128)(2,1)} copy(bf16[256,128]{1,0:T(8,128)(2,1)} %param.9) | data formatting | bytes 131072 | tf_op args[2]
  8.9 3.0 %collective-permute-start.7 = (bf16[256,128]{0,1:T(8,128)(2,1)}, bf16[256,128]{0,1:T(8,128)(2,1)}, u32[]{:S(2)}, u32[]{:S(2)}) collective-permute-start(bf16[256,128]{0,1:T(8,128)(2,1)} %copy.18), channel_id=1, source_target_pairs={{16,0},{20,4},{24,8},{28,12},{0,16},{4,20},{8,24},{12,28},{17,1},{... | collective-permute-start | bytes 196616 | tf_op jit(solution)/shard_map/ppermute | solution.py:15
  11.8 0.7 collective-permute-start.6
  12.5 0.8 collective-permute-start.5
  13.3 0.3 collective-permute-start.4
  13.8 1.0 collective-permute-start
  14.7 1.5 %fusion.128 = (s32[1]{0:T(128)}, s32[1]{0:T(128)}, s32[1]{0:T(128)}, s32[1]{0:T(128)}, s32[1]{0:T(128)}) fusion(s32[8]{0:T(128)} %param.13, s32[]{:T(128)S(6)} %select_n.102, s32[]{:T(128)S(6)} %select_n.96, s32[]{:T(128)S(6)} %select_n.93, s32[]{:T(128)S(6)} %select_n.90, s32[]{:T(128)S(6)} %select_n.99), kind=kLoop, calls=%fused_computation.199 | loop fusion | bytes 60 | tf_op jit(solution)/shard_map/dynamic_slice | solution.py:100
  19.5 0.3 broadcast_compare_fusion
  19.9 0.2 broadcast_subtract_fusion
  20.2 1.2 fusion.4
  21.4 1.6 %collective-permute-start.3 = (bf16[256,128]{1,0:T(8,128)(2,1)}, bf16[256,128]{1,0:T(8,128)(2,1)S(1)}, u32[]{:S(2)}, u32[]{:S(2)}) collective-permute-start(bf16[256,128]{1,0:T(8,128)(2,1)} %param.8), channel_id=1, source_target_pairs={{16,0},{20,4},{24,8},{28,12},{0,16},{4,20},{8,24},{12,28},{17,1},{... | collective-permute-start | bytes 196616 | tf_op jit(solution)/shard_map/ppermute | solution.py:15
  23.0 1.3 %select_reduce_fusion.3 = (f32[4,256]{1,0:T(4,128)S(1)}, f32[4,256]{1,0:T(4,128)S(1)}, f32[1,4,256,256]{2,3,1,0:T(8,128)S(1)}) fusion(s32[256,256]{0,1:T(8,128)S(1)} %get-tuple-element.32, pred[256,256]{0,1:T(8,128)(4,1)S(1)} %get-tuple-element.26, s32[4]{0:T(128)} %param.12, f32[1,4,256,256]{2,3,1,0:T(8,128)S(1)} %fusion.4, ...), kind=kOutput, calls=%fused_computation.87 | convolution fusion | flops 69466112 | bytes 3088400 | tf_op jit(solution)/shard_map/igrd,jgd->grij/dot_general | solution.py:21
  24.4 2.0 %collective-permute-done.3 = bf16[256,128]{1,0:T(8,128)(2,1)S(1)} collective-permute-done((bf16[256,128]{1,0:T(8,128)(2,1)}, bf16[256,128]{1,0:T(8,128)(2,1)S(1)}, u32[]{:S(2)}, u32[]{:S(2)}) %collective-permute-start.3) | collective-permute-done | bytes 65568 | tf_op jit(solution)/shard_map/ppermute | solution.py:15
  26.4 1.0 collective-permute-start.2
  27.4 0.3 fusion
  27.7 2.4 %collective-permute-done.2 = bf16[256,128]{1,0:T(8,128)(2,1)S(1)} collective-permute-done((bf16[256,128]{1,0:T(8,128)(2,1)S(1)}, bf16[256,128]{1,0:T(8,128)(2,1)S(1)}, u32[]{:S(2)}, u32[]{:S(2)}) %collective-permute-start.2) | collective-permute-done | bytes 65568 | tf_op jit(solution)/shard_map/ppermute | solution.py:15
  30.1 1.5 %collective-permute-start.1 = (bf16[256,128]{1,0:T(8,128)(2,1)S(1)}, bf16[256,128]{1,0:T(8,128)(2,1)S(1)}, u32[]{:S(2)}, u32[]{:S(2)}) collective-permute-start(bf16[256,128]{1,0:T(8,128)(2,1)S(1)} %copy-done.25), channel_id=1, source_target_pairs={{24,0},{28,4},{0,8},{4,12},{8,16},{12,20},{16,24},{20,28},{25,1},{... | collective-permute-start | bytes 196616 | tf_op jit(solution)/shard_map/ppermute | solution.py:15
  31.6 0.3 fusion.1
  31.9 3.8 %collective-permute-done.1 = bf16[256,128]{1,0:T(8,128)(2,1)S(1)} collective-permute-done((bf16[256,128]{1,0:T(8,128)(2,1)S(1)}, bf16[256,128]{1,0:T(8,128)(2,1)S(1)}, u32[]{:S(2)}, u32[]{:S(2)}) %collective-permute-start.1) | collective-permute-done | bytes 65568 | tf_op jit(solution)/shard_map/ppermute | solution.py:15
  35.7 1.6 %exponential_reduce_fusion.3 = (f32[4,256]{1,0:T(4,128)S(1)}, f32[4,256]{1,0:T(4,128)S(1)}, f32[4,256]{1,0:T(4,128)S(1)}, f32[4,256]{1,0:T(4,128)S(1)}, f32[4,256]{1,0:T(4,128)S(1)}, /*index=5*/f32[1,4,256,256]{2,3,1,0:T(8,128)S(1)}) fusion(f32[1,4,256,256]{2,3,1,0:T(8,128)S(1)} %get-tuple-element.38, f32[4,256]{1,0:T(4,128)S(1)} %get-tuple-element.13, ...), kind=kOutput, calls=%fused_computation.82 | convolution fusion | flops 73133056 | bytes 7237648 | tf_op jit(solution)/shard_map/igrd,jgd->grij/dot_general | solution.py:21
  37.3 1.0 exponential_reduce_fusion.2
  38.5 2.4 %fusion.55 = (bf16[4,256,256]{1,2,0:T(8,128)(2,1)}, bf16[4,256,256]{1,2,0:T(8,128)(2,1)S(1)}, bf16[4,256,256]{1,2,0:T(8,128)(2,1)S(1)}, bf16[4,256,256]{1,2,0:T(8,128)(2,1)S(1)}, bf16[4,256,256]{1,2,0:T(8,128)(2,1)S(1)}) fusion(f32[1,4,256,256]{2,3,1,0:T(8,128)S(1)} %get-tuple-element.39, f32[4,256]{1,0:T(4,128)S(1)} %log_add_fusion, ...), kind=kLoop, calls=%fused_computation.101 | loop fusion | flops 6553600 | bytes 9506832 | tf_op jit(solution)/shard_map/reshape.41
  40.9 0.3 fusion.79
  41.2 2.0 %fusion.72 = f32[4,256,128]{1,2,0:T(8,128)} fusion(bf16[4,256,256]{1,2,0:T(8,128)(2,1)S(1)} %get-tuple-element.20, bf16[256,128]{0,1:T(8,128)(2,1)} %collective-permute-done.6), kind=kOutput, calls=%fused_computation.131 | convolution fusion | flops 67108864 | bytes 1114112 | tf_op jit(solution)/shard_map/grij,jgd->igrd/dot_general | solution.py:48
  43.2 1.9 %fusion.69 = f32[4,256,128]{1,2,0:T(8,128)} fusion(bf16[4,256,256]{1,2,0:T(8,128)(2,1)S(1)} %get-tuple-element.21, bf16[256,128]{0,1:T(8,128)(2,1)} %collective-permute-done.7), kind=kOutput, calls=%fused_computation.128 | convolution fusion | flops 67108864 | bytes 1114112 | tf_op jit(solution)/shard_map/grij,jgd->igrd/dot_general | solution.py:48
  45.1 1.9 %convolution_add_fusion.1 = f32[4,256,128]{1,2,0:T(8,128)} fusion(f32[4,256,128]{1,2,0:T(8,128)S(1)} %fusion.79, bf16[4,256,256]{1,2,0:T(8,128)(2,1)S(1)} %get-tuple-element.19, bf16[256,128]{0,1:T(8,128)(2,1)} %collective-permute-done.4), kind=kOutput, calls=%fused_computation.44 | convolution fusion | flops 67239936 | bytes 1638400 | tf_op jit(solution)/shard_map/grij,jgd->igrd/dot_general | solution.py:48
  47.0 13.7 %all-gather.2.cloned.1.call-done = bf16[256,4096]{1,0:T(8,128)(2,1)} async-done(((bf16[256,1024]{1,0:T(8,128)(2,1)}), bf16[256,4096]{1,0:T(8,128)(2,1)}) %all-gather.2.cloned.1.call-update) | async-done | bytes 2097168 | tf_op jit(solution)/shard_map/all_gather | solution.py:104
  60.7 4.8 %convolution_convert_fusion.1 = bf16[256,512]{1,0:T(8,128)(2,1)} fusion(bf16[256,4096]{1,0:T(8,128)(2,1)} %all-gather.2.cloned.1.call-done, bf16[512,4096]{1,0:T(8,128)(2,1)} %param.10), kind=kOutput, calls=%fused_computation.51 | convolution fusion | flops 1073872896 | bytes 6553600 | tf_op jit(solution)/shard_map/dot_general | solution.py:103
  65.5 1.1 copy.108
  66.6 2.0 %fusion.47 = bf16[256,128]{0,1:T(8,128)(2,1)} fusion(bf16[256,4,128]{0,2,1:T(8,128)(2,1)S(1)} %bitcast.380, bf16[4,256,256]{1,2,0:T(8,128)(2,1)} %copy-done.3), kind=kOutput, calls=%fused_computation.73 | convolution fusion | flops 67141632 | bytes 851968 | tf_op jit(solution)/shard_map/grij,igrd->jgd/dot_general | solution.py:83
  68.6 2.0 %fusion.45 = bf16[256,128]{0,1:T(8,128)(2,1)} fusion(bf16[256,4,128]{0,2,1:T(8,128)(2,1)S(1)} %bitcast.381, bf16[4,256,256]{1,2,0:T(8,128)(2,1)} %copy-done.2), kind=kOutput, calls=%fused_computation.71 | convolution fusion | flops 67141632 | bytes 851968 | tf_op jit(solution)/shard_map/grij,igrd->jgd/dot_general | solution.py:83
  70.6 1.9 %copy.28 = f32[256,512]{0,1:T(8,128)} copy(bf16[256,512]{1,0:T(8,128)(2,1)} %convolution_convert_fusion.1) | data formatting | bytes 786432 | tf_op jit(solution)/shard_map/reshape | solution.py:59
  72.4 2.0 %multiply_reduce_fusion = (f32[256,4]{0,1:T(4,128)S(1)}, bf16[4,256,128]{1,2,0:T(8,128)(2,1)S(1)}) fusion(f32[256,1,4,128]{0,3,2,1:T(8,128)} %bitcast.390, f32[4,256,128]{1,2,0:T(8,128)} %fusion.69, f32[4,256,128]{1,2,0:T(8,128)} %fusion.72, f32[4,256,128]{1,2,0:T(8,128)} %convolution_add_fusion.1, bf16[4,256,256]{1,2,0:T(8,128)(2,1)} %get-tuple-element.18, ...), kind=kOutput, calls=%fused_computation.104 | convolution fusion | flops 68025344 | bytes 2953216 | tf_op jit(solution)/shard_map/grij,jgd->igrd/dot_general | solution.py:48
  74.4 4.8 %convolution_convert_fusion = bf16[256,4096]{1,0:T(8,128)(2,1)} fusion(bf16[256,512]{0,1:T(8,128)(2,1)S(1)} %bitcast.391, bf16[512,4096]{1,0:T(8,128)(2,1)} %param.10), kind=kOutput, calls=%fused_computation | convolution fusion | flops 1074790400 | bytes 6553600 | tf_op jit(solution)/shard_map/dot_general | solution.py:152
  79.3 2.1 %fusion.44 = bf16[256,128]{0,1:T(8,128)(2,1)} fusion(bf16[256,4,128]{0,2,1:T(8,128)(2,1)S(1)} %bitcast.382, bf16[4,256,256]{1,2,0:T(8,128)(2,1)} %copy-done.1), kind=kOutput, calls=%fused_computation.70 | convolution fusion | flops 67141632 | bytes 851968 | tf_op jit(solution)/shard_map/grij,igrd->jgd/dot_general | solution.py:83
  81.5 1.5 %collective-permute-start.15 = (bf16[256,128]{0,1:T(8,128)(2,1)}, bf16[256,128]{0,1:T(8,128)(2,1)}, u32[]{:S(2)}, u32[]{:S(2)}) collective-permute-start(bf16[256,128]{0,1:T(8,128)(2,1)} %fusion.44), channel_id=1, source_target_pairs={{16,0},{20,4},{24,8},{28,12},{0,16},{4,20},{8,24},{12,28},{17,1},{... | collective-permute-start | bytes 196616 | tf_op jit(solution)/shard_map/ppermute | solution.py:15
  83.0 1.7 %collective-permute-start.12 = (bf16[256,128]{0,1:T(8,128)(2,1)}, bf16[256,128]{0,1:T(8,128)(2,1)}, u32[]{:S(2)}, u32[]{:S(2)}) collective-permute-start(bf16[256,128]{0,1:T(8,128)(2,1)} %fusion.47), channel_id=1, source_target_pairs={{4,0},{8,4},{12,8},{16,12},{20,16},{24,20},{28,24},{0,28},{5,1},{9... | collective-permute-start | bytes 196616 | tf_op jit(solution)/shard_map/ppermute | solution.py:15
  84.7 2.0 %fusion.46 = bf16[256,128]{0,1:T(8,128)(2,1)} fusion(bf16[256,4,128]{0,2,1:T(8,128)(2,1)S(1)} %bitcast.383, bf16[4,256,256]{1,2,0:T(8,128)(2,1)} %get-tuple-element.18), kind=kOutput, calls=%fused_computation.72 | convolution fusion | flops 67141632 | bytes 851968 | tf_op jit(solution)/shard_map/grij,igrd->jgd/dot_general | solution.py:83
  86.7 2.4 %collective-permute-start.13 = (bf16[256,128]{0,1:T(8,128)(2,1)}, bf16[256,128]{0,1:T(8,128)(2,1)}, u32[]{:S(2)}, u32[]{:S(2)}) collective-permute-start(bf16[256,128]{0,1:T(8,128)(2,1)} %fusion.46), channel_id=1, source_target_pairs={{8,0},{12,4},{16,8},{20,12},{24,16},{28,20},{0,24},{4,28},{9,1},{1... | collective-permute-start | bytes 196616 | tf_op jit(solution)/shard_map/ppermute | solution.py:15
  89.0 1.9 %fusion.25 = bf16[4,256,256]{1,2,0:T(8,128)(2,1)S(1)} fusion(bf16[256,4,128]{0,2,1:T(8,128)(2,1)S(1)} %bitcast.384, f32[1,4,256,256]{2,3,1,0:T(8,128)} %copy-done.14, f32[4,256]{1,0:T(4,128)S(1)} %bitcast.393, f32[4,256]{1,0:T(4,128)S(1)} %log_add_fusion, s32[256,256]{0,1:T(8,128)} %copy-done.17, pred[256,256]{0,1:T(8,128)(4,1)} %copy-done.22, ...), kind=kOutput, calls=%fused_computation.36 | convolution fusion | flops 69206016 | bytes 2236432 | tf_op jit(solution)/shard_map/igrd,jgd->grij/dot_general | solution.py:73
  90.9 0.9 fusion.36
  91.9 0.5 fusion.29
  92.4 1.5 %fusion.26 = bf16[4,256,256]{1,2,0:T(8,128)(2,1)S(1)} fusion(bf16[256,4,128]{0,2,1:T(8,128)(2,1)S(1)} %bitcast.386, f32[1,4,256,256]{2,3,1,0:T(8,128)S(1)} %copy-done.7, f32[4,256]{1,0:T(4,128)S(1)} %bitcast.395, f32[4,256]{1,0:T(4,128)S(1)} %log_add_fusion, s32[256,256]{0,1:T(8,128)S(1)} %copy-done.11, pred[256,256]{0,1:T(8,128)(4,1)S(1)} %copy-done.19, ...), kind=kOutput, calls=%fused_computation.37 | convolution fusion | flops 69206016 | bytes 2236432 | tf_op jit(solution)/shard_map/igrd,jgd->grij/dot_general | solution.py:73
  93.9 1.4 %fusion.27 = bf16[4,256,256]{1,2,0:T(8,128)(2,1)S(1)} fusion(bf16[256,4,128]{0,2,1:T(8,128)(2,1)S(1)} %bitcast.387, f32[1,4,256,256]{2,3,1,0:T(8,128)S(1)} %fusion.1, f32[4,256]{1,0:T(4,128)S(1)} %bitcast.396, f32[4,256]{1,0:T(4,128)S(1)} %log_add_fusion, s32[256,256]{0,1:T(8,128)S(1)} %copy-done.9, pred[256,256]{0,1:T(8,128)(4,1)S(1)} %get-tuple-element.24, ...), kind=kOutput, calls=%fused_computation.38 | convolution fusion | flops 69206016 | bytes 2236432 | tf_op jit(solution)/shard_map/igrd,jgd->grij/dot_general | solution.py:73
  95.4 1.4 %fusion.28 = bf16[4,256,256]{1,2,0:T(8,128)(2,1)S(1)} fusion(bf16[256,4,128]{0,2,1:T(8,128)(2,1)S(1)} %bitcast.388, f32[1,4,256,256]{2,3,1,0:T(8,128)S(1)} %fusion, f32[4,256]{1,0:T(4,128)S(1)} %bitcast.397, f32[4,256]{1,0:T(4,128)S(1)} %log_add_fusion, s32[256,256]{0,1:T(8,128)S(1)} %get-tuple-element.28, pred[256,256]{0,1:T(8,128)(4,1)S(1)} %get-tuple-element.23, ...), kind=kOutput, calls=%fused_computation.39 | convolution fusion | flops 69206016 | bytes 2236432 | tf_op jit(solution)/shard_map/igrd,jgd->grij/dot_general | solution.py:73
  96.8 0.3 fusion.39
  97.1 0.3 fusion.38
  97.4 0.3 fusion.37
  97.7 0.3 fusion.91
  98.0 0.3 fusion.81
  98.3 0.3 fusion.84
  98.5 0.3 convolution_add_fusion.3
  98.8 0.3 fusion.34
  99.1 0.8 copy.66
  100.0 0.6 collective-permute-start.9
  100.6 0.4 collective-permute-start.10
  100.9 1.5 %collective-permute-start.11 = (bf16[256,128]{1,0:T(8,128)(2,1)S(1)}, bf16[256,128]{1,0:T(8,128)(2,1)S(1)}, u32[]{:S(2)}, u32[]{:S(2)}) collective-permute-start(bf16[256,128]{1,0:T(8,128)(2,1)S(1)} %fusion.39), channel_id=1, source_target_pairs={{16,0},{20,4},{24,8},{28,12},{0,16},{4,20},{8,24},{12,28},{17,1},{... | collective-permute-start | bytes 196616 | tf_op jit(solution)/shard_map/ppermute | solution.py:15
  102.4 1.2 add_convert_fusion
  103.7 0.7 copy.67
  104.4 0.5 collective-permute-done.9
  104.9 0.2 collective-permute-done.10
  105.2 0.8 collective-permute-done.11
  105.9 1.8 %add_convert_fusion.1 = bf16[256,128]{1,0:T(8,128)(2,1)} fusion(bf16[256,128]{1,0:T(8,128)(2,1)S(1)} %collective-permute-done.11, bf16[256,128]{1,0:T(8,128)(2,1)S(1)} %collective-permute-done.10, bf16[256,128]{1,0:T(8,128)(2,1)S(1)} %collective-permute-done.9, bf16[256,128]{1,0:T(8,128)(2,1)} %collective-permute-done.8, ...), kind=kOutput, calls=%fused_computation.116 | convolution fusion | flops 67403776 | bytes 1114112 | tf_op jit(solution)/shard_map/grij,igrd->jgd/dot_general | solution.py:80
  107.7 14.2 %reduce-scatter.2.cloned.1.call-done = bf16[256,1024]{1,0:T(8,128)(2,1)} async-done(((bf16[256,4096]{1,0:T(8,128)(2,1)}), bf16[256,1024]{1,0:T(8,128)(2,1)}) %reduce-scatter.2.cloned.1.call-update) | async-done | bytes 524304 | tf_op jit(solution)/shard_map/reduce_scatter | solution.py:153
  (92 shorter events, 0.4 us)
Async XLA Ops:
  7.2 13.0 %copy-start = (bf16[256,512]{1,0:T(8,128)(2,1)S(1)}, bf16[256,512]{1,0:T(8,128)(2,1)}, u32[]{:S(2)}) copy-start(bf16[256,512]{1,0:T(8,128)(2,1)} %param.7) | copy-start | bytes 786436
  7.2 19.2 %copy-start.25 = (bf16[256,128]{1,0:T(8,128)(2,1)S(1)}, bf16[256,128]{1,0:T(8,128)(2,1)}, u32[]{:S(2)}) copy-start(bf16[256,128]{1,0:T(8,128)(2,1)} %param.8) | copy-start | bytes 196612
  7.2 53.5 %all-gather.2.cloned.1.call-start = ((), (), s32[]{:S(2)}) async-start(), calls=%async_computation.2 | async-start | bytes 2621440 | tf_op jit(solution)/shard_map/all_gather | solution.py:104
  8.9 34.3 %collective-permute-start.7 = (bf16[256,128]{0,1:T(8,128)(2,1)}, bf16[256,128]{0,1:T(8,128)(2,1)}, u32[]{:S(2)}, u32[]{:S(2)}) collective-permute-start(bf16[256,128]{0,1:T(8,128)(2,1)} %copy.18), channel_id=1, source_target_pairs={{16,0},{20,4},{24,8},{28,12},{0,16},{4,20},{8,24},{12,28},{17,1},{... | collective-permute-start | bytes 196616 | tf_op jit(solution)/shard_map/ppermute | solution.py:15
  11.8 29.4 %collective-permute-start.6 = (bf16[256,128]{0,1:T(8,128)(2,1)}, bf16[256,128]{0,1:T(8,128)(2,1)}, u32[]{:S(2)}, u32[]{:S(2)}) collective-permute-start(bf16[256,128]{0,1:T(8,128)(2,1)} %copy.18), channel_id=1, source_target_pairs={{20,0},{24,4},{28,8},{0,12},{4,16},{8,20},{12,24},{16,28},{21,1},{... | collective-permute-start | bytes 196616 | tf_op jit(solution)/shard_map/ppermute | solution.py:15
  12.5 59.9 %collective-permute-start.5 = (bf16[256,128]{0,1:T(8,128)(2,1)}, bf16[256,128]{0,1:T(8,128)(2,1)}, u32[]{:S(2)}, u32[]{:S(2)}) collective-permute-start(bf16[256,128]{0,1:T(8,128)(2,1)} %copy.18), channel_id=1, source_target_pairs={{24,0},{28,4},{0,8},{4,12},{8,16},{12,20},{16,24},{20,28},{25,1},{... | collective-permute-start | bytes 196616 | tf_op jit(solution)/shard_map/ppermute | solution.py:15
  13.3 31.7 %collective-permute-start.4 = (bf16[256,128]{0,1:T(8,128)(2,1)}, bf16[256,128]{0,1:T(8,128)(2,1)}, u32[]{:S(2)}, u32[]{:S(2)}) collective-permute-start(bf16[256,128]{0,1:T(8,128)(2,1)} %copy.18), channel_id=1, source_target_pairs={{28,0},{0,4},{4,8},{8,12},{12,16},{16,20},{20,24},{24,28},{29,1},{... | collective-permute-start | bytes 196616 | tf_op jit(solution)/shard_map/ppermute | solution.py:15
  13.7 108.1 %reduce-scatter.2.cloned.1.call-start = ((), (), s32[]{:S(2)}) async-start(), calls=%async_computation.1 | async-start | bytes 2621440 | tf_op jit(solution)/shard_map/reduce_scatter | solution.py:153
  13.8 7.6 %collective-permute-start = (bf16[256,128]{1,0:T(8,128)(2,1)}, bf16[256,128]{1,0:T(8,128)(2,1)S(1)}, u32[]{:S(2)}, u32[]{:S(2)}) collective-permute-start(bf16[256,128]{1,0:T(8,128)(2,1)} %param.8), channel_id=1, source_target_pairs={{28,0},{0,4},{4,8},{8,12},{12,16},{16,20},{20,24},{24,28},{29,1},{... | collective-permute-start | bytes 196616 | tf_op jit(solution)/shard_map/ppermute | solution.py:15
  19.8 18.5 %copy-start.18 = (pred[256,256]{0,1:T(8,128)(4,1)}, pred[256,256]{0,1:T(8,128)(4,1)S(1)}, u32[]{:S(2)}) copy-start(pred[256,256]{0,1:T(8,128)(4,1)S(1)} %get-tuple-element.25) | copy-start | bytes 196612
  19.8 18.5 %copy-start.20 = (pred[256,256]{0,1:T(8,128)(4,1)}, pred[256,256]{0,1:T(8,128)(4,1)S(1)}, u32[]{:S(2)}) copy-start(pred[256,256]{0,1:T(8,128)(4,1)S(1)} %get-tuple-element.27) | copy-start | bytes 196612
  19.9 18.5 %copy-start.22 = (pred[256,256]{0,1:T(8,128)(4,1)}, pred[256,256]{0,1:T(8,128)(4,1)S(1)}, u32[]{:S(2)}) copy-start(pred[256,256]{0,1:T(8,128)(4,1)S(1)} %get-tuple-element.26) | copy-start | bytes 196612
  19.9 15.8 %copy-start.35 = (s32[4]{0:T(128)S(1)}, s32[4]{0:T(128)}, u32[]{:S(2)}) copy-start(s32[4]{0:T(128)} %param.12) | copy-start | bytes 52
  20.1 18.3 %copy-start.8 = (s32[256,256]{0,1:T(8,128)}, s32[256,256]{0,1:T(8,128)S(1)}, u32[]{:S(2)}) copy-start(s32[256,256]{0,1:T(8,128)S(1)} %get-tuple-element.30) | copy-start | bytes 786436
  20.1 18.3 %copy-start.10 = (s32[256,256]{0,1:T(8,128)}, s32[256,256]{0,1:T(8,128)S(1)}, u32[]{:S(2)}) copy-start(s32[256,256]{0,1:T(8,128)S(1)} %get-tuple-element.29) | copy-start | bytes 786436
  20.1 18.3 %copy-start.15 = (s32[256,256]{0,1:T(8,128)}, s32[256,256]{0,1:T(8,128)S(1)}, u32[]{:S(2)}) copy-start(s32[256,256]{0,1:T(8,128)S(1)} %get-tuple-element.31) | copy-start | bytes 786436
  20.2 18.3 %copy-start.17 = (s32[256,256]{0,1:T(8,128)}, s32[256,256]{0,1:T(8,128)S(1)}, u32[]{:S(2)}) copy-start(s32[256,256]{0,1:T(8,128)S(1)} %get-tuple-element.32) | copy-start | bytes 786436
  21.4 17.0 %copy-start.4 = (f32[1,4,256,256]{2,3,1,0:T(8,128)}, f32[1,4,256,256]{2,3,1,0:T(8,128)S(1)}, u32[]{:S(2)}) copy-start(f32[1,4,256,256]{2,3,1,0:T(8,128)S(1)} %fusion.4) | copy-start | bytes 3145732
  21.4 2.9 %copy-start.31 = (bf16[256,128]{1,0:T(8,128)(2,1)}, bf16[256,128]{1,0:T(8,128)(2,1)S(1)}, u32[]{:S(2)}) copy-start(bf16[256,128]{1,0:T(8,128)(2,1)S(1)} %collective-permute-done) | copy-start | bytes 196612
  21.4 5.0 %collective-permute-start.3 = (bf16[256,128]{1,0:T(8,128)(2,1)}, bf16[256,128]{1,0:T(8,128)(2,1)S(1)}, u32[]{:S(2)}, u32[]{:S(2)}) collective-permute-start(bf16[256,128]{1,0:T(8,128)(2,1)} %param.8), channel_id=1, source_target_pairs={{16,0},{20,4},{24,8},{28,12},{0,16},{4,20},{8,24},{12,28},{17,1},{... | collective-permute-start | bytes 196616 | tf_op jit(solution)/shard_map/ppermute | solution.py:15
  24.3 14.1 %copy-start.14 = (f32[1,4,256,256]{2,3,1,0:T(8,128)}, f32[1,4,256,256]{2,3,1,0:T(8,128)S(1)}, u32[]{:S(2)}) copy-start(f32[1,4,256,256]{2,3,1,0:T(8,128)S(1)} %get-tuple-element.38) | copy-start | bytes 3145732
  26.4 10.8 %copy-start.27 = (bf16[256,128]{1,0:T(8,128)(2,1)}, bf16[256,128]{1,0:T(8,128)(2,1)S(1)}, u32[]{:S(2)}) copy-start(bf16[256,128]{1,0:T(8,128)(2,1)S(1)} %collective-permute-done.3) | copy-start | bytes 196612
  26.4 3.7 %collective-permute-start.2 = (bf16[256,128]{1,0:T(8,128)(2,1)S(1)}, bf16[256,128]{1,0:T(8,128)(2,1)S(1)}, u32[]{:S(2)}, u32[]{:S(2)}) collective-permute-start(bf16[256,128]{1,0:T(8,128)(2,1)S(1)} %copy-done.25), channel_id=1, source_target_pairs={{20,0},{24,4},{28,8},{0,12},{4,16},{8,20},{12,24},{16,28},{21,1},{... | collective-permute-start | bytes 196616 | tf_op jit(solution)/shard_map/ppermute | solution.py:15
  30.1 7.2 %copy-start.29 = (bf16[256,128]{1,0:T(8,128)(2,1)}, bf16[256,128]{1,0:T(8,128)(2,1)S(1)}, u32[]{:S(2)}) copy-start(bf16[256,128]{1,0:T(8,128)(2,1)S(1)} %collective-permute-done.2) | copy-start | bytes 196612
  30.1 5.6 %collective-permute-start.1 = (bf16[256,128]{1,0:T(8,128)(2,1)S(1)}, bf16[256,128]{1,0:T(8,128)(2,1)S(1)}, u32[]{:S(2)}, u32[]{:S(2)}) collective-permute-start(bf16[256,128]{1,0:T(8,128)(2,1)S(1)} %copy-done.25), channel_id=1, source_target_pairs={{24,0},{28,4},{0,8},{4,12},{8,16},{12,20},{16,24},{20,28},{25,1},{... | collective-permute-start | bytes 196616 | tf_op jit(solution)/shard_map/ppermute | solution.py:15
  35.7 1.6 %copy-start.33 = (bf16[256,128]{1,0:T(8,128)(2,1)}, bf16[256,128]{1,0:T(8,128)(2,1)S(1)}, u32[]{:S(2)}) copy-start(bf16[256,128]{1,0:T(8,128)(2,1)S(1)} %collective-permute-done.1) | copy-start | bytes 196612
  37.3 3.6 %copy-start.6 = (f32[1,4,256,256]{2,3,1,0:T(8,128)}, f32[1,4,256,256]{2,3,1,0:T(8,128)S(1)}, u32[]{:S(2)}) copy-start(f32[1,4,256,256]{2,3,1,0:T(8,128)S(1)} %get-tuple-element.39) | copy-start | bytes 3145732
  38.5 2.5 %copy-start.23 = (bf16[256,128]{1,0:T(8,128)(2,1)S(1)}, bf16[256,128]{1,0:T(8,128)(2,1)}, u32[]{:S(2)}) copy-start(bf16[256,128]{1,0:T(8,128)(2,1)} %param.9) | copy-start | bytes 196612
  40.9 2.3 %copy-start.1 = (bf16[4,256,256]{1,2,0:T(8,128)(2,1)}, bf16[4,256,256]{1,2,0:T(8,128)(2,1)S(1)}, u32[]{:S(2)}) copy-start(bf16[4,256,256]{1,2,0:T(8,128)(2,1)S(1)} %get-tuple-element.21) | copy-start | bytes 1572868
  40.9 4.2 %copy-start.2 = (bf16[4,256,256]{1,2,0:T(8,128)(2,1)}, bf16[4,256,256]{1,2,0:T(8,128)(2,1)S(1)}, u32[]{:S(2)}) copy-start(bf16[4,256,256]{1,2,0:T(8,128)(2,1)S(1)} %get-tuple-element.20) | copy-start | bytes 1572868
  40.9 4.2 %copy-start.3 = (bf16[4,256,256]{1,2,0:T(8,128)(2,1)}, bf16[4,256,256]{1,2,0:T(8,128)(2,1)S(1)}, u32[]{:S(2)}) copy-start(bf16[4,256,256]{1,2,0:T(8,128)(2,1)S(1)} %get-tuple-element.19) | copy-start | bytes 1572868
  79.3 12.6 %copy-start.5 = (f32[1,4,256,256]{2,3,1,0:T(8,128)S(1)}, f32[1,4,256,256]{2,3,1,0:T(8,128)}, u32[]{:S(2)}) copy-start(f32[1,4,256,256]{2,3,1,0:T(8,128)} %copy-done.4) | copy-start | bytes 3145732
  79.3 12.6 %copy-start.16 = (s32[256,256]{0,1:T(8,128)S(1)}, s32[256,256]{0,1:T(8,128)}, u32[]{:S(2)}) copy-start(s32[256,256]{0,1:T(8,128)} %copy-done.15) | copy-start | bytes 786436
  79.3 12.6 %copy-start.21 = (pred[256,256]{0,1:T(8,128)(4,1)S(1)}, pred[256,256]{0,1:T(8,128)(4,1)}, u32[]{:S(2)}) copy-start(pred[256,256]{0,1:T(8,128)(4,1)} %copy-done.20) | copy-start | bytes 196612
  79.3 12.6 %copy-start.24 = (bf16[256,128]{1,0:T(8,128)(2,1)S(1)}, bf16[256,128]{1,0:T(8,128)(2,1)}, u32[]{:S(2)}) copy-start(bf16[256,128]{1,0:T(8,128)(2,1)} %param.9) | copy-start | bytes 196612
  79.3 13.1 %copy-start.7 = (f32[1,4,256,256]{2,3,1,0:T(8,128)S(1)}, f32[1,4,256,256]{2,3,1,0:T(8,128)}, u32[]{:S(2)}) copy-start(f32[1,4,256,256]{2,3,1,0:T(8,128)} %copy-done.6) | copy-start | bytes 3145732
  79.3 13.1 %copy-start.11 = (s32[256,256]{0,1:T(8,128)S(1)}, s32[256,256]{0,1:T(8,128)}, u32[]{:S(2)}) copy-start(s32[256,256]{0,1:T(8,128)} %copy-done.10) | copy-start | bytes 786436
  79.3 13.1 %copy-start.19 = (pred[256,256]{0,1:T(8,128)(4,1)S(1)}, pred[256,256]{0,1:T(8,128)(4,1)}, u32[]{:S(2)}) copy-start(pred[256,256]{0,1:T(8,128)(4,1)} %copy-done.18) | copy-start | bytes 196612
  81.5 18.5 %collective-permute-start.15 = (bf16[256,128]{0,1:T(8,128)(2,1)}, bf16[256,128]{0,1:T(8,128)(2,1)}, u32[]{:S(2)}, u32[]{:S(2)}) collective-permute-start(bf16[256,128]{0,1:T(8,128)(2,1)} %fusion.44), channel_id=1, source_target_pairs={{16,0},{20,4},{24,8},{28,12},{0,16},{4,20},{8,24},{12,28},{17,1},{... | collective-permute-start | bytes 196616 | tf_op jit(solution)/shard_map/ppermute | solution.py:15
  83.0 17.6 %collective-permute-start.14 = (bf16[256,128]{0,1:T(8,128)(2,1)}, bf16[256,128]{0,1:T(8,128)(2,1)}, u32[]{:S(2)}, u32[]{:S(2)}) collective-permute-start(bf16[256,128]{0,1:T(8,128)(2,1)} %fusion.45), channel_id=1, source_target_pairs={{12,0},{16,4},{20,8},{24,12},{28,16},{0,20},{4,24},{8,28},{13,1},{... | collective-permute-start | bytes 196616 | tf_op jit(solution)/shard_map/ppermute | solution.py:15
  83.0 18.0 %collective-permute-start.12 = (bf16[256,128]{0,1:T(8,128)(2,1)}, bf16[256,128]{0,1:T(8,128)(2,1)}, u32[]{:S(2)}, u32[]{:S(2)}) collective-permute-start(bf16[256,128]{0,1:T(8,128)(2,1)} %fusion.47), channel_id=1, source_target_pairs={{4,0},{8,4},{12,8},{16,12},{20,16},{24,20},{28,24},{0,28},{5,1},{9... | collective-permute-start | bytes 196616 | tf_op jit(solution)/shard_map/ppermute | solution.py:15
  86.7 15.8 %collective-permute-start.13 = (bf16[256,128]{0,1:T(8,128)(2,1)}, bf16[256,128]{0,1:T(8,128)(2,1)}, u32[]{:S(2)}, u32[]{:S(2)}) collective-permute-start(bf16[256,128]{0,1:T(8,128)(2,1)} %fusion.46), channel_id=1, source_target_pairs={{8,0},{12,4},{16,8},{20,12},{24,16},{28,20},{0,24},{4,28},{9,1},{1... | collective-permute-start | bytes 196616 | tf_op jit(solution)/shard_map/ppermute | solution.py:15
  89.0 4.9 %copy-start.9 = (s32[256,256]{0,1:T(8,128)S(1)}, s32[256,256]{0,1:T(8,128)}, u32[]{:S(2)}) copy-start(s32[256,256]{0,1:T(8,128)} %copy-done.8) | copy-start | bytes 786436
  91.8 12.6 %collective-permute-start.8 = (bf16[256,128]{1,0:T(8,128)(2,1)}, bf16[256,128]{1,0:T(8,128)(2,1)}, u32[]{:S(2)}, u32[]{:S(2)}) collective-permute-start(bf16[256,128]{1,0:T(8,128)(2,1)} %fusion.36), channel_id=1, source_target_pairs={{4,0},{8,4},{12,8},{16,12},{20,16},{24,20},{28,24},{0,28},{5,1},{9... | collective-permute-start | bytes 196616 | tf_op jit(solution)/shard_map/ppermute | solution.py:15
  92.4 5.3 %copy-start.12 = (bf16[4,256,256]{1,2,0:T(8,128)(2,1)}, bf16[4,256,256]{1,2,0:T(8,128)(2,1)S(1)}, u32[]{:S(2)}) copy-start(bf16[4,256,256]{1,2,0:T(8,128)(2,1)S(1)} %fusion.29) | copy-start | bytes 1572868
  93.9 3.8 %copy-start.26 = (bf16[256,128]{1,0:T(8,128)(2,1)S(1)}, bf16[256,128]{1,0:T(8,128)(2,1)}, u32[]{:S(2)}) copy-start(bf16[256,128]{1,0:T(8,128)(2,1)} %param.8) | copy-start | bytes 196612
  93.9 4.1 %copy-start.28 = (bf16[256,128]{1,0:T(8,128)(2,1)S(1)}, bf16[256,128]{1,0:T(8,128)(2,1)}, u32[]{:S(2)}) copy-start(bf16[256,128]{1,0:T(8,128)(2,1)} %copy-done.27) | copy-start | bytes 196612
  95.4 2.9 %copy-start.30 = (bf16[256,128]{1,0:T(8,128)(2,1)S(1)}, bf16[256,128]{1,0:T(8,128)(2,1)}, u32[]{:S(2)}) copy-start(bf16[256,128]{1,0:T(8,128)(2,1)} %copy-done.29) | copy-start | bytes 196612
  95.4 3.2 %copy-start.32 = (bf16[256,128]{1,0:T(8,128)(2,1)S(1)}, bf16[256,128]{1,0:T(8,128)(2,1)}, u32[]{:S(2)}) copy-start(bf16[256,128]{1,0:T(8,128)(2,1)} %copy-done.31) | copy-start | bytes 196612
  96.8 2.0 %copy-start.34 = (bf16[256,128]{1,0:T(8,128)(2,1)S(1)}, bf16[256,128]{1,0:T(8,128)(2,1)}, u32[]{:S(2)}) copy-start(bf16[256,128]{1,0:T(8,128)(2,1)} %copy-done.33) | copy-start | bytes 196612
  98.0 8.0 %copy-start.13 = (bf16[4,256,256]{1,2,0:T(8,128)(2,1)S(1)}, bf16[4,256,256]{1,2,0:T(8,128)(2,1)}, u32[]{:S(2)}) copy-start(bf16[4,256,256]{1,2,0:T(8,128)(2,1)} %copy-done.12) | copy-start | bytes 1572868
  100.0 5.0 %collective-permute-start.9 = (bf16[256,128]{1,0:T(8,128)(2,1)S(1)}, bf16[256,128]{1,0:T(8,128)(2,1)S(1)}, u32[]{:S(2)}, u32[]{:S(2)}) collective-permute-start(bf16[256,128]{1,0:T(8,128)(2,1)S(1)} %fusion.37), channel_id=1, source_target_pairs={{8,0},{12,4},{16,8},{20,12},{24,16},{28,20},{0,24},{4,28},{9,1},{1... | collective-permute-start | bytes 196616 | tf_op jit(solution)/shard_map/ppermute | solution.py:15
  100.6 4.6 %collective-permute-start.10 = (bf16[256,128]{1,0:T(8,128)(2,1)S(1)}, bf16[256,128]{1,0:T(8,128)(2,1)S(1)}, u32[]{:S(2)}, u32[]{:S(2)}) collective-permute-start(bf16[256,128]{1,0:T(8,128)(2,1)S(1)} %fusion.38), channel_id=1, source_target_pairs={{12,0},{16,4},{20,8},{24,12},{28,16},{0,20},{4,24},{8,28},{13,1},{... | collective-permute-start | bytes 196616 | tf_op jit(solution)/shard_map/ppermute | solution.py:15
  100.9 5.0 %collective-permute-start.11 = (bf16[256,128]{1,0:T(8,128)(2,1)S(1)}, bf16[256,128]{1,0:T(8,128)(2,1)S(1)}, u32[]{:S(2)}, u32[]{:S(2)}) collective-permute-start(bf16[256,128]{1,0:T(8,128)(2,1)S(1)} %fusion.39), channel_id=1, source_target_pairs={{16,0},{20,4},{24,8},{28,12},{0,16},{4,20},{8,24},{12,28},{17,1},{... | collective-permute-start | bytes 196616 | tf_op jit(solution)/shard_map/ppermute | solution.py:15
Sparse Core Ops, SparseCore 0:
  13.8 46.8 all-gather.1
  79.4 42.4 reduce-scatter.1
where the time goes:
time: 130 us; the launch traced here: 129 us
  matrix products  43.2 us (33%)
  waiting for transfers between devices  37.7 us (29%)
  starting transfers between devices  18 us (14%)
  between operations  18 us (14%)
  local copies, waits for them, and re-layouts  7.84 us (6%)
  other arithmetic  4.06 us (3%)
    ppermute x16, starting transfers between devices, shifted(): return lax.ppermute(block, axis, route)  17.9 us
    reduce_scatter x1, waiting for transfers between devices, body(): lax.psum_scatter(share.astype(jnp.bfloat16), 'head', scatter_dimension=1,...  14.2 us
    all_gather x1, waiting for transfers between devices, body(): lax.all_gather(grad_out, 'head', axis=1, tiled=True)  13.7 us
    ppermute x16, waiting for transfers between devices, shifted(): return lax.ppermute(block, axis, route)  9.77 us
    dot_general x5, matrix products, block_grads(): jnp.einsum('grij,igrd->jgd', probs.astype(jnp.bfloat16), grad_heads, pref...  9.29 us
    dot_general x5, matrix products, weighted_values(): jnp.einsum('grij,jgd->igrd', probs.astype(jnp.bfloat16), value_heads, pre...  7.99 us
    dot_general x5, matrix products, block_grads(): jnp.einsum('igrd,jgd->grij', grad_heads, value_heads, preferred_element_t...  6.7 us
    dot_general x1, matrix products, body(): share = jnp.dot(attention, out_proj, preferred_element_type=jnp.float32)  4.83 us
  transfers between devices with their start and end apart: 18, of which 8 were waited for; matrix products, arithmetic and copies ran while one was open for 36% of the time, Pallas kernels for 0%

commit v1 on v0

v1 whole, which is shorter than its diff:
```python
import functools

import jax
import jax.numpy as jnp
from jax import lax
from jax.experimental import pallas as pl
from jax.experimental.pallas import tpu as pltpu
from jax.sharding import PartitionSpec as P

HEAD_DIM = 128
LOWEST = -1e30
LOG2_E = 1.4426950408889634
F32 = jnp.float32
BF16 = jnp.bfloat16

NT = (((1,), (1,)), ((), ()))
NN = (((1,), (0,)), ((), ()))

WHOLE = pl.BlockSpec(memory_space=pltpu.VMEM)
MAIN = pl.BlockSpec(memory_space=pltpu.HBM)
PARAMS = pltpu.CompilerParams(vmem_limit_bytes=24 * 1024 * 1024)


def dot(a, b, dims=NN):
    return lax.dot_general(a, b, dims, preferred_element_type=F32)


def head_of(array, index):
    return array[:, index * HEAD_DIM : (index + 1) * HEAD_DIM]


def columns_at(proj, index, share):
    return proj.at[:, pl.ds(pl.multiple_of(index * share, share), share)]


def main(array):
    return pltpu.with_memory_space_constraint(array, pltpu.HBM)


def estimate(flops, size):
    return pl.CostEstimate(flops=flops, bytes_accessed=size, transcendentals=0)


def stage_kernel(keys, values, queries, windows, order, pair, query, limits, spans, slabs, sems, *, reach):
    rows, width = keys.shape
    copies = [
        pltpu.make_async_copy(windows, spans, sems.at[0]),
        pltpu.make_async_copy(order, slabs, sems.at[1]),
        pltpu.make_async_copy(keys, pair.at[:, pl.ds(0, width)], sems.at[2]),
        pltpu.make_async_copy(values, pair.at[:, pl.ds(width, width)], sems.at[3]),
        pltpu.make_async_copy(queries, query, sems.at[4]),
    ]
    for copy in copies:
        copy.start()
    copies[0].wait()
    copies[1].wait()
    slab = slabs[lax.axis_index("seq")]
    for head in range(windows.shape[0]):
        for step in range(reach + 1):
            limit = jnp.where(slab >= step, spans[head] - step * rows, -rows)
            limits[pl.ds(head * (reach + 1) + step, 1), :] = jnp.full((1, rows), limit, jnp.int32)
    for copy in copies[2:]:
        copy.wait()


def stage(key_vectors, values, queries, windows, slab_order, reach):
    rows, width = key_vectors.shape
    heads = windows.shape[0]
    return pl.pallas_call(
        functools.partial(stage_kernel, reach=reach),
        in_specs=[MAIN] * 5,
        out_specs=[WHOLE] * 3,
        out_shape=[
            pltpu.VMEM((rows, 2 * width), BF16),
            pltpu.VMEM(queries.shape, BF16),
            pltpu.VMEM((heads * (reach + 1), rows), jnp.int32),
        ],
        scratch_shapes=[
            pltpu.SMEM(windows.shape, jnp.int32),
            pltpu.SMEM(slab_order.shape, jnp.int32),
            pltpu.SemaphoreType.DMA((5,)),
        ],
        compiler_params=PARAMS,
        cost_estimate=estimate(rows * width, 8 * rows * width),
        name="stage",
    )(*[main(array) for array in (key_vectors, values, queries, windows, slab_order)])


def forward_kernel(limits, query, proj, *refs, reach, groups):
    blocks = refs[: reach + 1]
    attention, turned, probs, lead, local = refs[reach + 1 : reach + 6]
    (sem,) = refs[reach + 6 :]
    rows, width = query.shape
    heads = width // HEAD_DIM
    size = lax.axis_size("head")
    place = size - 1 - lax.axis_index("head")
    copy = pltpu.make_async_copy(proj, local, sem)
    copy.start()
    scale = HEAD_DIM ** (-0.5) * LOG2_E
    offset = lax.broadcasted_iota(jnp.int32, (rows, rows), 1) - lax.broadcasted_iota(
        jnp.int32, (rows, rows), 0
    )
    turned_values = [
        [head_of(blocks[step], groups + group).T for step in range(reach + 1)]
        for group in range(groups)
    ]

    def head_scores(head):
        scores = []
        for step in range(reach + 1):
            score = dot(head_of(blocks[step], head * groups // heads), head_of(query, head), NT)
            mask = offset < limits[pl.ds(head * (reach + 1) + step, 1), :]
            if step == 0:
                mask = mask & (offset >= 0)
            scores.append(jnp.where(mask, score, LOWEST))
        return scores

    scores = head_scores(0)
    for head in range(heads):
        following = head_scores(head + 1) if head + 1 < heads else None
        peak = functools.reduce(
            jnp.maximum, [jnp.max(score, 0, keepdims=True) for score in scores]
        )
        powers = [jnp.exp2((score - peak) * scale) for score in scores]
        inverse = 1.0 / sum(jnp.sum(power, 0, keepdims=True) for power in powers)
        mixed = jnp.zeros((HEAD_DIM, rows), F32)
        for step in range(reach + 1):
            prob = (powers[step] * inverse).astype(BF16)
            probs[pl.ds(step * rows, rows), pl.ds(head * rows, rows)] = prob
            mixed = mixed + dot(turned_values[head * groups // heads][step], prob)
        turned[pl.ds(head * HEAD_DIM, HEAD_DIM), :] = mixed.astype(BF16)
        attention[:, pl.ds(head * HEAD_DIM, HEAD_DIM)] = mixed.T.astype(BF16)
        scores = following
    copy.wait()
    lead[0] = dot(attention[...], columns_at(local, place, lead.shape[2])[...]).astype(BF16)


def forward(limits, query, out_proj, blocks, groups, size):
    rows, width = query.shape
    heads = width // HEAD_DIM
    reach = len(blocks) - 1
    share = out_proj.shape[1] // size
    span = (reach + 1) * rows
    return pl.pallas_call(
        functools.partial(forward_kernel, reach=reach, groups=groups),
        in_specs=[WHOLE, WHOLE, MAIN] + [WHOLE] * (reach + 1),
        out_specs=[WHOLE] * 5,
        out_shape=[
            pltpu.VMEM((rows, width), BF16),
            pltpu.VMEM((width, rows), BF16),
            pltpu.VMEM((span, heads * rows), BF16),
            pltpu.VMEM((1, rows, share), BF16),
            pltpu.VMEM(out_proj.shape, BF16),
        ],
        scratch_shapes=[pltpu.SemaphoreType.DMA],
        compiler_params=PARAMS,
        cost_estimate=estimate(4 * rows * span * width, 8 * rows * span),
        name="forward",
    )(limits, query, main(out_proj), *blocks)


def send_kernel(shares, passed, out, *, end, inner):
    z = lax.axis_index("head")

    @pl.when(z == end)
    def _():
        out[...] = shares[0]

    if inner is None:

        @pl.when(z != end)
        def _():
            out[...] = passed[...]

    else:

        @pl.when(z == inner)
        def _():
            out[...] = passed[...]

        @pl.when((z != end) & (z != inner))
        def _():
            out[...] = shares[0] + passed[...]


def send(shares, passed, end, inner, name):
    return pl.pallas_call(
        functools.partial(send_kernel, end=end, inner=inner),
        in_specs=[WHOLE] * 2,
        out_specs=WHOLE,
        out_shape=pltpu.VMEM(passed.shape, BF16),
        compiler_params=PARAMS,
        cost_estimate=estimate(passed.size, 6 * passed.size),
        name=name,
    )(shares, passed)


def middle_kernel(attention, own, above, below, proj, shares, partial, extra, sem):
    size = lax.axis_size("head")
    z = lax.axis_index("head")
    share = extra.shape[1]
    copy = pltpu.make_async_copy(own, extra, sem)
    copy.start()
    places = [lax.rem(z + size // 2, size), jnp.minimum(z + 1, size - 1), jnp.maximum(z - 1, 0), z]
    total = None
    for slot, source in enumerate((None, below, above, extra)):
        block = columns_at(proj, places[slot], share)[...]
        shares[slot] = dot(attention[...], block).astype(BF16)
        if source is extra:
            copy.wait()
        if source is not None:
            part = dot(block, source[...], NT)
            total = part if total is None else total + part
    partial[...] = total


def middle(attention, own, above, below, out_proj, size):
    rows, width = attention.shape
    share = out_proj.shape[1] // size
    return pl.pallas_call(
        middle_kernel,
        in_specs=[WHOLE, MAIN, WHOLE, WHOLE, WHOLE],
        out_specs=[WHOLE] * 2,
        out_shape=[
            pltpu.VMEM((4, rows, share), BF16),
            pltpu.VMEM((width, rows), F32),
        ],
        scratch_shapes=[pltpu.VMEM(own.shape, BF16), pltpu.SemaphoreType.DMA],
        compiler_params=PARAMS,
        cost_estimate=estimate(14 * rows * share * width, 8 * share * width),
        name="middle",
    )(attention, main(own), above, below, out_proj)


def far_kernel(partial, above, below, proj, out):
    size = lax.axis_size("head")
    z = lax.axis_index("head")
    share = above.shape[1]
    block = columns_at(proj, lax.rem(z + size // 2, size), share)

    @pl.when(z >= size // 2)
    def _():
        out[...] = partial[...] + dot(block[...], above[...], NT)

    @pl.when(z < size // 2)
    def _():
        out[...] = partial[...] + dot(block[...], below[...], NT)


def far(partial, above, below, out_proj):
    rows, share = above.shape
    width = out_proj.shape[0]
    return pl.pallas_call(
        far_kernel,
        in_specs=[WHOLE] * 4,
        out_specs=WHOLE,
        out_shape=pltpu.VMEM((width, rows), F32),
        compiler_params=PARAMS,
        cost_estimate=estimate(2 * rows * share * width, 2 * share * width),
        name="far",
    )(partial, above, below, out_proj)


def backward_kernel(partial, above, below, query, turned, probs, proj, *refs, reach, groups):
    blocks = refs[: reach + 1]
    grads = refs[reach + 1 : 2 * reach + 1]
    scores, ups, upstream = refs[2 * reach + 1 :]
    rows, width = query.shape
    heads = width // HEAD_DIM
    ratio = heads // groups
    size = lax.axis_size("head")
    z = lax.axis_index("head")
    share = above.shape[1]
    scale = HEAD_DIM ** (-0.5)
    block = columns_at(proj, size - 1 - z, share)

    @pl.when(z == size - 1)
    def _():
        upstream[...] = (partial[...] + dot(block[...], above[...], NT)).astype(BF16)

    @pl.when(z == 0)
    def _():
        upstream[...] = (partial[...] + dot(block[...], below[...], NT)).astype(BF16)

    @pl.when((z > 0) & (z < size - 1))
    def _():
        upstream[...] = partial[...].astype(BF16)

    for head in range(heads):
        up = upstream[pl.ds(head * HEAD_DIM, HEAD_DIM), :]
        ups[pl.ds(head * rows, rows), :] = up.T
        wide = up.astype(F32) * turned[pl.ds(head * HEAD_DIM, HEAD_DIM), :].astype(F32)
        delta = jnp.sum(wide, 0, keepdims=True)
        columns = pl.ds(head * rows, rows)
        for step in range(reach + 1):
            spot = pl.ds(step * rows, rows)
            grad_prob = dot(head_of(blocks[step], groups + head // ratio), up)
            scores[spot, columns] = (
                probs[spot, columns].astype(F32) * (grad_prob - delta)
            ).astype(BF16)
    for group in range(groups):
        tall_query = jnp.concatenate(
            [head_of(query, head) for head in range(group * ratio, (group + 1) * ratio)], 0
        )
        columns = pl.ds(group * ratio * rows, ratio * rows)
        for step in range(1, reach + 1):
            spot = pl.ds(step * rows, rows)
            grads[step - 1][:, pl.ds(group * HEAD_DIM, HEAD_DIM)] = (
                dot(scores[spot, columns], tall_query) * scale
            ).astype(BF16)
            grads[step - 1][:, pl.ds((groups + group) * HEAD_DIM, HEAD_DIM)] = dot(
                probs[spot, columns], ups[columns, :]
            ).astype(BF16)


def backward(partial, above, below, query, turned, probs, out_proj, blocks, groups):
    rows, width = query.shape
    heads = width // HEAD_DIM
    reach = len(blocks) - 1
    span = (reach + 1) * rows
    outs = pl.pallas_call(
        functools.partial(backward_kernel, reach=reach, groups=groups),
        in_specs=[WHOLE] * (reach + 8),
        out_specs=[WHOLE] * (reach + 2),
        out_shape=[pltpu.VMEM((rows, 2 * groups * HEAD_DIM), BF16)] * reach
        + [
            pltpu.VMEM(probs.shape, BF16),
            pltpu.VMEM((heads * rows, HEAD_DIM), BF16),
        ],
        scratch_shapes=[pltpu.VMEM((width, rows), BF16)],
        compiler_params=PARAMS,
        cost_estimate=estimate(8 * rows * span * width, 8 * rows * span),
        name="backward",
    )(partial, above, below, query, turned, probs, out_proj, *blocks)
    return outs[:reach], outs[reach], outs[reach + 1]


def finish_kernel(scores, ups, query, probs, *refs, reach, groups):
    blocks = refs[: reach + 1]
    grad_query, grad = refs[reach + 1 :]
    rows, width = query.shape
    heads = width // HEAD_DIM
    ratio = heads // groups
    scale = HEAD_DIM ** (-0.5)
    spot = pl.ds(0, rows)
    for group in range(groups):
        picked = range(group * ratio, (group + 1) * ratio)
        tall_query = jnp.concatenate([head_of(query, head) for head in picked], 0)
        columns = pl.ds(group * ratio * rows, ratio * rows)
        grad[:, pl.ds(group * HEAD_DIM, HEAD_DIM)] = dot(scores[spot, columns], tall_query) * scale
        grad[:, pl.ds((groups + group) * HEAD_DIM, HEAD_DIM)] = dot(
            probs[spot, columns], ups[columns, :]
        )
        keys = jnp.concatenate([head_of(blocks[step], group) for step in range(reach + 1)], 0).T
        for head in picked:
            total = dot(keys, scores[:, pl.ds(head * rows, rows)])
            grad_query[:, pl.ds(head * HEAD_DIM, HEAD_DIM)] = (total * scale).T.astype(BF16)


def finish(scores, ups, query, probs, blocks, groups):
    rows, width = query.shape
    reach = len(blocks) - 1
    span = (reach + 1) * rows
    return pl.pallas_call(
        functools.partial(finish_kernel, reach=reach, groups=groups),
        in_specs=[WHOLE] * (reach + 5),
        out_specs=[WHOLE] * 2,
        out_shape=[
            jax.ShapeDtypeStruct((rows, width), BF16),
            pltpu.VMEM((rows, 2 * groups * HEAD_DIM), F32),
        ],
        compiler_params=PARAMS,
        cost_estimate=estimate(2 * rows * span * width, 4 * rows * span),
        name="finish",
    )(scores, ups, query, probs, *blocks)


def body(queries, key_vectors, values, out_proj, grad_out, windows, slab_order):
    groups = key_vectors.shape[1] // HEAD_DIM
    devices = lax.axis_size("seq")
    size = lax.axis_size("head")
    assert size == 4 and devices % 4 == 0
    reach = min(8, devices // 2)
    half = reach // 2
    even = lax.axis_index("seq") % 2 == 0
    nothing = jnp.zeros((), BF16)

    def climb(array):
        return lax.ppermute(array, "head", [(i, i + 1) for i in range(size - 1)])

    def descend(array):
        return lax.ppermute(array, "head", [(i + 1, i) for i in range(size - 1)])

    def shifted(array, step):
        return lax.ppermute(array, "seq", [((i - step) % devices, i) for i in range(devices)])

    def swapped(array):
        return lax.ppermute(array, "seq", [(i ^ 1, i) for i in range(devices)])

    pair, query, limits = stage(key_vectors, values, queries, windows, slab_order, reach)
    fetched = [pair] + [shifted(pair, 2 * step) for step in range(1, half + 1)]
    traded = [swapped(jnp.where(even, pair, fetched[half]))]
    traded += [swapped(fetched[step]) for step in range(1, half)]
    blocks = [pair]
    for step in range(half):
        blocks.append(jnp.where(even, traded[(step + 1) % half], traded[step]))
        blocks.append(fetched[step + 1])

    above1, below1 = climb(grad_out), descend(grad_out)
    attention, turned, probs, lead, proj = forward(limits, query, out_proj, blocks, groups, size)

    above2 = climb(send(lead, above1, 0, None, "send_up2"))
    below2 = descend(send(lead, below1, size - 1, None, "send_down2"))
    rest, partial = middle(attention, grad_out, above1, below1, proj, size)

    above3 = climb(send(rest, above2, 0, size // 2, "send_up3"))
    below3 = descend(send(rest, below2, size - 1, size // 2 - 1, "send_down3"))
    partial = far(partial, above2, below2, proj)

    sent, scores, ups = backward(
        partial, above3, below3, query, turned, probs, proj, blocks, groups
    )
    above4 = climb(rest[1] + above3)
    below4 = descend(rest[2] + below3)

    taken = [swapped(sent[2 * step]) for step in range(half)]
    total = []
    for step in range(half):
        near = taken[step]
        if step + 1 < half:
            near = jnp.where(even, taken[step + 1], near)
        else:
            near = jnp.where(even, nothing, near)
        total.append(shifted(sent[2 * step + 1] + near, -2 * (step + 1)))
    grad_queries, own = finish(scores, ups, query, probs, blocks, groups)
    own = own + jnp.where(even, taken[0], nothing).astype(F32)
    for part in total:
        own = own + part.astype(F32)
    grad_keys = own[:, : groups * HEAD_DIM].astype(BF16)
    grad_values = own[:, groups * HEAD_DIM :].astype(BF16)
    layer_out = (rest[3].astype(F32) + above4.astype(F32) + below4.astype(F32)).astype(BF16)
    return layer_out, grad_queries, grad_keys, grad_values


def solution(mesh):
    in_specs = (
        P("seq", "head"),
        P("seq", "head"),
        P("seq", "head"),
        P("head", None),
        P("seq", "head"),
        P("head"),
        P(),
    )
    out_specs = (P("seq", "head"), P("seq", "head"), P("seq", "head"), P("seq", "head"))
    return jax.shard_map(body, mesh=mesh, in_specs=in_specs, out_specs=out_specs, check_vma=False)
```

time: 130 us -> 76.5 us (0.59)
  matrix products: 43.2 us -> 0 us
  between operations: 18 us -> 0.86 us
  starting transfers between devices: 18 us -> 29.7 us
  Pallas kernels: 0 us -> 11.6 us
  local copies, waits for them, and re-layouts: 7.84 us -> 0.66 us
  waiting for transfers between devices: 37.7 us -> 32.1 us
  other arithmetic: 4.06 us -> 1.31 us
    dot_general x32 -> x0, matrix products: 43.2 us -> none  [the longest x5 9.29 us: block_grads(): jnp.einsum('grij,igrd->jgd', probs.astype(jnp.bfloat16), grad_heads, pref...]
    ppermute x16, waiting for transfers between devices: 9.77 us -> 32.1 us  [the longest x4 18.5 us: climb(): return lax.ppermute(array, 'head', [(i, i + 1) for i in range(size - 1)])]
    reduce_scatter x1 -> x0, waiting for transfers between devices: 14.2 us -> none  [body(): lax.psum_scatter(share.astype(jnp.bfloat16), 'head', scatter_dimension=1,...]
    all_gather x1 -> x0, waiting for transfers between devices: 13.7 us -> none  [body(): lax.all_gather(grad_out, 'head', axis=1, tiled=True)]
    ppermute x16, starting transfers between devices: 17.9 us -> 29.7 us  [the longest x4 16.8 us: climb(): return lax.ppermute(array, 'head', [(i, i + 1) for i in range(size - 1)])]
    pallas_call x0 -> x10, Pallas kernels: none -> 11.6 us  [the longest x1 3.04 us: forward(): pl.pallas_call(functools.partial(forward_kernel, reach=reach, groups=grou...]
    unnamed x75 -> x0, local copies, waits for them, and re-layouts: 3.36 us -> none
    another operation x1, other arithmetic: 2.44 us -> 0.07 us
  transfers between devices with their start and end apart: 18 -> 16, of which waited for: 8 -> 10; matrix products, arithmetic and copies ran while one was open for 36% -> 1% of each run, Pallas kernels for 0% -> 11%
where the time goes in v1:
time: 76.5 us; the launch traced here: 76.2 us
  waiting for transfers between devices  32.1 us (42%)
  starting transfers between devices  29.7 us (39%)
  Pallas kernels  11.6 us (15%)
  other arithmetic  1.31 us (2%)
  between operations  0.86 us (1%)
    ppermute x4, waiting for transfers between devices, climb(): return lax.ppermute(array, 'head', [(i, i + 1) for i in range(size - 1)])  18.5 us
    ppermute x4, starting transfers between devices, climb(): return lax.ppermute(array, 'head', [(i, i + 1) for i in range(size - 1)])  16.8 us
    ppermute x4, waiting for transfers between devices, descend(): return lax.ppermute(array, 'head', [(i + 1, i) for i in range(size - 1)])  11.6 us
    ppermute x4, starting transfers between devices, shifted(): lax.ppermute(array, 'seq', [((i - step) % devices, i) for i in range(devi...  6.56 us
    ppermute x4, starting transfers between devices, descend(): return lax.ppermute(array, 'head', [(i + 1, i) for i in range(size - 1)])  5.17 us
    pallas_call x1, Pallas kernels, forward(): pl.pallas_call(functools.partial(forward_kernel, reach=reach, groups=grou...  3.04 us
    pallas_call x1, Pallas kernels, middle(): pl.pallas_call(middle_kernel, in_specs=[WHOLE, MAIN, WHOLE, WHOLE, WHOLE]...  2.81 us
    pallas_call x1, Pallas kernels, backward(): pl.pallas_call(functools.partial(backward_kernel, reach=reach, groups=gro...  2.42 us
  transfers between devices with their start and end apart: 16, of which 10 were waited for; matrix products, arithmetic and copies ran while one was open for 1% of the time, Pallas kernels for 11%

profile of v1, /device:TPU:0, one launch (start us, length us, event | category | flops | bytes accessed | tf_op | source)
XLA Modules:
  0.0 76.2 jit_solution(18248065024898441127)
XLA Ops:
  0.6 1.1 %stage.1 = (bf16[256,256]{1,0:T(8,128)(2,1)S(1)}, bf16[256,512]{1,0:T(8,128)(2,1)S(1)}, s32[20,256]{1,0:T(8,128)S(1)}) custom-call(bf16[256,128]{1,0:T(8,128)(2,1)} %keys.1, bf16[256,128]{1,0:T(8,128)(2,1)} %values.1, bf16[256,512]{1,0:T(8,128)(2,1)} %queries.1, s32[4]{0:T(128)} %windows.1, s32[8]{0:T(128)} %order.1), custom_call_target="tpu_custom_call" | custom-call | flops 32768 | bytes 262144 | tf_op jit(solution)/shard_map/stage/pallas_call | solution.py:69
  1.7 3.1 %collective-permute-start.2 = (bf16[256,256]{1,0:T(8,128)(2,1)S(1)}, bf16[256,256]{1,0:T(8,128)(2,1)S(1)}, u32[]{:S(2)}, u32[]{:S(2)}) collective-permute-start(bf16[256,256]{1,0:T(8,128)(2,1)S(1)} %get-tuple-element.24.refs_0_), channel_id=1, source_target_pairs={{16,0},{20,4},{24,8},{28,12},{0,16},{4,20},{8,24},{12,28},{17,1},{... | collective-permute-start | bytes 393224 | tf_op jit(solution)/shard_map/ppermute | solution.py:395
  4.8 1.5 %collective-permute-start = (bf16[256,256]{1,0:T(8,128)(2,1)S(1)}, bf16[256,256]{1,0:T(8,128)(2,1)S(1)}, u32[]{:S(2)}, u32[]{:S(2)}) collective-permute-start(bf16[256,256]{1,0:T(8,128)(2,1)S(1)} %get-tuple-element.24.refs_0_), channel_id=1, source_target_pairs={{24,0},{28,4},{0,8},{4,12},{8,16},{12,20},{16,24},{20,28},{25,1},{... | collective-permute-start | bytes 393224 | tf_op jit(solution)/shard_map/ppermute | solution.py:395
  6.3 3.5 %collective-permute-start.4 = (bf16[256,1024]{1,0:T(8,128)(2,1)}, bf16[256,1024]{1,0:T(8,128)(2,1)S(1)}, u32[]{:S(2)}, u32[]{:S(2)}) collective-permute-start(bf16[256,1024]{1,0:T(8,128)(2,1)} %own.1), channel_id=1, source_target_pairs={{0,1},{1,2},{2,3},{4,5},{5,6},{6,7},{8,9},{9,10},{10,11},{12,13},{... | collective-permute-start | bytes 1572872 | tf_op jit(solution)/shard_map/ppermute | solution.py:389
  9.8 1.3 %collective-permute-start.5 = (bf16[256,1024]{1,0:T(8,128)(2,1)}, bf16[256,1024]{1,0:T(8,128)(2,1)S(1)}, u32[]{:S(2)}, u32[]{:S(2)}) collective-permute-start(bf16[256,1024]{1,0:T(8,128)(2,1)} %own.1), channel_id=1, source_target_pairs={{1,0},{2,1},{3,2},{5,4},{6,5},{7,6},{9,8},{10,9},{11,10},{13,12},{... | collective-permute-start | bytes 1572872 | tf_op jit(solution)/shard_map/ppermute | solution.py:392
  11.1 0.0 collective-permute-done.2.refs_4_
  11.1 0.1 collective-permute-start.3
  11.2 0.0 collective-permute-done.refs_2_
  11.2 0.5 collective-permute-start.1
  11.7 0.8 %collective-permute-done.3 = bf16[256,256]{1,0:T(8,128)(2,1)S(1)} collective-permute-done((bf16[256,256]{1,0:T(8,128)(2,1)S(1)}, bf16[256,256]{1,0:T(8,128)(2,1)S(1)}, u32[]{:S(2)}, u32[]{:S(2)}) %collective-permute-start.3) | collective-permute-done | bytes 131104 | tf_op jit(solution)/shard_map/ppermute | solution.py:398
  12.5 0.2 collective-permute-done.1
  12.8 3.0 %forward.1 = (bf16[256,512]{1,0:T(8,128)(2,1)S(1)}, bf16[512,256]{1,0:T(8,128)(2,1)S(1)}, bf16[1280,1024]{1,0:T(8,128)(2,1)S(1)}, bf16[1,256,1024]{2,1,0:T(8,128)(2,1)S(1)}, bf16[512,4096]{1,0:T(8,128)(2,1)S(1)}) custom-call(s32[20,256]{1,0:T(8,128)S(1)} %get-tuple-element.22.limits, bf16[256,512]{1,0:T(8,128)(2,1)S(1)} %get-tuple-element.23.query, ...), custom_call_target="tpu_custom_call" | custom-call | flops 671088640 | bytes 2621440 | tf_op jit(solution)/shard_map/forward/pallas_call | solution.py:144
  15.8 4.9 %collective-permute-done.4.above.passed = bf16[256,1024]{1,0:T(8,128)(2,1)S(1)} collective-permute-done((bf16[256,1024]{1,0:T(8,128)(2,1)}, bf16[256,1024]{1,0:T(8,128)(2,1)S(1)}, u32[]{:S(2)}, u32[]{:S(2)}) %collective-permute-start.4) | collective-permute-done | bytes 524320 | tf_op jit(solution)/shard_map/ppermute | solution.py:389
  20.7 4.3 %collective-permute-start.6 = (bf16[256,1024]{1,0:T(8,128)(2,1)S(1)}, bf16[256,1024]{1,0:T(8,128)(2,1)S(1)}, u32[]{:S(2)}, u32[]{:S(2)}) collective-permute-start(bf16[256,1024]{1,0:T(8,128)(2,1)S(1)} %send_up2.1), channel_id=1, source_target_pairs={{0,1},{1,2},{2,3},{4,5},{5,6},{6,7},{8,9},{9,10},{10,11},{12,13},{... | collective-permute-start | bytes 1572872 | tf_op jit(solution)/shard_map/ppermute | solution.py:389
  25.0 0.0 collective-permute-done.5.below.passed
  25.1 1.3 %collective-permute-start.9 = (bf16[256,1024]{1,0:T(8,128)(2,1)S(1)}, bf16[256,1024]{1,0:T(8,128)(2,1)S(1)}, u32[]{:S(2)}, u32[]{:S(2)}) collective-permute-start(bf16[256,1024]{1,0:T(8,128)(2,1)S(1)} %send_down2.1), channel_id=1, source_target_pairs={{1,0},{2,1},{3,2},{5,4},{6,5},{7,6},{9,8},{10,9},{11,10},{13,12},{... | collective-permute-start | bytes 1572872 | tf_op jit(solution)/shard_map/ppermute | solution.py:392
  26.4 2.8 %middle.1 = (bf16[4,256,1024]{2,1,0:T(8,128)(2,1)S(1)}, f32[512,256]{1,0:T(8,128)S(1)}) custom-call(bf16[256,512]{1,0:T(8,128)(2,1)S(1)} %get-tuple-element.25.attention, bf16[256,1024]{1,0:T(8,128)(2,1)} %own.1, bf16[256,1024]{1,0:T(8,128)(2,1)S(1)} %collective-permute-done.4.above.passed, bf16[256,1024]{1,0:T(8,128)(2,1)S(1)} %collective-permute-done.5.below.passed, ...), custom_call_target="tpu_custom_call" | custom-call | flops 1879048192 | bytes 4194304 | tf_op jit(solution)/shard_map/middle/pallas_call | solution.py:220
  29.2 5.5 %collective-permute-done.6.passed.above = bf16[256,1024]{1,0:T(8,128)(2,1)S(1)} collective-permute-done((bf16[256,1024]{1,0:T(8,128)(2,1)S(1)}, bf16[256,1024]{1,0:T(8,128)(2,1)S(1)}, u32[]{:S(2)}, u32[]{:S(2)}) %collective-permute-start.6) | collective-permute-done | bytes 524320 | tf_op jit(solution)/shard_map/ppermute | solution.py:389
  34.8 4.4 %collective-permute-start.7 = (bf16[256,1024]{1,0:T(8,128)(2,1)S(1)}, bf16[256,1024]{1,0:T(8,128)(2,1)S(1)}, u32[]{:S(2)}, u32[]{:S(2)}) collective-permute-start(bf16[256,1024]{1,0:T(8,128)(2,1)S(1)} %send_up3.1), channel_id=1, source_target_pairs={{0,1},{1,2},{2,3},{4,5},{5,6},{6,7},{8,9},{9,10},{10,11},{12,13},{... | collective-permute-start | bytes 1572872 | tf_op jit(solution)/shard_map/ppermute | solution.py:389
  39.2 0.0 collective-permute-done.9.passed.below
  39.2 0.1 send_down3.1
  39.3 1.3 %collective-permute-start.10 = (bf16[256,1024]{1,0:T(8,128)(2,1)S(1)}, bf16[256,1024]{1,0:T(8,128)(2,1)S(1)}, u32[]{:S(2)}, u32[]{:S(2)}) collective-permute-start(bf16[256,1024]{1,0:T(8,128)(2,1)S(1)} %send_down3.1), channel_id=1, source_target_pairs={{1,0},{2,1},{3,2},{5,4},{6,5},{7,6},{9,8},{10,9},{11,10},{13,12},{... | collective-permute-start | bytes 1572872 | tf_op jit(solution)/shard_map/ppermute | solution.py:392
  40.6 0.5 far.1.partial
  41.1 7.0 %collective-permute-done.7.above = bf16[256,1024]{1,0:T(8,128)(2,1)S(1)} collective-permute-done((bf16[256,1024]{1,0:T(8,128)(2,1)S(1)}, bf16[256,1024]{1,0:T(8,128)(2,1)S(1)}, u32[]{:S(2)}, u32[]{:S(2)}) %collective-permute-start.7) | collective-permute-done | bytes 524320 | tf_op jit(solution)/shard_map/ppermute | solution.py:389
  48.1 4.2 %collective-permute-done.10.below = bf16[256,1024]{1,0:T(8,128)(2,1)S(1)} collective-permute-done((bf16[256,1024]{1,0:T(8,128)(2,1)S(1)}, bf16[256,1024]{1,0:T(8,128)(2,1)S(1)}, u32[]{:S(2)}, u32[]{:S(2)}) %collective-permute-start.10) | collective-permute-done | bytes 524320 | tf_op jit(solution)/shard_map/ppermute | solution.py:392
  52.3 2.4 %backward.1 = (bf16[256,256]{1,0:T(8,128)(2,1)S(1)}, bf16[256,256]{1,0:T(8,128)(2,1)S(1)}, bf16[256,256]{1,0:T(8,128)(2,1)S(1)}, bf16[256,256]{1,0:T(8,128)(2,1)...) custom-call(f32[512,256]{1,0:T(8,128)S(1)} %far.1.partial, ...), custom_call_target="tpu_custom_call" | custom-call | flops 1342177280 | bytes 2621440 | tf_op jit(solution)/shard_map/backward/pallas_call | solution.py:321
  54.7 0.1 collective-permute-start.13
  54.8 0.5 collective-permute-start.12
  55.3 0.8 %collective-permute-done.13 = bf16[256,256]{1,0:T(8,128)(2,1)S(1)} collective-permute-done((bf16[256,256]{1,0:T(8,128)(2,1)S(1)}, bf16[256,256]{1,0:T(8,128)(2,1)S(1)}, u32[]{:S(2)}, u32[]{:S(2)}) %collective-permute-start.13) | collective-permute-done | bytes 131104 | tf_op jit(solution)/shard_map/ppermute | solution.py:398
  56.2 0.2 collective-permute-done.12
  56.4 0.6 collective-permute-start.15
  56.9 1.4 %collective-permute-start.14 = (bf16[256,256]{1,0:T(8,128)(2,1)S(1)}, bf16[256,256]{1,0:T(8,128)(2,1)S(1)}, u32[]{:S(2)}, u32[]{:S(2)}) collective-permute-start(bf16[256,256]{1,0:T(8,128)(2,1)S(1)} %get-tuple-element.46), channel_id=1, source_target_pairs={{8,0},{12,4},{16,8},{20,12},{24,16},{28,20},{0,24},{4,28},{9,1},{1... | collective-permute-start | bytes 393224 | tf_op jit(solution)/shard_map/ppermute | solution.py:395
  58.4 0.1 bitcast_add_fusion.1
  58.5 1.3 %collective-permute-start.11 = (bf16[256,1024]{1,0:T(8,128)(2,1)S(1)}, bf16[256,1024]{1,0:T(8,128)(2,1)S(1)}, u32[]{:S(2)}, u32[]{:S(2)}) collective-permute-start(bf16[256,1024]{1,0:T(8,128)(2,1)S(1)} %get-tuple-element.41), channel_id=1, source_target_pairs={{1,0},{2,1},{3,2},{5,4},{6,5},{7,6},{9,8},{10,9},{11,10},{13,12},{... | collective-permute-start | bytes 1572872 | tf_op jit(solution)/shard_map/ppermute | solution.py:392
  59.8 4.6 %collective-permute-start.8 = (bf16[256,1024]{1,0:T(8,128)(2,1)S(1)}, bf16[256,1024]{1,0:T(8,128)(2,1)S(1)}, u32[]{:S(2)}, u32[]{:S(2)}) collective-permute-start(bf16[256,1024]{1,0:T(8,128)(2,1)S(1)} %get-tuple-element.40), channel_id=1, source_target_pairs={{0,1},{1,2},{2,3},{4,5},{5,6},{6,7},{8,9},{9,10},{10,11},{12,13},{... | collective-permute-start | bytes 1572872 | tf_op jit(solution)/shard_map/ppermute | solution.py:389
  64.4 1.5 %finish.1 = (bf16[256,512]{1,0:T(8,128)(2,1)}, f32[256,256]{1,0:T(8,128)S(1)}) custom-call(bf16[1280,1024]{1,0:T(8,128)(2,1)S(1)} %get-tuple-element.32.scores, bf16[1024,128]{1,0:T(8,128)(2,1)S(1)} %get-tuple-element.33.ups, bf16[256,512]{1,0:T(8,128)(2,1)S(1)} %get-tuple-element.23.query, bf16[1280,1024]{1,0:T(8,128)(2,1)S(1)} %get-tuple-element.31.probs, ...), custom_call_target="tpu_custom_call" | custom-call | flops 335544320 | bytes 1310720 | tf_op jit(solution)/shard_map/finish/pallas_call | solution.py:364
  65.9 0.0 collective-permute-done.15
  65.9 0.0 collective-permute-done.14
  65.9 0.1 add_convert_fusion
  66.0 0.7 fusion.2
  66.7 7.3 %collective-permute-done.11 = bf16[256,1024]{1,0:T(8,128)(2,1)S(1)} collective-permute-done((bf16[256,1024]{1,0:T(8,128)(2,1)S(1)}, bf16[256,1024]{1,0:T(8,128)(2,1)S(1)}, u32[]{:S(2)}, u32[]{:S(2)}) %collective-permute-start.11) | collective-permute-done | bytes 524320 | tf_op jit(solution)/shard_map/ppermute | solution.py:392
  74.0 1.2 %collective-permute-done.8 = bf16[256,1024]{1,0:T(8,128)(2,1)S(1)} collective-permute-done((bf16[256,1024]{1,0:T(8,128)(2,1)S(1)}, bf16[256,1024]{1,0:T(8,128)(2,1)S(1)}, u32[]{:S(2)}, u32[]{:S(2)}) %collective-permute-start.8) | collective-permute-done | bytes 524320 | tf_op jit(solution)/shard_map/ppermute | solution.py:389
  75.2 1.1 %fusion.1 = bf16[256,1024]{1,0:T(8,128)(2,1)} fusion(bf16[256,1024]{1,0:T(8,128)(2,1)S(1)} %collective-permute-done.11, bf16[256,1024]{1,0:T(8,128)(2,1)S(1)} %collective-permute-done.8, bf16[4,256,1024]{2,1,0:T(8,128)(2,1)S(1)} %get-tuple-element.27.shares), kind=kLoop, calls=%fused_computation.2 | loop fusion | flops 1572864 | bytes 2097152 | tf_op jit(solution)/shard_map/convert_element_type | solution.py:441
  (6 shorter events, 0.2 us)
Async XLA Ops:
  1.7 9.4 %collective-permute-start.2 = (bf16[256,256]{1,0:T(8,128)(2,1)S(1)}, bf16[256,256]{1,0:T(8,128)(2,1)S(1)}, u32[]{:S(2)}, u32[]{:S(2)}) collective-permute-start(bf16[256,256]{1,0:T(8,128)(2,1)S(1)} %get-tuple-element.24.refs_0_), channel_id=1, source_target_pairs={{16,0},{20,4},{24,8},{28,12},{0,16},{4,20},{8,24},{12,28},{17,1},{... | collective-permute-start | bytes 393224 | tf_op jit(solution)/shard_map/ppermute | solution.py:395
  4.8 6.4 %collective-permute-start = (bf16[256,256]{1,0:T(8,128)(2,1)S(1)}, bf16[256,256]{1,0:T(8,128)(2,1)S(1)}, u32[]{:S(2)}, u32[]{:S(2)}) collective-permute-start(bf16[256,256]{1,0:T(8,128)(2,1)S(1)} %get-tuple-element.24.refs_0_), channel_id=1, source_target_pairs={{24,0},{28,4},{0,8},{4,12},{8,16},{12,20},{16,24},{20,28},{25,1},{... | collective-permute-start | bytes 393224 | tf_op jit(solution)/shard_map/ppermute | solution.py:395
  6.3 14.4 %collective-permute-start.4 = (bf16[256,1024]{1,0:T(8,128)(2,1)}, bf16[256,1024]{1,0:T(8,128)(2,1)S(1)}, u32[]{:S(2)}, u32[]{:S(2)}) collective-permute-start(bf16[256,1024]{1,0:T(8,128)(2,1)} %own.1), channel_id=1, source_target_pairs={{0,1},{1,2},{2,3},{4,5},{5,6},{6,7},{8,9},{9,10},{10,11},{12,13},{... | collective-permute-start | bytes 1572872 | tf_op jit(solution)/shard_map/ppermute | solution.py:389
  9.8 15.2 %collective-permute-start.5 = (bf16[256,1024]{1,0:T(8,128)(2,1)}, bf16[256,1024]{1,0:T(8,128)(2,1)S(1)}, u32[]{:S(2)}, u32[]{:S(2)}) collective-permute-start(bf16[256,1024]{1,0:T(8,128)(2,1)} %own.1), channel_id=1, source_target_pairs={{1,0},{2,1},{3,2},{5,4},{6,5},{7,6},{9,8},{10,9},{11,10},{13,12},{... | collective-permute-start | bytes 1572872 | tf_op jit(solution)/shard_map/ppermute | solution.py:392
  11.1 1.4 %collective-permute-start.3 = (bf16[256,256]{1,0:T(8,128)(2,1)S(1)}, bf16[256,256]{1,0:T(8,128)(2,1)S(1)}, u32[]{:S(2)}, u32[]{:S(2)}) collective-permute-start(bf16[256,256]{1,0:T(8,128)(2,1)S(1)} %broadcast_select_fusion.2), channel_id=1, source_target_pairs={{4,0},{0,4},{12,8},{8,12},{20,16},{16,20},{28,24},{24,28},{5,1},{1... | collective-permute-start | bytes 393224 | tf_op jit(solution)/shard_map/ppermute | solution.py:398
  11.2 1.5 %collective-permute-start.1 = (bf16[256,256]{1,0:T(8,128)(2,1)S(1)}, bf16[256,256]{1,0:T(8,128)(2,1)S(1)}, u32[]{:S(2)}, u32[]{:S(2)}) collective-permute-start(bf16[256,256]{1,0:T(8,128)(2,1)S(1)} %collective-permute-done.refs_2_), channel_id=1, source_target_pairs={{4,0},{0,4},{12,8},{8,12},{20,16},{16,20},{28,24},{24,28},{5,1},{1... | collective-permute-start | bytes 393224 | tf_op jit(solution)/shard_map/ppermute | solution.py:398
  20.7 14.0 %collective-permute-start.6 = (bf16[256,1024]{1,0:T(8,128)(2,1)S(1)}, bf16[256,1024]{1,0:T(8,128)(2,1)S(1)}, u32[]{:S(2)}, u32[]{:S(2)}) collective-permute-start(bf16[256,1024]{1,0:T(8,128)(2,1)S(1)} %send_up2.1), channel_id=1, source_target_pairs={{0,1},{1,2},{2,3},{4,5},{5,6},{6,7},{8,9},{9,10},{10,11},{12,13},{... | collective-permute-start | bytes 1572872 | tf_op jit(solution)/shard_map/ppermute | solution.py:389
  25.1 14.1 %collective-permute-start.9 = (bf16[256,1024]{1,0:T(8,128)(2,1)S(1)}, bf16[256,1024]{1,0:T(8,128)(2,1)S(1)}, u32[]{:S(2)}, u32[]{:S(2)}) collective-permute-start(bf16[256,1024]{1,0:T(8,128)(2,1)S(1)} %send_down2.1), channel_id=1, source_target_pairs={{1,0},{2,1},{3,2},{5,4},{6,5},{7,6},{9,8},{10,9},{11,10},{13,12},{... | collective-permute-start | bytes 1572872 | tf_op jit(solution)/shard_map/ppermute | solution.py:392
  34.8 13.3 %collective-permute-start.7 = (bf16[256,1024]{1,0:T(8,128)(2,1)S(1)}, bf16[256,1024]{1,0:T(8,128)(2,1)S(1)}, u32[]{:S(2)}, u32[]{:S(2)}) collective-permute-start(bf16[256,1024]{1,0:T(8,128)(2,1)S(1)} %send_up3.1), channel_id=1, source_target_pairs={{0,1},{1,2},{2,3},{4,5},{5,6},{6,7},{8,9},{9,10},{10,11},{12,13},{... | collective-permute-start | bytes 1572872 | tf_op jit(solution)/shard_map/ppermute | solution.py:389
  39.3 13.0 %collective-permute-start.10 = (bf16[256,1024]{1,0:T(8,128)(2,1)S(1)}, bf16[256,1024]{1,0:T(8,128)(2,1)S(1)}, u32[]{:S(2)}, u32[]{:S(2)}) collective-permute-start(bf16[256,1024]{1,0:T(8,128)(2,1)S(1)} %send_down3.1), channel_id=1, source_target_pairs={{1,0},{2,1},{3,2},{5,4},{6,5},{7,6},{9,8},{10,9},{11,10},{13,12},{... | collective-permute-start | bytes 1572872 | tf_op jit(solution)/shard_map/ppermute | solution.py:392
  54.7 1.4 %collective-permute-start.13 = (bf16[256,256]{1,0:T(8,128)(2,1)S(1)}, bf16[256,256]{1,0:T(8,128)(2,1)S(1)}, u32[]{:S(2)}, u32[]{:S(2)}) collective-permute-start(bf16[256,256]{1,0:T(8,128)(2,1)S(1)} %get-tuple-element.38), channel_id=1, source_target_pairs={{4,0},{0,4},{12,8},{8,12},{20,16},{16,20},{28,24},{24,28},{5,1},{1... | collective-permute-start | bytes 393224 | tf_op jit(solution)/shard_map/ppermute | solution.py:398
  54.8 1.5 %collective-permute-start.12 = (bf16[256,256]{1,0:T(8,128)(2,1)S(1)}, bf16[256,256]{1,0:T(8,128)(2,1)S(1)}, u32[]{:S(2)}, u32[]{:S(2)}) collective-permute-start(bf16[256,256]{1,0:T(8,128)(2,1)S(1)} %get-tuple-element.36), channel_id=1, source_target_pairs={{4,0},{0,4},{12,8},{8,12},{20,16},{16,20},{28,24},{24,28},{5,1},{1... | collective-permute-start | bytes 393224 | tf_op jit(solution)/shard_map/ppermute | solution.py:398
  56.4 9.5 %collective-permute-start.15 = (bf16[256,256]{1,0:T(8,128)(2,1)S(1)}, bf16[256,256]{1,0:T(8,128)(2,1)S(1)}, u32[]{:S(2)}, u32[]{:S(2)}) collective-permute-start(bf16[256,256]{1,0:T(8,128)(2,1)S(1)} %get-tuple-element.47), channel_id=1, source_target_pairs={{16,0},{20,4},{24,8},{28,12},{0,16},{4,20},{8,24},{12,28},{17,1},{... | collective-permute-start | bytes 393224 | tf_op jit(solution)/shard_map/ppermute | solution.py:395
  56.9 9.0 %collective-permute-start.14 = (bf16[256,256]{1,0:T(8,128)(2,1)S(1)}, bf16[256,256]{1,0:T(8,128)(2,1)S(1)}, u32[]{:S(2)}, u32[]{:S(2)}) collective-permute-start(bf16[256,256]{1,0:T(8,128)(2,1)S(1)} %get-tuple-element.46), channel_id=1, source_target_pairs={{8,0},{12,4},{16,8},{20,12},{24,16},{28,20},{0,24},{4,28},{9,1},{1... | collective-permute-start | bytes 393224 | tf_op jit(solution)/shard_map/ppermute | solution.py:395
  58.5 15.5 %collective-permute-start.11 = (bf16[256,1024]{1,0:T(8,128)(2,1)S(1)}, bf16[256,1024]{1,0:T(8,128)(2,1)S(1)}, u32[]{:S(2)}, u32[]{:S(2)}) collective-permute-start(bf16[256,1024]{1,0:T(8,128)(2,1)S(1)} %get-tuple-element.41), channel_id=1, source_target_pairs={{1,0},{2,1},{3,2},{5,4},{6,5},{7,6},{9,8},{10,9},{11,10},{13,12},{... | collective-permute-start | bytes 1572872 | tf_op jit(solution)/shard_map/ppermute | solution.py:392
  59.8 15.4 %collective-permute-start.8 = (bf16[256,1024]{1,0:T(8,128)(2,1)S(1)}, bf16[256,1024]{1,0:T(8,128)(2,1)S(1)}, u32[]{:S(2)}, u32[]{:S(2)}) collective-permute-start(bf16[256,1024]{1,0:T(8,128)(2,1)S(1)} %get-tuple-element.40), channel_id=1, source_target_pairs={{0,1},{1,2},{2,3},{4,5},{5,6},{6,7},{8,9},{9,10},{10,11},{12,13},{... | collective-permute-start | bytes 1572872 | tf_op jit(solution)/shard_map/ppermute | solution.py:389

commit v2 on v1

--- a/solution.py
+++ b/solution.py
@@ -7,6 +7,7 @@
 from jax.experimental.pallas import tpu as pltpu
 from jax.sharding import PartitionSpec as P
 
+
 HEAD_DIM = 128
 LOWEST = -1e30
 LOG2_E = 1.4426950408889634
@@ -31,6 +32,19 @@
 
 def columns_at(proj, index, share):
     return proj.at[:, pl.ds(pl.multiple_of(index * share, share), share)]
+
+
+PARTS = 2
+
+
+def parts_of(rows, width):
+    return [pltpu.VMEM((rows // PARTS, width), BF16)] * PARTS
+
+
+def in_parts(refs, whole):
+    rows = refs[0].shape[0]
+    for index, ref in enumerate(refs):
+        ref[...] = whole[index * rows : (index + 1) * rows].astype(BF16)
 
 
 def main(array):
@@ -88,8 +102,8 @@
 
 def forward_kernel(limits, query, proj, *refs, reach, groups):
     blocks = refs[: reach + 1]
-    attention, turned, probs, lead, local = refs[reach + 1 : reach + 6]
-    (sem,) = refs[reach + 6 :]
+    attention, turned, probs, local = refs[reach + 1 : reach + 5]
+    leads, sem = refs[reach + 5 : -1], refs[-1]
     rows, width = query.shape
     heads = width // HEAD_DIM
     size = lax.axis_size("head")
@@ -132,7 +146,7 @@
         attention[:, pl.ds(head * HEAD_DIM, HEAD_DIM)] = mixed.T.astype(BF16)
         scores = following
     copy.wait()
-    lead[0] = dot(attention[...], columns_at(local, place, lead.shape[2])[...]).astype(BF16)
+    in_parts(leads, dot(attention[...], columns_at(local, place, leads[0].shape[1])[...]))
 
 
 def forward(limits, query, out_proj, blocks, groups, size):
@@ -141,150 +155,192 @@
     reach = len(blocks) - 1
     share = out_proj.shape[1] // size
     span = (reach + 1) * rows
-    return pl.pallas_call(
+    outs = pl.pallas_call(
         functools.partial(forward_kernel, reach=reach, groups=groups),
         in_specs=[WHOLE, WHOLE, MAIN] + [WHOLE] * (reach + 1),
-        out_specs=[WHOLE] * 5,
+        out_specs=[WHOLE] * (4 + PARTS),
         out_shape=[
             pltpu.VMEM((rows, width), BF16),
             pltpu.VMEM((width, rows), BF16),
             pltpu.VMEM((span, heads * rows), BF16),
-            pltpu.VMEM((1, rows, share), BF16),
             pltpu.VMEM(out_proj.shape, BF16),
-        ],
+        ]
+        + parts_of(rows, share),
         scratch_shapes=[pltpu.SemaphoreType.DMA],
         compiler_params=PARAMS,
         cost_estimate=estimate(4 * rows * span * width, 8 * rows * span),
         name="forward",
     )(limits, query, main(out_proj), *blocks)
-
-
-def send_kernel(shares, passed, out, *, end, inner):
+    return outs[:4], outs[4:]
+
+
+def at_end():
     z = lax.axis_index("head")
-
-    @pl.when(z == end)
-    def _():
-        out[...] = shares[0]
-
-    if inner is None:
-
-        @pl.when(z != end)
+    return (z == 0) | (z == lax.axis_size("head") - 1)
+
+
+def either_kernel(*refs):
+    count = (len(refs) - 1) // 2
+    ends, inner, outs = refs[:count], refs[count], refs[count + 1 :]
+    rows = outs[0].shape[0]
+    for index, out in enumerate(outs):
+
+        @pl.when(at_end())
         def _():
-            out[...] = passed[...]
-
-    else:
-
-        @pl.when(z == inner)
+            out[...] = ends[index][...]
+
+        @pl.when(jnp.logical_not(at_end()))
         def _():
-            out[...] = passed[...]
-
-        @pl.when((z != end) & (z != inner))
-        def _():
-            out[...] = shares[0] + passed[...]
-
-
-def send(shares, passed, end, inner, name):
+            out[...] = inner[pl.ds(index * rows, rows), :]
+
+
+def either(ends, inner):
+    rows, width = inner.shape
+    count = len(ends)
     return pl.pallas_call(
-        functools.partial(send_kernel, end=end, inner=inner),
-        in_specs=[WHOLE] * 2,
-        out_specs=WHOLE,
-        out_shape=pltpu.VMEM(passed.shape, BF16),
-        compiler_params=PARAMS,
-        cost_estimate=estimate(passed.size, 6 * passed.size),
-        name=name,
-    )(shares, passed)
-
-
-def middle_kernel(attention, own, above, below, proj, shares, partial, extra, sem):
+        either_kernel,
+        in_specs=[WHOLE] * (count + 1),
+        out_specs=[WHOLE] * count,
+        out_shape=[pltpu.VMEM((rows // count, width), BF16)] * count,
+        compiler_params=PARAMS,
+        cost_estimate=estimate(inner.size, 6 * inner.size),
+    )(*ends, inner)
+
+
+def split_kernel(whole, *parts):
+    in_parts(parts, whole[...])
+
+
+def split(whole):
+    return pl.pallas_call(
+        split_kernel,
+        in_specs=[WHOLE],
+        out_specs=[WHOLE] * PARTS,
+        out_shape=parts_of(*whole.shape),
+        compiler_params=PARAMS,
+        cost_estimate=estimate(whole.size, 4 * whole.size),
+        name="split",
+    )(whole)
+
+
+def total_kernel(own, *refs):
+    parts, out, buffer, sems = refs[:-3], refs[-3], refs[-2], refs[-1]
+    rows = parts[0].shape[0]
+    copies = []
+    for index in range(PARTS):
+        spot = pl.ds(index * rows, rows)
+        value = own[spot, :].astype(F32)
+        for part in parts[index::PARTS]:
+            value = value + part[...].astype(F32)
+        buffer[spot, :] = value.astype(BF16)
+        copies.append(pltpu.make_async_copy(buffer.at[spot], out.at[spot], sems.at[index]))
+        copies[-1].start()
+    for copy in copies:
+        copy.wait()
+
+
+def total_of(own, *parts):
+    return pl.pallas_call(
+        total_kernel,
+        in_specs=[WHOLE] * (len(parts) + 1),
+        out_specs=MAIN,
+        out_shape=jax.ShapeDtypeStruct(own.shape, BF16),
+        scratch_shapes=[pltpu.VMEM(own.shape, BF16), pltpu.SemaphoreType.DMA((PARTS,))],
+        compiler_params=PARAMS,
+        cost_estimate=estimate(3 * own.size, 8 * own.size),
+        name="total",
+    )(own, *parts)
+
+
+def middle_kernel(attention, own, paired, proj, own_share, partial, *refs):
+    far_shares, pair_shares, extra, sem = refs[:PARTS], refs[PARTS:-2], refs[-2], refs[-1]
     size = lax.axis_size("head")
     z = lax.axis_index("head")
     share = extra.shape[1]
     copy = pltpu.make_async_copy(own, extra, sem)
     copy.start()
-    places = [lax.rem(z + size // 2, size), jnp.minimum(z + 1, size - 1), jnp.maximum(z - 1, 0), z]
-    total = None
-    for slot, source in enumerate((None, below, above, extra)):
-        block = columns_at(proj, places[slot], share)[...]
-        shares[slot] = dot(attention[...], block).astype(BF16)
-        if source is extra:
-            copy.wait()
-        if source is not None:
-            part = dot(block, source[...], NT)
-            total = part if total is None else total + part
-    partial[...] = total
-
-
-def middle(attention, own, above, below, out_proj, size):
+    block = columns_at(proj, lax.rem(z + size // 2, size), share)
+    in_parts(far_shares, dot(attention[...], block[...]))
+    block = columns_at(proj, z + 1 - 2 * lax.rem(z, 2), share)
+    in_parts(pair_shares, dot(attention[...], block[...]))
+    total = dot(block[...], paired[...], NT)
+    block = columns_at(proj, z, share)
+    own_share[...] = dot(attention[...], block[...]).astype(BF16)
+    copy.wait()
+    partial[...] = total + dot(block[...], extra[...], NT)
+
+
+def middle(attention, own, paired, out_proj):
     rows, width = attention.shape
-    share = out_proj.shape[1] // size
-    return pl.pallas_call(
+    share = own.shape[1]
+    outs = pl.pallas_call(
         middle_kernel,
-        in_specs=[WHOLE, MAIN, WHOLE, WHOLE, WHOLE],
-        out_specs=[WHOLE] * 2,
-        out_shape=[
-            pltpu.VMEM((4, rows, share), BF16),
-            pltpu.VMEM((width, rows), F32),
-        ],
+        in_specs=[WHOLE, MAIN, WHOLE, WHOLE],
+        out_specs=[WHOLE] * (2 + 2 * PARTS),
+        out_shape=[pltpu.VMEM(own.shape, BF16), pltpu.VMEM((width, rows), F32)]
+        + parts_of(rows, share) * 2,
         scratch_shapes=[pltpu.VMEM(own.shape, BF16), pltpu.SemaphoreType.DMA],
         compiler_params=PARAMS,
-        cost_estimate=estimate(14 * rows * share * width, 8 * share * width),
+        cost_estimate=estimate(10 * own.size * width, 8 * own.size),
         name="middle",
-    )(attention, main(own), above, below, out_proj)
-
-
-def far_kernel(partial, above, below, proj, out):
+    )(attention, main(own), paired, out_proj)
+    return outs[0], outs[1], outs[2 : 2 + PARTS], outs[2 + PARTS :]
+
+
+def add_term(target, partial, block, sources):
+    rows = sources[0].shape[0]
+    for index, source in enumerate(sources):
+        spot = pl.ds(index * rows, rows)
+        target[:, spot] = (partial[:, spot] + dot(block[...], source[...], NT)).astype(target.dtype)
+
+
+def far_kernel(partial, proj, out, *, sources):
     size = lax.axis_size("head")
     z = lax.axis_index("head")
-    share = above.shape[1]
-    block = columns_at(proj, lax.rem(z + size // 2, size), share)
-
-    @pl.when(z >= size // 2)
+    ends, inner = sources[:PARTS], sources[PARTS:]
+    block = columns_at(proj, lax.rem(z + size // 2, size), ends[0].shape[1])
+
+    @pl.when(at_end())
     def _():
-        out[...] = partial[...] + dot(block[...], above[...], NT)
-
-    @pl.when(z < size // 2)
+        add_term(out, partial, block, ends)
+
+    @pl.when(jnp.logical_not(at_end()))
     def _():
-        out[...] = partial[...] + dot(block[...], below[...], NT)
-
-
-def far(partial, above, below, out_proj):
-    rows, share = above.shape
-    width = out_proj.shape[0]
+        add_term(out, partial, block, inner)
+
+
+def far(partial, ends, inner, out_proj):
+    width, rows = partial.shape
     return pl.pallas_call(
-        far_kernel,
-        in_specs=[WHOLE] * 4,
+        lambda partial, proj, *refs: far_kernel(partial, proj, refs[-1], sources=refs[:-1]),
+        in_specs=[WHOLE] * (2 + 2 * PARTS),
         out_specs=WHOLE,
         out_shape=pltpu.VMEM((width, rows), F32),
         compiler_params=PARAMS,
-        cost_estimate=estimate(2 * rows * share * width, 2 * share * width),
+        cost_estimate=estimate(2 * rows * width * ends[0].shape[1], 8 * rows * width),
         name="far",
-    )(partial, above, below, out_proj)
-
-
-def backward_kernel(partial, above, below, query, turned, probs, proj, *refs, reach, groups):
+    )(partial, out_proj, *ends, *inner)
+
+
+def backward_kernel(partial, inner, query, turned, probs, proj, *refs, reach, groups):
+    ends, refs = refs[:PARTS], refs[PARTS:]
     blocks = refs[: reach + 1]
     grads = refs[reach + 1 : 2 * reach + 1]
     scores, ups, upstream = refs[2 * reach + 1 :]
     rows, width = query.shape
     heads = width // HEAD_DIM
     ratio = heads // groups
-    size = lax.axis_size("head")
-    z = lax.axis_index("head")
-    share = above.shape[1]
+    place = lax.axis_size("head") - 1 - lax.axis_index("head")
     scale = HEAD_DIM ** (-0.5)
-    block = columns_at(proj, size - 1 - z, share)
-
-    @pl.when(z == size - 1)
+    block = columns_at(proj, place, inner.shape[1])
+
+    @pl.when(at_end())
     def _():
-        upstream[...] = (partial[...] + dot(block[...], above[...], NT)).astype(BF16)
-
-    @pl.when(z == 0)
+        add_term(upstream, partial, block, ends)
+
+    @pl.when(jnp.logical_not(at_end()))
     def _():
-        upstream[...] = (partial[...] + dot(block[...], below[...], NT)).astype(BF16)
-
-    @pl.when((z > 0) & (z < size - 1))
-    def _():
-        upstream[...] = partial[...].astype(BF16)
+        add_term(upstream, partial, block, [inner])
 
     for head in range(heads):
         up = upstream[pl.ds(head * HEAD_DIM, HEAD_DIM), :]
@@ -313,14 +369,14 @@
             ).astype(BF16)
 
 
-def backward(partial, above, below, query, turned, probs, out_proj, blocks, groups):
+def backward(partial, ends, inner, query, turned, probs, out_proj, blocks, groups):
     rows, width = query.shape
     heads = width // HEAD_DIM
     reach = len(blocks) - 1
     span = (reach + 1) * rows
     outs = pl.pallas_call(
         functools.partial(backward_kernel, reach=reach, groups=groups),
-        in_specs=[WHOLE] * (reach + 8),
+        in_specs=[WHOLE] * (reach + 7 + PARTS),
         out_specs=[WHOLE] * (reach + 2),
         out_shape=[pltpu.VMEM((rows, 2 * groups * HEAD_DIM), BF16)] * reach
         + [
@@ -331,7 +387,7 @@
         compiler_params=PARAMS,
         cost_estimate=estimate(8 * rows * span * width, 8 * rows * span),
         name="backward",
-    )(partial, above, below, query, turned, probs, out_proj, *blocks)
+    )(partial, inner, query, turned, probs, out_proj, *ends, *blocks)
     return outs[:reach], outs[reach], outs[reach + 1]
 
 
@@ -385,14 +441,15 @@
     even = lax.axis_index("seq") % 2 == 0
     nothing = jnp.zeros((), BF16)
 
-    def climb(array):
-        return lax.ppermute(array, "head", [(i, i + 1) for i in range(size - 1)])
-
-    def descend(array):
-        return lax.ppermute(array, "head", [(i + 1, i) for i in range(size - 1)])
+    def outer(array):
+        return lax.ppermute(array, "head", [(i ^ 1, i) for i in range(size)])
+
+    def inner(array):
+        return lax.ppermute(array, "head", [(1, 2), (2, 1)])
 
     def shifted(array, step):
-        return lax.ppermute(array, "seq", [((i - step) % devices, i) for i in range(devices)])
+        pairs = [((i - step) % devices, i) for i in range(devices)]
+        return lax.ppermute(array, "seq", pairs)
 
     def swapped(array):
         return lax.ppermute(array, "seq", [(i ^ 1, i) for i in range(devices)])
@@ -406,22 +463,25 @@
         blocks.append(jnp.where(even, traded[(step + 1) % half], traded[step]))
         blocks.append(fetched[step + 1])
 
-    above1, below1 = climb(grad_out), descend(grad_out)
-    attention, turned, probs, lead, proj = forward(limits, query, out_proj, blocks, groups, size)
-
-    above2 = climb(send(lead, above1, 0, None, "send_up2"))
-    below2 = descend(send(lead, below1, size - 1, None, "send_down2"))
-    rest, partial = middle(attention, grad_out, above1, below1, proj, size)
-
-    above3 = climb(send(rest, above2, 0, size // 2, "send_up3"))
-    below3 = descend(send(rest, below2, size - 1, size // 2 - 1, "send_down3"))
-    partial = far(partial, above2, below2, proj)
-
+    both = range(PARTS)
+    outer1, inner1 = outer(grad_out), inner(grad_out)
+    (attention, turned, probs, proj), lead = forward(
+        limits, query, out_proj, blocks, groups, size
+    )
+    split1 = split(outer1)
+    inner2 = [inner(split1[i]) for i in both]
+    send2 = either(lead, inner1)
+    outer2 = [outer(send2[i]) for i in both]
+    own_share, partial, far_share, pair_share = middle(attention, grad_out, outer1, proj)
+    send3 = [either([far_share[i]], inner2[i])[0] for i in both]
+    outer3 = [outer(send3[i]) for i in both]
+    inner3 = [inner(far_share[i] + outer2[i]) for i in both]
+    partial = far(partial, outer2, inner2, proj)
     sent, scores, ups = backward(
-        partial, above3, below3, query, turned, probs, proj, blocks, groups
+        partial, outer3, inner1, query, turned, probs, proj, blocks, groups
     )
-    above4 = climb(rest[1] + above3)
-    below4 = descend(rest[2] + below3)
+    inner4 = [inner(lead[i] + outer3[i]) for i in both]
+    outer4 = [outer(pair_share[i] + inner3[i]) for i in both]
 
     taken = [swapped(sent[2 * step]) for step in range(half)]
     total = []
@@ -438,7 +498,7 @@
         own = own + part.astype(F32)
     grad_keys = own[:, : groups * HEAD_DIM].astype(BF16)
     grad_values = own[:, groups * HEAD_DIM :].astype(BF16)
-    layer_out = (rest[3].astype(F32) + above4.astype(F32) + below4.astype(F32)).astype(BF16)
+    layer_out = total_of(own_share, *outer4, *inner4)
     return layer_out, grad_queries, grad_keys, grad_values
 
 

time: 76.5 us -> 82.5 us (1.078)
  the two profiles are of different devices: /device:TPU:0 before, /device:TPU:12 now
where the time goes in v2:
time: 82.5 us; the launch traced here: 82.2 us
  waiting for transfers between devices  36.4 us (44%)
  starting transfers between devices  31.3 us (38%)
  Pallas kernels  12.3 us (15%)
  between operations  0.95 us (1%)
    ppermute x7, starting transfers between devices, inner(): return lax.ppermute(array, 'head', [(1, 2), (2, 1)])  22.1 us
    ppermute x7, waiting for transfers between devices, outer(): return lax.ppermute(array, 'head', [(i ^ 1, i) for i in range(size)])  18.9 us
    ppermute x7, waiting for transfers between devices, inner(): return lax.ppermute(array, 'head', [(1, 2), (2, 1)])  16.4 us
    ppermute x4, starting transfers between devices, shifted(): return lax.ppermute(array, 'seq', pairs)  5.07 us
    pallas_call x1, Pallas kernels, forward(): pl.pallas_call(functools.partial(forward_kernel, reach=reach, groups=grou...  3.04 us
    ppermute x7, starting transfers between devices, outer(): return lax.ppermute(array, 'head', [(i ^ 1, i) for i in range(size)])  2.95 us
    pallas_call x1, Pallas kernels, middle(): pl.pallas_call(middle_kernel, in_specs=[WHOLE, MAIN, WHOLE, WHOLE], out_s...  2.48 us
    pallas_call x1, Pallas kernels, backward(): pl.pallas_call(functools.partial(backward_kernel, reach=reach, groups=gro...  2.43 us
  transfers between devices with their start and end apart: 22, of which 11 were waited for; matrix products, arithmetic and copies ran while one was open for 1% of the time, Pallas kernels for 11%

profile of v2, /device:TPU:12, one launch (start us, length us, event | category | flops | bytes accessed | tf_op | source)
XLA Modules:
  0.0 82.2 jit_solution(6321035171104178882)
XLA Ops:
  0.6 0.5 collective-permute-start.4
  1.1 1.1 %stage.1 = (bf16[256,256]{1,0:T(8,128)(2,1)S(1)}, bf16[256,512]{1,0:T(8,128)(2,1)S(1)}, s32[20,256]{1,0:T(8,128)S(1)}) custom-call(bf16[256,128]{1,0:T(8,128)(2,1)} %keys.1, bf16[256,128]{1,0:T(8,128)(2,1)} %values.1, bf16[256,512]{1,0:T(8,128)(2,1)} %queries.1, s32[4]{0:T(128)} %windows.1, s32[8]{0:T(128)} %order.1), custom_call_target="tpu_custom_call" | custom-call | flops 32768 | bytes 262144 | tf_op jit(solution)/shard_map/stage/pallas_call | solution.py:83
  2.2 0.1 collective-permute-start.2
  2.4 1.9 %collective-permute-start = (bf16[256,256]{1,0:T(8,128)(2,1)S(1)}, bf16[256,256]{1,0:T(8,128)(2,1)S(1)}, u32[]{:S(2)}, u32[]{:S(2)}) collective-permute-start(bf16[256,256]{1,0:T(8,128)(2,1)S(1)} %get-tuple-element.33.refs_0_.refs_2_), channel_id=1, source_target_pairs={{24,0},{28,4},{0,8},{4,12},{8,16},{12,20},{16,24},{20,28},{25,1},{... | collective-permute-start | bytes 393224 | tf_op jit(solution)/shard_map/ppermute | solution.py:452
  4.3 4.6 %collective-permute-start.5 = (bf16[256,1024]{1,0:T(8,128)(2,1)}, bf16[256,1024]{1,0:T(8,128)(2,1)S(1)}, u32[]{:S(2)}, u32[]{:S(2)}) collective-permute-start(bf16[256,1024]{1,0:T(8,128)(2,1)} %own.1), channel_id=1, source_target_pairs={{1,2},{2,1},{5,6},{6,5},{9,10},{10,9},{13,14},{14,13},{17,18},{18,... | collective-permute-start | bytes 1572872 | tf_op jit(solution)/shard_map/ppermute | solution.py:448
  8.9 1.1 %collective-permute-done.2.refs_4_.refs_6_ = bf16[256,256]{1,0:T(8,128)(2,1)S(1)} collective-permute-done((bf16[256,256]{1,0:T(8,128)(2,1)S(1)}, bf16[256,256]{1,0:T(8,128)(2,1)S(1)}, u32[]{:S(2)}, u32[]{:S(2)}) %collective-permute-start.2) | collective-permute-done | bytes 131104 | tf_op jit(solution)/shard_map/ppermute | solution.py:452
  10.1 0.1 collective-permute-start.3
  10.2 0.0 collective-permute-done.refs_2_.refs_4_
  10.2 0.5 collective-permute-start.1
  10.7 3.9 %collective-permute-done.4.paired.whole = bf16[256,1024]{1,0:T(8,128)(2,1)S(1)} collective-permute-done((bf16[256,1024]{1,0:T(8,128)(2,1)}, bf16[256,1024]{1,0:T(8,128)(2,1)S(1)}, u32[]{:S(2)}, u32[]{:S(2)}) %collective-permute-start.4) | collective-permute-done | bytes 524320 | tf_op jit(solution)/shard_map/ppermute | solution.py:445
  14.6 3.5 %collective-permute-start.12 = (bf16[128,1024]{1,0:T(8,128)(2,1)S(1)}, bf16[128,1024]{1,0:T(8,128)(2,1)S(1)}, u32[]{:S(2)}, u32[]{:S(2)}) collective-permute-start(bf16[128,1024]{1,0:T(8,128)(2,1)S(1)} %get-tuple-element.45), channel_id=1, source_target_pairs={{1,2},{2,1},{5,6},{6,5},{9,10},{10,9},{13,14},{14,13},{17,18},{18,... | collective-permute-start | bytes 786440 | tf_op jit(solution)/shard_map/ppermute | solution.py:448
  18.1 2.4 %collective-permute-start.15 = (bf16[128,1024]{1,0:T(8,128)(2,1)S(1)}, bf16[128,1024]{1,0:T(8,128)(2,1)S(1)}, u32[]{:S(2)}, u32[]{:S(2)}) collective-permute-start(bf16[128,1024]{1,0:T(8,128)(2,1)S(1)} %get-tuple-element.46), channel_id=1, source_target_pairs={{1,2},{2,1},{5,6},{6,5},{9,10},{10,9},{13,14},{14,13},{17,18},{18,... | collective-permute-start | bytes 786440 | tf_op jit(solution)/shard_map/ppermute | solution.py:448
  20.5 0.0 collective-permute-done.3
  20.5 0.0 collective-permute-done.1
  20.5 3.0 %forward.1 = (bf16[256,512]{1,0:T(8,128)(2,1)S(1)}, bf16[512,256]{1,0:T(8,128)(2,1)S(1)}, bf16[1280,1024]{1,0:T(8,128)(2,1)S(1)}, bf16[512,4096]{1,0:T(8,128)(2,...) custom-call(s32[20,256]{1,0:T(8,128)S(1)} %get-tuple-element.31.limits, ...), custom_call_target="tpu_custom_call" | custom-call | flops 671088640 | bytes 2621440 | tf_op jit(solution)/shard_map/forward/pallas_call | solution.py:158
  23.6 0.0 collective-permute-done.5.refs_2_.inner
  23.6 0.1 collective-permute-start.6
  23.7 2.0 %collective-permute-start.9 = (bf16[128,1024]{1,0:T(8,128)(2,1)S(1)}, bf16[128,1024]{1,0:T(8,128)(2,1)S(1)}, u32[]{:S(2)}, u32[]{:S(2)}) collective-permute-start(bf16[128,1024]{1,0:T(8,128)(2,1)S(1)} %get-tuple-element.44), channel_id=1, source_target_pairs={{1,0},{0,1},{3,2},{2,3},{5,4},{4,5},{7,6},{6,7},{9,8},{8,9},{11,10... | collective-permute-start | bytes 786440 | tf_op jit(solution)/shard_map/ppermute | solution.py:445
  25.7 2.5 %middle.1 = (bf16[256,1024]{1,0:T(8,128)(2,1)S(1)}, f32[512,256]{1,0:T(8,128)S(1)}, bf16[128,1024]{1,0:T(8,128)(2,1)S(1)}, bf16[128,1024]{1,0:T(8,128)(2,1)S(1)}...) custom-call(bf16[256,512]{1,0:T(8,128)(2,1)S(1)} %get-tuple-element.34.attention, bf16[256,1024]{1,0:T(8,128)(2,1)} %own.1, ...), custom_call_target="tpu_custom_call" | custom-call | flops 1342177280 | bytes 2097152 | tf_op jit(solution)/shard_map/middle/pallas_call | solution.py:276
  28.2 0.0 collective-permute-done.12.refs_1_.refs_2_
  28.3 0.1 collective-permute-start.13
  28.4 3.0 %collective-permute-done.15.refs_1_.refs_3_ = bf16[128,1024]{1,0:T(8,128)(2,1)S(1)} collective-permute-done((bf16[128,1024]{1,0:T(8,128)(2,1)S(1)}, bf16[128,1024]{1,0:T(8,128)(2,1)S(1)}, u32[]{:S(2)}, u32[]{:S(2)}) %collective-permute-start.15) | collective-permute-done | bytes 262176 | tf_op jit(solution)/shard_map/ppermute | solution.py:448
  31.4 0.1 collective-permute-start.16
  31.5 1.4 %collective-permute-done.6.refs_0_ = bf16[128,1024]{1,0:T(8,128)(2,1)S(1)} collective-permute-done((bf16[128,1024]{1,0:T(8,128)(2,1)S(1)}, bf16[128,1024]{1,0:T(8,128)(2,1)S(1)}, u32[]{:S(2)}, u32[]{:S(2)}) %collective-permute-start.6) | collective-permute-done | bytes 262176 | tf_op jit(solution)/shard_map/ppermute | solution.py:445
  32.9 5.6 %collective-permute-done.9.refs_1_ = bf16[128,1024]{1,0:T(8,128)(2,1)S(1)} collective-permute-done((bf16[128,1024]{1,0:T(8,128)(2,1)S(1)}, bf16[128,1024]{1,0:T(8,128)(2,1)S(1)}, u32[]{:S(2)}, u32[]{:S(2)}) %collective-permute-start.9) | collective-permute-done | bytes 262176 | tf_op jit(solution)/shard_map/ppermute | solution.py:445
  38.5 0.7 far.1.partial
  39.2 4.9 %collective-permute-done.13.refs_0_ = bf16[128,1024]{1,0:T(8,128)(2,1)S(1)} collective-permute-done((bf16[128,1024]{1,0:T(8,128)(2,1)S(1)}, bf16[128,1024]{1,0:T(8,128)(2,1)S(1)}, u32[]{:S(2)}, u32[]{:S(2)}) %collective-permute-start.13) | collective-permute-done | bytes 262176 | tf_op jit(solution)/shard_map/ppermute | solution.py:445
  44.1 3.1 %collective-permute-done.16.refs_1_ = bf16[128,1024]{1,0:T(8,128)(2,1)S(1)} collective-permute-done((bf16[128,1024]{1,0:T(8,128)(2,1)S(1)}, bf16[128,1024]{1,0:T(8,128)(2,1)S(1)}, u32[]{:S(2)}, u32[]{:S(2)}) %collective-permute-start.16) | collective-permute-done | bytes 262176 | tf_op jit(solution)/shard_map/ppermute | solution.py:445
  47.2 2.4 %backward.1 = (bf16[256,256]{1,0:T(8,128)(2,1)S(1)}, bf16[256,256]{1,0:T(8,128)(2,1)S(1)}, bf16[256,256]{1,0:T(8,128)(2,1)S(1)}, bf16[256,256]{1,0:T(8,128)(2,1)...) custom-call(f32[512,256]{1,0:T(8,128)S(1)} %far.1.partial, ...), custom_call_target="tpu_custom_call" | custom-call | flops 1342177280 | bytes 2621440 | tf_op jit(solution)/shard_map/backward/pallas_call | solution.py:377
  49.6 0.1 collective-permute-start.19
  49.7 0.5 collective-permute-start.18
  50.2 0.1 add.38
  50.3 3.5 %collective-permute-start.7 = (bf16[128,1024]{1,0:T(8,128)(2,1)S(1)}, bf16[128,1024]{1,0:T(8,128)(2,1)S(1)}, u32[]{:S(2)}, u32[]{:S(2)}) collective-permute-start(bf16[128,1024]{1,0:T(8,128)(2,1)S(1)} %add.38), channel_id=1, source_target_pairs={{1,2},{2,1},{5,6},{6,5},{9,10},{10,9},{13,14},{14,13},{17,18},{18,... | collective-permute-start | bytes 786440 | tf_op jit(solution)/shard_map/ppermute | solution.py:448
  53.8 0.1 add.40
  53.8 2.4 %collective-permute-start.10 = (bf16[128,1024]{1,0:T(8,128)(2,1)S(1)}, bf16[128,1024]{1,0:T(8,128)(2,1)S(1)}, u32[]{:S(2)}, u32[]{:S(2)}) collective-permute-start(bf16[128,1024]{1,0:T(8,128)(2,1)S(1)} %add.40), channel_id=1, source_target_pairs={{1,2},{2,1},{5,6},{6,5},{9,10},{10,9},{13,14},{14,13},{17,18},{18,... | collective-permute-start | bytes 786440 | tf_op jit(solution)/shard_map/ppermute | solution.py:448
  56.2 0.0 collective-permute-done.19
  56.2 0.0 collective-permute-done.18
  56.3 0.6 collective-permute-start.21
  56.8 2.5 %collective-permute-start.20 = (bf16[256,256]{1,0:T(8,128)(2,1)S(1)}, bf16[256,256]{1,0:T(8,128)(2,1)S(1)}, u32[]{:S(2)}, u32[]{:S(2)}) collective-permute-start(bf16[256,256]{1,0:T(8,128)(2,1)S(1)} %get-tuple-element.62), channel_id=1, source_target_pairs={{8,0},{12,4},{16,8},{20,12},{24,16},{28,20},{0,24},{4,28},{9,1},{1... | collective-permute-start | bytes 393224 | tf_op jit(solution)/shard_map/ppermute | solution.py:452
  59.3 2.1 %collective-permute-done.7 = bf16[128,1024]{1,0:T(8,128)(2,1)S(1)} collective-permute-done((bf16[128,1024]{1,0:T(8,128)(2,1)S(1)}, bf16[128,1024]{1,0:T(8,128)(2,1)S(1)}, u32[]{:S(2)}, u32[]{:S(2)}) %collective-permute-start.7) | collective-permute-done | bytes 262176 | tf_op jit(solution)/shard_map/ppermute | solution.py:448
  61.4 0.1 add.39
  61.4 0.1 collective-permute-start.8
  61.5 4.6 %collective-permute-done.10 = bf16[128,1024]{1,0:T(8,128)(2,1)S(1)} collective-permute-done((bf16[128,1024]{1,0:T(8,128)(2,1)S(1)}, bf16[128,1024]{1,0:T(8,128)(2,1)S(1)}, u32[]{:S(2)}, u32[]{:S(2)}) %collective-permute-start.10) | collective-permute-done | bytes 262176 | tf_op jit(solution)/shard_map/ppermute | solution.py:448
  66.1 0.1 add.41
  66.2 0.1 collective-permute-start.11
  66.2 0.1 add.42
  66.3 3.5 %collective-permute-start.14 = (bf16[128,1024]{1,0:T(8,128)(2,1)S(1)}, bf16[128,1024]{1,0:T(8,128)(2,1)S(1)}, u32[]{:S(2)}, u32[]{:S(2)}) collective-permute-start(bf16[128,1024]{1,0:T(8,128)(2,1)S(1)} %add.42), channel_id=1, source_target_pairs={{1,2},{2,1},{5,6},{6,5},{9,10},{10,9},{13,14},{14,13},{17,18},{18,... | collective-permute-start | bytes 786440 | tf_op jit(solution)/shard_map/ppermute | solution.py:448
  69.8 0.1 add.43
  69.9 1.5 %finish.1 = (bf16[256,512]{1,0:T(8,128)(2,1)}, f32[256,256]{1,0:T(8,128)S(1)}) custom-call(bf16[1280,1024]{1,0:T(8,128)(2,1)S(1)} %get-tuple-element.50.scores, bf16[1024,128]{1,0:T(8,128)(2,1)S(1)} %get-tuple-element.51.ups, bf16[256,512]{1,0:T(8,128)(2,1)S(1)} %get-tuple-element.32.query, bf16[1280,1024]{1,0:T(8,128)(2,1)S(1)} %get-tuple-element.49.probs, ...), custom_call_target="tpu_custom_call" | custom-call | flops 335544320 | bytes 1310720 | tf_op jit(solution)/shard_map/finish/pallas_call | solution.py:420
  71.4 0.0 collective-permute-done.21
  71.4 2.4 %collective-permute-start.17 = (bf16[128,1024]{1,0:T(8,128)(2,1)S(1)}, bf16[128,1024]{1,0:T(8,128)(2,1)S(1)}, u32[]{:S(2)}, u32[]{:S(2)}) collective-permute-start(bf16[128,1024]{1,0:T(8,128)(2,1)S(1)} %add.43), channel_id=1, source_target_pairs={{1,2},{2,1},{5,6},{6,5},{9,10},{10,9},{13,14},{14,13},{17,18},{18,... | collective-permute-start | bytes 786440 | tf_op jit(solution)/shard_map/ppermute | solution.py:448
  73.8 0.0 collective-permute-done.20
  73.8 0.1 add_convert_fusion
  73.9 0.7 fusion
  74.5 0.0 collective-permute-done.8.refs_0_
  74.5 0.0 collective-permute-done.11.refs_1_
  74.5 1.9 %collective-permute-done.14.refs_2_ = bf16[128,1024]{1,0:T(8,128)(2,1)S(1)} collective-permute-done((bf16[128,1024]{1,0:T(8,128)(2,1)S(1)}, bf16[128,1024]{1,0:T(8,128)(2,1)S(1)}, u32[]{:S(2)}, u32[]{:S(2)}) %collective-permute-start.14) | collective-permute-done | bytes 262176 | tf_op jit(solution)/shard_map/ppermute | solution.py:448
  76.5 4.8 %collective-permute-done.17.refs_3_ = bf16[128,1024]{1,0:T(8,128)(2,1)S(1)} collective-permute-done((bf16[128,1024]{1,0:T(8,128)(2,1)S(1)}, bf16[128,1024]{1,0:T(8,128)(2,1)S(1)}, u32[]{:S(2)}, u32[]{:S(2)}) %collective-permute-start.17) | collective-permute-done | bytes 262176 | tf_op jit(solution)/shard_map/ppermute | solution.py:448
  81.3 0.9 %total.1 = bf16[256,1024]{1,0:T(8,128)(2,1)} custom-call(bf16[256,1024]{1,0:T(8,128)(2,1)S(1)} %get-tuple-element.36.own, bf16[128,1024]{1,0:T(8,128)(2,1)S(1)} %collective-permute-done.8.refs_0_, bf16[128,1024]{1,0:T(8,128)(2,1)S(1)} %collective-permute-done.11.refs_1_, bf16[128,1024]{1,0:T(8,128)(2,1)S(1)} %collective-permute-done.14.refs_2_, ...), custom_call_target="tpu_custom_call" | custom-call | flops 786432 | bytes 2097152 | tf_op jit(solution)/shard_map/total/pallas_call | solution.py:243
  (7 shorter events, 0.2 us)
Async XLA Ops:
  0.6 13.9 %collective-permute-start.4 = (bf16[256,1024]{1,0:T(8,128)(2,1)}, bf16[256,1024]{1,0:T(8,128)(2,1)S(1)}, u32[]{:S(2)}, u32[]{:S(2)}) collective-permute-start(bf16[256,1024]{1,0:T(8,128)(2,1)} %own.1), channel_id=1, source_target_pairs={{1,0},{0,1},{3,2},{2,3},{5,4},{4,5},{7,6},{6,7},{9,8},{8,9},{11,10... | collective-permute-start | bytes 1572872 | tf_op jit(solution)/shard_map/ppermute | solution.py:445
  2.2 7.8 %collective-permute-start.2 = (bf16[256,256]{1,0:T(8,128)(2,1)S(1)}, bf16[256,256]{1,0:T(8,128)(2,1)S(1)}, u32[]{:S(2)}, u32[]{:S(2)}) collective-permute-start(bf16[256,256]{1,0:T(8,128)(2,1)S(1)} %get-tuple-element.33.refs_0_.refs_2_), channel_id=1, source_target_pairs={{16,0},{20,4},{24,8},{28,12},{0,16},{4,20},{8,24},{12,28},{17,1},{... | collective-permute-start | bytes 393224 | tf_op jit(solution)/shard_map/ppermute | solution.py:452
  2.4 7.8 %collective-permute-start = (bf16[256,256]{1,0:T(8,128)(2,1)S(1)}, bf16[256,256]{1,0:T(8,128)(2,1)S(1)}, u32[]{:S(2)}, u32[]{:S(2)}) collective-permute-start(bf16[256,256]{1,0:T(8,128)(2,1)S(1)} %get-tuple-element.33.refs_0_.refs_2_), channel_id=1, source_target_pairs={{24,0},{28,4},{0,8},{4,12},{8,16},{12,20},{16,24},{20,28},{25,1},{... | collective-permute-start | bytes 393224 | tf_op jit(solution)/shard_map/ppermute | solution.py:452
  4.3 19.3 %collective-permute-start.5 = (bf16[256,1024]{1,0:T(8,128)(2,1)}, bf16[256,1024]{1,0:T(8,128)(2,1)S(1)}, u32[]{:S(2)}, u32[]{:S(2)}) collective-permute-start(bf16[256,1024]{1,0:T(8,128)(2,1)} %own.1), channel_id=1, source_target_pairs={{1,2},{2,1},{5,6},{6,5},{9,10},{10,9},{13,14},{14,13},{17,18},{18,... | collective-permute-start | bytes 1572872 | tf_op jit(solution)/shard_map/ppermute | solution.py:448
  10.1 10.4 %collective-permute-start.3 = (bf16[256,256]{1,0:T(8,128)(2,1)S(1)}, bf16[256,256]{1,0:T(8,128)(2,1)S(1)}, u32[]{:S(2)}, u32[]{:S(2)}) collective-permute-start(bf16[256,256]{1,0:T(8,128)(2,1)S(1)} %broadcast_select_fusion.2), channel_id=1, source_target_pairs={{4,0},{0,4},{12,8},{8,12},{20,16},{16,20},{28,24},{24,28},{5,1},{1... | collective-permute-start | bytes 393224 | tf_op jit(solution)/shard_map/ppermute | solution.py:455
  10.2 10.3 %collective-permute-start.1 = (bf16[256,256]{1,0:T(8,128)(2,1)S(1)}, bf16[256,256]{1,0:T(8,128)(2,1)S(1)}, u32[]{:S(2)}, u32[]{:S(2)}) collective-permute-start(bf16[256,256]{1,0:T(8,128)(2,1)S(1)} %collective-permute-done.refs_2_.refs_4_), channel_id=1, source_target_pairs={{4,0},{0,4},{12,8},{8,12},{20,16},{16,20},{28,24},{24,28},{5,1},{1... | collective-permute-start | bytes 393224 | tf_op jit(solution)/shard_map/ppermute | solution.py:455
  14.6 13.6 %collective-permute-start.12 = (bf16[128,1024]{1,0:T(8,128)(2,1)S(1)}, bf16[128,1024]{1,0:T(8,128)(2,1)S(1)}, u32[]{:S(2)}, u32[]{:S(2)}) collective-permute-start(bf16[128,1024]{1,0:T(8,128)(2,1)S(1)} %get-tuple-element.45), channel_id=1, source_target_pairs={{1,2},{2,1},{5,6},{6,5},{9,10},{10,9},{13,14},{14,13},{17,18},{18,... | collective-permute-start | bytes 786440 | tf_op jit(solution)/shard_map/ppermute | solution.py:448
  18.1 13.3 %collective-permute-start.15 = (bf16[128,1024]{1,0:T(8,128)(2,1)S(1)}, bf16[128,1024]{1,0:T(8,128)(2,1)S(1)}, u32[]{:S(2)}, u32[]{:S(2)}) collective-permute-start(bf16[128,1024]{1,0:T(8,128)(2,1)S(1)} %get-tuple-element.46), channel_id=1, source_target_pairs={{1,2},{2,1},{5,6},{6,5},{9,10},{10,9},{13,14},{14,13},{17,18},{18,... | collective-permute-start | bytes 786440 | tf_op jit(solution)/shard_map/ppermute | solution.py:448
  23.6 9.2 %collective-permute-start.6 = (bf16[128,1024]{1,0:T(8,128)(2,1)S(1)}, bf16[128,1024]{1,0:T(8,128)(2,1)S(1)}, u32[]{:S(2)}, u32[]{:S(2)}) collective-permute-start(bf16[128,1024]{1,0:T(8,128)(2,1)S(1)} %get-tuple-element.41), channel_id=1, source_target_pairs={{1,0},{0,1},{3,2},{2,3},{5,4},{4,5},{7,6},{6,7},{9,8},{8,9},{11,10... | collective-permute-start | bytes 786440 | tf_op jit(solution)/shard_map/ppermute | solution.py:445
  23.7 14.8 %collective-permute-start.9 = (bf16[128,1024]{1,0:T(8,128)(2,1)S(1)}, bf16[128,1024]{1,0:T(8,128)(2,1)S(1)}, u32[]{:S(2)}, u32[]{:S(2)}) collective-permute-start(bf16[128,1024]{1,0:T(8,128)(2,1)S(1)} %get-tuple-element.44), channel_id=1, source_target_pairs={{1,0},{0,1},{3,2},{2,3},{5,4},{4,5},{7,6},{6,7},{9,8},{8,9},{11,10... | collective-permute-start | bytes 786440 | tf_op jit(solution)/shard_map/ppermute | solution.py:445
  28.3 15.8 %collective-permute-start.13 = (bf16[128,1024]{1,0:T(8,128)(2,1)S(1)}, bf16[128,1024]{1,0:T(8,128)(2,1)S(1)}, u32[]{:S(2)}, u32[]{:S(2)}) collective-permute-start(bf16[128,1024]{1,0:T(8,128)(2,1)S(1)} %shard_map.103), channel_id=1, source_target_pairs={{1,0},{0,1},{3,2},{2,3},{5,4},{4,5},{7,6},{6,7},{9,8},{8,9},{11,10... | collective-permute-start | bytes 786440 | tf_op jit(solution)/shard_map/ppermute | solution.py:445
  31.4 15.8 %collective-permute-start.16 = (bf16[128,1024]{1,0:T(8,128)(2,1)S(1)}, bf16[128,1024]{1,0:T(8,128)(2,1)S(1)}, u32[]{:S(2)}, u32[]{:S(2)}) collective-permute-start(bf16[128,1024]{1,0:T(8,128)(2,1)S(1)} %shard_map.104), channel_id=1, source_target_pairs={{1,0},{0,1},{3,2},{2,3},{5,4},{4,5},{7,6},{6,7},{9,8},{8,9},{11,10... | collective-permute-start | bytes 786440 | tf_op jit(solution)/shard_map/ppermute | solution.py:445
  49.6 6.6 %collective-permute-start.19 = (bf16[256,256]{1,0:T(8,128)(2,1)S(1)}, bf16[256,256]{1,0:T(8,128)(2,1)S(1)}, u32[]{:S(2)}, u32[]{:S(2)}) collective-permute-start(bf16[256,256]{1,0:T(8,128)(2,1)S(1)} %get-tuple-element.56), channel_id=1, source_target_pairs={{4,0},{0,4},{12,8},{8,12},{20,16},{16,20},{28,24},{24,28},{5,1},{1... | collective-permute-start | bytes 393224 | tf_op jit(solution)/shard_map/ppermute | solution.py:455
  49.7 6.5 %collective-permute-start.18 = (bf16[256,256]{1,0:T(8,128)(2,1)S(1)}, bf16[256,256]{1,0:T(8,128)(2,1)S(1)}, u32[]{:S(2)}, u32[]{:S(2)}) collective-permute-start(bf16[256,256]{1,0:T(8,128)(2,1)S(1)} %get-tuple-element.54), channel_id=1, source_target_pairs={{4,0},{0,4},{12,8},{8,12},{20,16},{16,20},{28,24},{24,28},{5,1},{1... | collective-permute-start | bytes 393224 | tf_op jit(solution)/shard_map/ppermute | solution.py:455
  50.3 11.1 %collective-permute-start.7 = (bf16[128,1024]{1,0:T(8,128)(2,1)S(1)}, bf16[128,1024]{1,0:T(8,128)(2,1)S(1)}, u32[]{:S(2)}, u32[]{:S(2)}) collective-permute-start(bf16[128,1024]{1,0:T(8,128)(2,1)S(1)} %add.38), channel_id=1, source_target_pairs={{1,2},{2,1},{5,6},{6,5},{9,10},{10,9},{13,14},{14,13},{17,18},{18,... | collective-permute-start | bytes 786440 | tf_op jit(solution)/shard_map/ppermute | solution.py:448
  53.8 12.3 %collective-permute-start.10 = (bf16[128,1024]{1,0:T(8,128)(2,1)S(1)}, bf16[128,1024]{1,0:T(8,128)(2,1)S(1)}, u32[]{:S(2)}, u32[]{:S(2)}) collective-permute-start(bf16[128,1024]{1,0:T(8,128)(2,1)S(1)} %add.40), channel_id=1, source_target_pairs={{1,2},{2,1},{5,6},{6,5},{9,10},{10,9},{13,14},{14,13},{17,18},{18,... | collective-permute-start | bytes 786440 | tf_op jit(solution)/shard_map/ppermute | solution.py:448
  56.3 15.1 %collective-permute-start.21 = (bf16[256,256]{1,0:T(8,128)(2,1)S(1)}, bf16[256,256]{1,0:T(8,128)(2,1)S(1)}, u32[]{:S(2)}, u32[]{:S(2)}) collective-permute-start(bf16[256,256]{1,0:T(8,128)(2,1)S(1)} %get-tuple-element.63), channel_id=1, source_target_pairs={{16,0},{20,4},{24,8},{28,12},{0,16},{4,20},{8,24},{12,28},{17,1},{... | collective-permute-start | bytes 393224 | tf_op jit(solution)/shard_map/ppermute | solution.py:452
  56.8 17.0 %collective-permute-start.20 = (bf16[256,256]{1,0:T(8,128)(2,1)S(1)}, bf16[256,256]{1,0:T(8,128)(2,1)S(1)}, u32[]{:S(2)}, u32[]{:S(2)}) collective-permute-start(bf16[256,256]{1,0:T(8,128)(2,1)S(1)} %get-tuple-element.62), channel_id=1, source_target_pairs={{8,0},{12,4},{16,8},{20,12},{24,16},{28,20},{0,24},{4,28},{9,1},{1... | collective-permute-start | bytes 393224 | tf_op jit(solution)/shard_map/ppermute | solution.py:452
  61.4 13.1 %collective-permute-start.8 = (bf16[128,1024]{1,0:T(8,128)(2,1)S(1)}, bf16[128,1024]{1,0:T(8,128)(2,1)S(1)}, u32[]{:S(2)}, u32[]{:S(2)}) collective-permute-start(bf16[128,1024]{1,0:T(8,128)(2,1)S(1)} %add.39), channel_id=1, source_target_pairs={{1,0},{0,1},{3,2},{2,3},{5,4},{4,5},{7,6},{6,7},{9,8},{8,9},{11,10... | collective-permute-start | bytes 786440 | tf_op jit(solution)/shard_map/ppermute | solution.py:445
  66.2 8.4 %collective-permute-start.11 = (bf16[128,1024]{1,0:T(8,128)(2,1)S(1)}, bf16[128,1024]{1,0:T(8,128)(2,1)S(1)}, u32[]{:S(2)}, u32[]{:S(2)}) collective-permute-start(bf16[128,1024]{1,0:T(8,128)(2,1)S(1)} %add.41), channel_id=1, source_target_pairs={{1,0},{0,1},{3,2},{2,3},{5,4},{4,5},{7,6},{6,7},{9,8},{8,9},{11,10... | collective-permute-start | bytes 786440 | tf_op jit(solution)/shard_map/ppermute | solution.py:445
  66.3 10.1 %collective-permute-start.14 = (bf16[128,1024]{1,0:T(8,128)(2,1)S(1)}, bf16[128,1024]{1,0:T(8,128)(2,1)S(1)}, u32[]{:S(2)}, u32[]{:S(2)}) collective-permute-start(bf16[128,1024]{1,0:T(8,128)(2,1)S(1)} %add.42), channel_id=1, source_target_pairs={{1,2},{2,1},{5,6},{6,5},{9,10},{10,9},{13,14},{14,13},{17,18},{18,... | collective-permute-start | bytes 786440 | tf_op jit(solution)/shard_map/ppermute | solution.py:448
  71.4 9.9 %collective-permute-start.17 = (bf16[128,1024]{1,0:T(8,128)(2,1)S(1)}, bf16[128,1024]{1,0:T(8,128)(2,1)S(1)}, u32[]{:S(2)}, u32[]{:S(2)}) collective-permute-start(bf16[128,1024]{1,0:T(8,128)(2,1)S(1)} %add.43), channel_id=1, source_target_pairs={{1,2},{2,1},{5,6},{6,5},{9,10},{10,9},{13,14},{14,13},{17,18},{18,... | collective-permute-start | bytes 786440 | tf_op jit(solution)/shard_map/ppermute | solution.py:448

commit v3 on v2

--- a/solution.py
+++ b/solution.py
@@ -207,6 +207,27 @@
     )(*ends, inner)
 
 
+def carry_kernel(share, passed, out):
+    @pl.when(at_end())
+    def _():
+        out[...] = share[...]
+
+    @pl.when(jnp.logical_not(at_end()))
+    def _():
+        out[...] = share[...] + passed[...]
+
+
+def carry(share, passed):
+    return pl.pallas_call(
+        carry_kernel,
+        in_specs=[WHOLE] * 2,
+        out_specs=WHOLE,
+        out_shape=pltpu.VMEM(share.shape, BF16),
+        compiler_params=PARAMS,
+        cost_estimate=estimate(share.size, 6 * share.size),
+    )(share, passed)
+
+
 def split_kernel(whole, *parts):
     in_parts(parts, whole[...])
 
@@ -224,15 +245,21 @@
 
 
 def total_kernel(own, *refs):
-    parts, out, buffer, sems = refs[:-3], refs[-3], refs[-2], refs[-1]
-    rows = parts[0].shape[0]
+    outer, inner, (out, buffer, sems) = refs[:PARTS], refs[PARTS:-3], refs[-3:]
+    rows = outer[0].shape[0]
     copies = []
     for index in range(PARTS):
         spot = pl.ds(index * rows, rows)
-        value = own[spot, :].astype(F32)
-        for part in parts[index::PARTS]:
-            value = value + part[...].astype(F32)
-        buffer[spot, :] = value.astype(BF16)
+        value = own[spot, :].astype(F32) + outer[index][...].astype(F32)
+
+        @pl.when(at_end())
+        def _():
+            buffer[spot, :] = value.astype(BF16)
+
+        @pl.when(jnp.logical_not(at_end()))
+        def _():
+            buffer[spot, :] = (value + inner[index][...].astype(F32)).astype(BF16)
+
         copies.append(pltpu.make_async_copy(buffer.at[spot], out.at[spot], sems.at[index]))
         copies[-1].start()
     for copy in copies:
@@ -441,11 +468,16 @@
     even = lax.axis_index("seq") % 2 == 0
     nothing = jnp.zeros((), BF16)
 
+    across = []
+    for i in range(devices):
+        for first, second in ((1, (i, 2)), (2, (i, 1)), (0, (i ^ 1, 0)), (3, (i ^ 1, 3))):
+            across.append((i * size + first, second[0] * size + second[1]))
+
     def outer(array):
         return lax.ppermute(array, "head", [(i ^ 1, i) for i in range(size)])
 
     def inner(array):
-        return lax.ppermute(array, "head", [(1, 2), (2, 1)])
+        return lax.ppermute(array, ("seq", "head"), across)
 
     def shifted(array, step):
         pairs = [((i - step) % devices, i) for i in range(devices)]
@@ -481,7 +513,7 @@
         partial, outer3, inner1, query, turned, probs, proj, blocks, groups
     )
     inner4 = [inner(lead[i] + outer3[i]) for i in both]
-    outer4 = [outer(pair_share[i] + inner3[i]) for i in both]
+    outer4 = [outer(carry(pair_share[i], inner3[i])) for i in both]
 
     taken = [swapped(sent[2 * step]) for step in range(half)]
     total = []

time: 82.5 us -> 75 us (0.909)
  starting transfers between devices: 31.3 us -> 18.1 us
  waiting for transfers between devices: 36.4 us -> 42.3 us
    ppermute x7, starting transfers between devices: 22.1 us -> 9.04 us  [inner(): return lax.ppermute(array, ('seq', 'head'), across)]
    ppermute x7, waiting for transfers between devices: 16.4 us -> 19.3 us  [inner(): return lax.ppermute(array, ('seq', 'head'), across)]
    ppermute x4, waiting for transfers between devices: 1.15 us -> 3.07 us  [shifted(): return lax.ppermute(array, 'seq', pairs)]
    ppermute x7, waiting for transfers between devices: 18.9 us -> 19.9 us  [outer(): return lax.ppermute(array, 'head', [(i ^ 1, i) for i in range(size)])]
  transfers between devices with their start and end apart: 22 -> 22, of which waited for: 11 -> 13; matrix products, arithmetic and copies ran while one was open for 1% -> 1% of each run, Pallas kernels for 11% -> 12%
where the time goes in v3:
time: 75 us; the launch traced here: 74.8 us
  waiting for transfers between devices  42.3 us (56%)
  starting transfers between devices  18.1 us (24%)
  Pallas kernels  12.4 us (17%)
  between operations  0.82 us (1%)
    ppermute x7, waiting for transfers between devices, outer(): return lax.ppermute(array, 'head', [(i ^ 1, i) for i in range(size)])  19.9 us
    ppermute x7, waiting for transfers between devices, inner(): return lax.ppermute(array, ('seq', 'head'), across)  19.3 us
    ppermute x7, starting transfers between devices, inner(): return lax.ppermute(array, ('seq', 'head'), across)  9.04 us
    ppermute x4, starting transfers between devices, shifted(): return lax.ppermute(array, 'seq', pairs)  5.08 us
    ppermute x4, waiting for transfers between devices, shifted(): return lax.ppermute(array, 'seq', pairs)  3.07 us
    pallas_call x1, Pallas kernels, forward(): pl.pallas_call(functools.partial(forward_kernel, reach=reach, groups=grou...  3.05 us
    ppermute x7, starting transfers between devices, outer(): return lax.ppermute(array, 'head', [(i ^ 1, i) for i in range(size)])  2.88 us
    pallas_call x1, Pallas kernels, middle(): pl.pallas_call(middle_kernel, in_specs=[WHOLE, MAIN, WHOLE, WHOLE], out_s...  2.48 us
  transfers between devices with their start and end apart: 22, of which 13 were waited for; matrix products, arithmetic and copies ran while one was open for 1% of the time, Pallas kernels for 12%

profile of v3, /device:TPU:12, one launch (start us, length us, event | category | flops | bytes accessed | tf_op | source)
XLA Modules:
  0.0 74.8 jit_solution(15104259617438934153)
XLA Ops:
  0.6 0.5 collective-permute-start.4
  1.1 1.1 %stage.1 = (bf16[256,256]{1,0:T(8,128)(2,1)S(1)}, bf16[256,512]{1,0:T(8,128)(2,1)S(1)}, s32[20,256]{1,0:T(8,128)S(1)}) custom-call(bf16[256,128]{1,0:T(8,128)(2,1)} %keys.1, bf16[256,128]{1,0:T(8,128)(2,1)} %values.1, bf16[256,512]{1,0:T(8,128)(2,1)} %queries.1, s32[4]{0:T(128)} %windows.1, s32[8]{0:T(128)} %order.1), custom_call_target="tpu_custom_call" | custom-call | flops 32768 | bytes 262144 | tf_op jit(solution)/shard_map/stage/pallas_call | solution.py:83
  2.2 0.1 collective-permute-start.2
  2.4 1.9 %collective-permute-start = (bf16[256,256]{1,0:T(8,128)(2,1)S(1)}, bf16[256,256]{1,0:T(8,128)(2,1)S(1)}, u32[]{:S(2)}, u32[]{:S(2)}) collective-permute-start(bf16[256,256]{1,0:T(8,128)(2,1)S(1)} %get-tuple-element.33.refs_0_.refs_2_), channel_id=1, source_target_pairs={{24,0},{28,4},{0,8},{4,12},{8,16},{12,20},{16,24},{20,28},{25,1},{... | collective-permute-start | bytes 393224 | tf_op jit(solution)/shard_map/ppermute | solution.py:484
  4.3 2.7 %collective-permute-start.5 = (bf16[256,1024]{1,0:T(8,128)(2,1)}, bf16[256,1024]{1,0:T(8,128)(2,1)S(1)}, u32[]{:S(2)}, u32[]{:S(2)}) collective-permute-start(bf16[256,1024]{1,0:T(8,128)(2,1)} %own.1), channel_id=1, source_target_pairs={{1,2},{2,1},{0,4},{3,7},{5,6},{6,5},{4,0},{7,3},{9,10},{10,9},{8,1... | collective-permute-start | bytes 1572872 | tf_op jit(solution)/shard_map/ppermute | solution.py:480
  7.0 3.1 %collective-permute-done.2.refs_4_.refs_6_ = bf16[256,256]{1,0:T(8,128)(2,1)S(1)} collective-permute-done((bf16[256,256]{1,0:T(8,128)(2,1)S(1)}, bf16[256,256]{1,0:T(8,128)(2,1)S(1)}, u32[]{:S(2)}, u32[]{:S(2)}) %collective-permute-start.2) | collective-permute-done | bytes 131104 | tf_op jit(solution)/shard_map/ppermute | solution.py:484
  10.1 0.1 collective-permute-start.3
  10.2 0.0 collective-permute-done.refs_2_.refs_4_
  10.2 0.5 collective-permute-start.1
  10.7 3.9 %collective-permute-done.4.paired.whole = bf16[256,1024]{1,0:T(8,128)(2,1)S(1)} collective-permute-done((bf16[256,1024]{1,0:T(8,128)(2,1)}, bf16[256,1024]{1,0:T(8,128)(2,1)S(1)}, u32[]{:S(2)}, u32[]{:S(2)}) %collective-permute-start.4) | collective-permute-done | bytes 524320 | tf_op jit(solution)/shard_map/ppermute | solution.py:477
  14.6 1.6 %collective-permute-start.12 = (bf16[128,1024]{1,0:T(8,128)(2,1)S(1)}, bf16[128,1024]{1,0:T(8,128)(2,1)S(1)}, u32[]{:S(2)}, u32[]{:S(2)}) collective-permute-start(bf16[128,1024]{1,0:T(8,128)(2,1)S(1)} %get-tuple-element.45), channel_id=1, source_target_pairs={{1,2},{2,1},{0,4},{3,7},{5,6},{6,5},{4,0},{7,3},{9,10},{10,9},{8,1... | collective-permute-start | bytes 786440 | tf_op jit(solution)/shard_map/ppermute | solution.py:480
  16.3 0.4 collective-permute-start.15
  16.7 0.0 collective-permute-done.3
  16.7 0.0 collective-permute-done.1
  16.7 3.0 %forward.1 = (bf16[256,512]{1,0:T(8,128)(2,1)S(1)}, bf16[512,256]{1,0:T(8,128)(2,1)S(1)}, bf16[1280,1024]{1,0:T(8,128)(2,1)S(1)}, bf16[512,4096]{1,0:T(8,128)(2,...) custom-call(s32[20,256]{1,0:T(8,128)S(1)} %get-tuple-element.31.limits, ...), custom_call_target="tpu_custom_call" | custom-call | flops 671088640 | bytes 2621440 | tf_op jit(solution)/shard_map/forward/pallas_call | solution.py:158
  19.8 0.2 collective-permute-done.5.refs_2_.inner
  20.0 0.1 collective-permute-start.6
  20.1 2.0 %collective-permute-start.9 = (bf16[128,1024]{1,0:T(8,128)(2,1)S(1)}, bf16[128,1024]{1,0:T(8,128)(2,1)S(1)}, u32[]{:S(2)}, u32[]{:S(2)}) collective-permute-start(bf16[128,1024]{1,0:T(8,128)(2,1)S(1)} %get-tuple-element.44), channel_id=1, source_target_pairs={{1,0},{0,1},{3,2},{2,3},{5,4},{4,5},{7,6},{6,7},{9,8},{8,9},{11,10... | collective-permute-start | bytes 786440 | tf_op jit(solution)/shard_map/ppermute | solution.py:477
  22.1 2.5 %middle.1 = (bf16[256,1024]{1,0:T(8,128)(2,1)S(1)}, f32[512,256]{1,0:T(8,128)S(1)}, bf16[128,1024]{1,0:T(8,128)(2,1)S(1)}, bf16[128,1024]{1,0:T(8,128)(2,1)S(1)}...) custom-call(bf16[256,512]{1,0:T(8,128)(2,1)S(1)} %get-tuple-element.34.attention, bf16[256,1024]{1,0:T(8,128)(2,1)} %own.1, ...), custom_call_target="tpu_custom_call" | custom-call | flops 1342177280 | bytes 2097152 | tf_op jit(solution)/shard_map/middle/pallas_call | solution.py:303
  24.6 1.0 %collective-permute-done.12.refs_1_.refs_2_ = bf16[128,1024]{1,0:T(8,128)(2,1)S(1)} collective-permute-done((bf16[128,1024]{1,0:T(8,128)(2,1)S(1)}, bf16[128,1024]{1,0:T(8,128)(2,1)S(1)}, u32[]{:S(2)}, u32[]{:S(2)}) %collective-permute-start.12) | collective-permute-done | bytes 262176 | tf_op jit(solution)/shard_map/ppermute | solution.py:480
  25.6 0.1 collective-permute-start.13
  25.7 3.8 %collective-permute-done.15.refs_1_.refs_3_ = bf16[128,1024]{1,0:T(8,128)(2,1)S(1)} collective-permute-done((bf16[128,1024]{1,0:T(8,128)(2,1)S(1)}, bf16[128,1024]{1,0:T(8,128)(2,1)S(1)}, u32[]{:S(2)}, u32[]{:S(2)}) %collective-permute-start.15) | collective-permute-done | bytes 262176 | tf_op jit(solution)/shard_map/ppermute | solution.py:480
  29.5 0.1 collective-permute-start.16
  29.6 0.0 collective-permute-done.6.refs_0_
  29.6 5.3 %collective-permute-done.9.refs_1_ = bf16[128,1024]{1,0:T(8,128)(2,1)S(1)} collective-permute-done((bf16[128,1024]{1,0:T(8,128)(2,1)S(1)}, bf16[128,1024]{1,0:T(8,128)(2,1)S(1)}, u32[]{:S(2)}, u32[]{:S(2)}) %collective-permute-start.9) | collective-permute-done | bytes 262176 | tf_op jit(solution)/shard_map/ppermute | solution.py:477
  34.9 0.7 far.1.partial
  35.6 4.9 %collective-permute-done.13.refs_0_ = bf16[128,1024]{1,0:T(8,128)(2,1)S(1)} collective-permute-done((bf16[128,1024]{1,0:T(8,128)(2,1)S(1)}, bf16[128,1024]{1,0:T(8,128)(2,1)S(1)}, u32[]{:S(2)}, u32[]{:S(2)}) %collective-permute-start.13) | collective-permute-done | bytes 262176 | tf_op jit(solution)/shard_map/ppermute | solution.py:477
  40.5 2.9 %collective-permute-done.16.refs_1_ = bf16[128,1024]{1,0:T(8,128)(2,1)S(1)} collective-permute-done((bf16[128,1024]{1,0:T(8,128)(2,1)S(1)}, bf16[128,1024]{1,0:T(8,128)(2,1)S(1)}, u32[]{:S(2)}, u32[]{:S(2)}) %collective-permute-start.16) | collective-permute-done | bytes 262176 | tf_op jit(solution)/shard_map/ppermute | solution.py:477
  43.4 2.4 %backward.1 = (bf16[256,256]{1,0:T(8,128)(2,1)S(1)}, bf16[256,256]{1,0:T(8,128)(2,1)S(1)}, bf16[256,256]{1,0:T(8,128)(2,1)S(1)}, bf16[256,256]{1,0:T(8,128)(2,1)...) custom-call(f32[512,256]{1,0:T(8,128)S(1)} %far.1.partial, ...), custom_call_target="tpu_custom_call" | custom-call | flops 1342177280 | bytes 2621440 | tf_op jit(solution)/shard_map/backward/pallas_call | solution.py:404
  45.8 0.1 collective-permute-start.19
  45.9 0.5 collective-permute-start.18
  46.4 0.1 add.32
  46.5 1.6 %collective-permute-start.7 = (bf16[128,1024]{1,0:T(8,128)(2,1)S(1)}, bf16[128,1024]{1,0:T(8,128)(2,1)S(1)}, u32[]{:S(2)}, u32[]{:S(2)}) collective-permute-start(bf16[128,1024]{1,0:T(8,128)(2,1)S(1)} %add.32), channel_id=1, source_target_pairs={{1,2},{2,1},{0,4},{3,7},{5,6},{6,5},{4,0},{7,3},{9,10},{10,9},{8,1... | collective-permute-start | bytes 786440 | tf_op jit(solution)/shard_map/ppermute | solution.py:480
  48.1 0.1 add.33
  48.2 0.5 collective-permute-start.10
  48.7 0.0 collective-permute-done.19
  48.7 0.0 collective-permute-done.18
  48.8 0.6 collective-permute-start.21
  49.3 2.5 %collective-permute-start.20 = (bf16[256,256]{1,0:T(8,128)(2,1)S(1)}, bf16[256,256]{1,0:T(8,128)(2,1)S(1)}, u32[]{:S(2)}, u32[]{:S(2)}) collective-permute-start(bf16[256,256]{1,0:T(8,128)(2,1)S(1)} %get-tuple-element.62), channel_id=1, source_target_pairs={{8,0},{12,4},{16,8},{20,12},{24,16},{28,20},{0,24},{4,28},{9,1},{1... | collective-permute-start | bytes 393224 | tf_op jit(solution)/shard_map/ppermute | solution.py:484
  51.8 4.0 %collective-permute-done.7.passed = bf16[128,1024]{1,0:T(8,128)(2,1)S(1)} collective-permute-done((bf16[128,1024]{1,0:T(8,128)(2,1)S(1)}, bf16[128,1024]{1,0:T(8,128)(2,1)S(1)}, u32[]{:S(2)}, u32[]{:S(2)}) %collective-permute-start.7) | collective-permute-done | bytes 262176 | tf_op jit(solution)/shard_map/ppermute | solution.py:480
  55.8 0.1 collective-permute-start.8
  55.8 4.6 %collective-permute-done.10.passed = bf16[128,1024]{1,0:T(8,128)(2,1)S(1)} collective-permute-done((bf16[128,1024]{1,0:T(8,128)(2,1)S(1)}, bf16[128,1024]{1,0:T(8,128)(2,1)S(1)}, u32[]{:S(2)}, u32[]{:S(2)}) %collective-permute-start.10) | collective-permute-done | bytes 262176 | tf_op jit(solution)/shard_map/ppermute | solution.py:480
  60.5 0.1 collective-permute-start.11
  60.6 0.1 add.34
  60.6 1.6 %collective-permute-start.14 = (bf16[128,1024]{1,0:T(8,128)(2,1)S(1)}, bf16[128,1024]{1,0:T(8,128)(2,1)S(1)}, u32[]{:S(2)}, u32[]{:S(2)}) collective-permute-start(bf16[128,1024]{1,0:T(8,128)(2,1)S(1)} %add.34), channel_id=1, source_target_pairs={{1,2},{2,1},{0,4},{3,7},{5,6},{6,5},{4,0},{7,3},{9,10},{10,9},{8,1... | collective-permute-start | bytes 786440 | tf_op jit(solution)/shard_map/ppermute | solution.py:480
  62.3 0.1 add.35
  62.4 1.5 %finish.1 = (bf16[256,512]{1,0:T(8,128)(2,1)}, f32[256,256]{1,0:T(8,128)S(1)}) custom-call(bf16[1280,1024]{1,0:T(8,128)(2,1)S(1)} %get-tuple-element.50.scores, bf16[1024,128]{1,0:T(8,128)(2,1)S(1)} %get-tuple-element.51.ups, bf16[256,512]{1,0:T(8,128)(2,1)S(1)} %get-tuple-element.32.query, bf16[1280,1024]{1,0:T(8,128)(2,1)S(1)} %get-tuple-element.49.probs, ...), custom_call_target="tpu_custom_call" | custom-call | flops 335544320 | bytes 1310720 | tf_op jit(solution)/shard_map/finish/pallas_call | solution.py:447
  63.9 0.0 collective-permute-done.21
  63.9 0.5 collective-permute-start.17
  64.4 0.0 collective-permute-done.20
  64.4 0.1 add_convert_fusion
  64.4 0.7 fusion
  65.1 0.0 collective-permute-done.8.refs_0_
  65.1 2.9 %collective-permute-done.11.refs_1_ = bf16[128,1024]{1,0:T(8,128)(2,1)S(1)} collective-permute-done((bf16[128,1024]{1,0:T(8,128)(2,1)S(1)}, bf16[128,1024]{1,0:T(8,128)(2,1)S(1)}, u32[]{:S(2)}, u32[]{:S(2)}) %collective-permute-start.11) | collective-permute-done | bytes 262176 | tf_op jit(solution)/shard_map/ppermute | solution.py:477
  68.0 1.9 %collective-permute-done.14.refs_2_ = bf16[128,1024]{1,0:T(8,128)(2,1)S(1)} collective-permute-done((bf16[128,1024]{1,0:T(8,128)(2,1)S(1)}, bf16[128,1024]{1,0:T(8,128)(2,1)S(1)}, u32[]{:S(2)}, u32[]{:S(2)}) %collective-permute-start.14) | collective-permute-done | bytes 262176 | tf_op jit(solution)/shard_map/ppermute | solution.py:480
  69.9 3.9 %collective-permute-done.17.refs_3_ = bf16[128,1024]{1,0:T(8,128)(2,1)S(1)} collective-permute-done((bf16[128,1024]{1,0:T(8,128)(2,1)S(1)}, bf16[128,1024]{1,0:T(8,128)(2,1)S(1)}, u32[]{:S(2)}, u32[]{:S(2)}) %collective-permute-start.17) | collective-permute-done | bytes 262176 | tf_op jit(solution)/shard_map/ppermute | solution.py:480
  73.8 1.0 %total.1 = bf16[256,1024]{1,0:T(8,128)(2,1)} custom-call(bf16[256,1024]{1,0:T(8,128)(2,1)S(1)} %get-tuple-element.36.own, bf16[128,1024]{1,0:T(8,128)(2,1)S(1)} %collective-permute-done.8.refs_0_, bf16[128,1024]{1,0:T(8,128)(2,1)S(1)} %collective-permute-done.11.refs_1_, bf16[128,1024]{1,0:T(8,128)(2,1)S(1)} %collective-permute-done.14.refs_2_, ...), custom_call_target="tpu_custom_call" | custom-call | flops 786432 | bytes 2097152 | tf_op jit(solution)/shard_map/total/pallas_call | solution.py:270
  (9 shorter events, 0.2 us)
Async XLA Ops:
  0.6 13.9 %collective-permute-start.4 = (bf16[256,1024]{1,0:T(8,128)(2,1)}, bf16[256,1024]{1,0:T(8,128)(2,1)S(1)}, u32[]{:S(2)}, u32[]{:S(2)}) collective-permute-start(bf16[256,1024]{1,0:T(8,128)(2,1)} %own.1), channel_id=1, source_target_pairs={{1,0},{0,1},{3,2},{2,3},{5,4},{4,5},{7,6},{6,7},{9,8},{8,9},{11,10... | collective-permute-start | bytes 1572872 | tf_op jit(solution)/shard_map/ppermute | solution.py:477
  2.2 7.8 %collective-permute-start.2 = (bf16[256,256]{1,0:T(8,128)(2,1)S(1)}, bf16[256,256]{1,0:T(8,128)(2,1)S(1)}, u32[]{:S(2)}, u32[]{:S(2)}) collective-permute-start(bf16[256,256]{1,0:T(8,128)(2,1)S(1)} %get-tuple-element.33.refs_0_.refs_2_), channel_id=1, source_target_pairs={{16,0},{20,4},{24,8},{28,12},{0,16},{4,20},{8,24},{12,28},{17,1},{... | collective-permute-start | bytes 393224 | tf_op jit(solution)/shard_map/ppermute | solution.py:484
  2.4 7.8 %collective-permute-start = (bf16[256,256]{1,0:T(8,128)(2,1)S(1)}, bf16[256,256]{1,0:T(8,128)(2,1)S(1)}, u32[]{:S(2)}, u32[]{:S(2)}) collective-permute-start(bf16[256,256]{1,0:T(8,128)(2,1)S(1)} %get-tuple-element.33.refs_0_.refs_2_), channel_id=1, source_target_pairs={{24,0},{28,4},{0,8},{4,12},{8,16},{12,20},{16,24},{20,28},{25,1},{... | collective-permute-start | bytes 393224 | tf_op jit(solution)/shard_map/ppermute | solution.py:484
  4.3 15.7 %collective-permute-start.5 = (bf16[256,1024]{1,0:T(8,128)(2,1)}, bf16[256,1024]{1,0:T(8,128)(2,1)S(1)}, u32[]{:S(2)}, u32[]{:S(2)}) collective-permute-start(bf16[256,1024]{1,0:T(8,128)(2,1)} %own.1), channel_id=1, source_target_pairs={{1,2},{2,1},{0,4},{3,7},{5,6},{6,5},{4,0},{7,3},{9,10},{10,9},{8,1... | collective-permute-start | bytes 1572872 | tf_op jit(solution)/shard_map/ppermute | solution.py:480
  10.1 6.6 %collective-permute-start.3 = (bf16[256,256]{1,0:T(8,128)(2,1)S(1)}, bf16[256,256]{1,0:T(8,128)(2,1)S(1)}, u32[]{:S(2)}, u32[]{:S(2)}) collective-permute-start(bf16[256,256]{1,0:T(8,128)(2,1)S(1)} %broadcast_select_fusion.2), channel_id=1, source_target_pairs={{4,0},{0,4},{12,8},{8,12},{20,16},{16,20},{28,24},{24,28},{5,1},{1... | collective-permute-start | bytes 393224 | tf_op jit(solution)/shard_map/ppermute | solution.py:487
  10.2 6.5 %collective-permute-start.1 = (bf16[256,256]{1,0:T(8,128)(2,1)S(1)}, bf16[256,256]{1,0:T(8,128)(2,1)S(1)}, u32[]{:S(2)}, u32[]{:S(2)}) collective-permute-start(bf16[256,256]{1,0:T(8,128)(2,1)S(1)} %collective-permute-done.refs_2_.refs_4_), channel_id=1, source_target_pairs={{4,0},{0,4},{12,8},{8,12},{20,16},{16,20},{28,24},{24,28},{5,1},{1... | collective-permute-start | bytes 393224 | tf_op jit(solution)/shard_map/ppermute | solution.py:487
  14.6 11.0 %collective-permute-start.12 = (bf16[128,1024]{1,0:T(8,128)(2,1)S(1)}, bf16[128,1024]{1,0:T(8,128)(2,1)S(1)}, u32[]{:S(2)}, u32[]{:S(2)}) collective-permute-start(bf16[128,1024]{1,0:T(8,128)(2,1)S(1)} %get-tuple-element.45), channel_id=1, source_target_pairs={{1,2},{2,1},{0,4},{3,7},{5,6},{6,5},{4,0},{7,3},{9,10},{10,9},{8,1... | collective-permute-start | bytes 786440 | tf_op jit(solution)/shard_map/ppermute | solution.py:480
  16.3 13.3 %collective-permute-start.15 = (bf16[128,1024]{1,0:T(8,128)(2,1)S(1)}, bf16[128,1024]{1,0:T(8,128)(2,1)S(1)}, u32[]{:S(2)}, u32[]{:S(2)}) collective-permute-start(bf16[128,1024]{1,0:T(8,128)(2,1)S(1)} %get-tuple-element.46), channel_id=1, source_target_pairs={{1,2},{2,1},{0,4},{3,7},{5,6},{6,5},{4,0},{7,3},{9,10},{10,9},{8,1... | collective-permute-start | bytes 786440 | tf_op jit(solution)/shard_map/ppermute | solution.py:480
  20.0 9.6 %collective-permute-start.6 = (bf16[128,1024]{1,0:T(8,128)(2,1)S(1)}, bf16[128,1024]{1,0:T(8,128)(2,1)S(1)}, u32[]{:S(2)}, u32[]{:S(2)}) collective-permute-start(bf16[128,1024]{1,0:T(8,128)(2,1)S(1)} %get-tuple-element.41), channel_id=1, source_target_pairs={{1,0},{0,1},{3,2},{2,3},{5,4},{4,5},{7,6},{6,7},{9,8},{8,9},{11,10... | collective-permute-start | bytes 786440 | tf_op jit(solution)/shard_map/ppermute | solution.py:477
  20.1 14.8 %collective-permute-start.9 = (bf16[128,1024]{1,0:T(8,128)(2,1)S(1)}, bf16[128,1024]{1,0:T(8,128)(2,1)S(1)}, u32[]{:S(2)}, u32[]{:S(2)}) collective-permute-start(bf16[128,1024]{1,0:T(8,128)(2,1)S(1)} %get-tuple-element.44), channel_id=1, source_target_pairs={{1,0},{0,1},{3,2},{2,3},{5,4},{4,5},{7,6},{6,7},{9,8},{8,9},{11,10... | collective-permute-start | bytes 786440 | tf_op jit(solution)/shard_map/ppermute | solution.py:477
  25.6 14.9 %collective-permute-start.13 = (bf16[128,1024]{1,0:T(8,128)(2,1)S(1)}, bf16[128,1024]{1,0:T(8,128)(2,1)S(1)}, u32[]{:S(2)}, u32[]{:S(2)}) collective-permute-start(bf16[128,1024]{1,0:T(8,128)(2,1)S(1)} %shard_map.105), channel_id=1, source_target_pairs={{1,0},{0,1},{3,2},{2,3},{5,4},{4,5},{7,6},{6,7},{9,8},{8,9},{11,10... | collective-permute-start | bytes 786440 | tf_op jit(solution)/shard_map/ppermute | solution.py:477
  29.5 13.9 %collective-permute-start.16 = (bf16[128,1024]{1,0:T(8,128)(2,1)S(1)}, bf16[128,1024]{1,0:T(8,128)(2,1)S(1)}, u32[]{:S(2)}, u32[]{:S(2)}) collective-permute-start(bf16[128,1024]{1,0:T(8,128)(2,1)S(1)} %shard_map.106), channel_id=1, source_target_pairs={{1,0},{0,1},{3,2},{2,3},{5,4},{4,5},{7,6},{6,7},{9,8},{8,9},{11,10... | collective-permute-start | bytes 786440 | tf_op jit(solution)/shard_map/ppermute | solution.py:477
  45.8 2.9 %collective-permute-start.19 = (bf16[256,256]{1,0:T(8,128)(2,1)S(1)}, bf16[256,256]{1,0:T(8,128)(2,1)S(1)}, u32[]{:S(2)}, u32[]{:S(2)}) collective-permute-start(bf16[256,256]{1,0:T(8,128)(2,1)S(1)} %get-tuple-element.56), channel_id=1, source_target_pairs={{4,0},{0,4},{12,8},{8,12},{20,16},{16,20},{28,24},{24,28},{5,1},{1... | collective-permute-start | bytes 393224 | tf_op jit(solution)/shard_map/ppermute | solution.py:487
  45.9 2.8 %collective-permute-start.18 = (bf16[256,256]{1,0:T(8,128)(2,1)S(1)}, bf16[256,256]{1,0:T(8,128)(2,1)S(1)}, u32[]{:S(2)}, u32[]{:S(2)}) collective-permute-start(bf16[256,256]{1,0:T(8,128)(2,1)S(1)} %get-tuple-element.54), channel_id=1, source_target_pairs={{4,0},{0,4},{12,8},{8,12},{20,16},{16,20},{28,24},{24,28},{5,1},{1... | collective-permute-start | bytes 393224 | tf_op jit(solution)/shard_map/ppermute | solution.py:487
  46.5 9.2 %collective-permute-start.7 = (bf16[128,1024]{1,0:T(8,128)(2,1)S(1)}, bf16[128,1024]{1,0:T(8,128)(2,1)S(1)}, u32[]{:S(2)}, u32[]{:S(2)}) collective-permute-start(bf16[128,1024]{1,0:T(8,128)(2,1)S(1)} %add.32), channel_id=1, source_target_pairs={{1,2},{2,1},{0,4},{3,7},{5,6},{6,5},{4,0},{7,3},{9,10},{10,9},{8,1... | collective-permute-start | bytes 786440 | tf_op jit(solution)/shard_map/ppermute | solution.py:480
  48.2 12.3 %collective-permute-start.10 = (bf16[128,1024]{1,0:T(8,128)(2,1)S(1)}, bf16[128,1024]{1,0:T(8,128)(2,1)S(1)}, u32[]{:S(2)}, u32[]{:S(2)}) collective-permute-start(bf16[128,1024]{1,0:T(8,128)(2,1)S(1)} %add.33), channel_id=1, source_target_pairs={{1,2},{2,1},{0,4},{3,7},{5,6},{6,5},{4,0},{7,3},{9,10},{10,9},{8,1... | collective-permute-start | bytes 786440 | tf_op jit(solution)/shard_map/ppermute | solution.py:480
  48.8 15.1 %collective-permute-start.21 = (bf16[256,256]{1,0:T(8,128)(2,1)S(1)}, bf16[256,256]{1,0:T(8,128)(2,1)S(1)}, u32[]{:S(2)}, u32[]{:S(2)}) collective-permute-start(bf16[256,256]{1,0:T(8,128)(2,1)S(1)} %get-tuple-element.63), channel_id=1, source_target_pairs={{16,0},{20,4},{24,8},{28,12},{0,16},{4,20},{8,24},{12,28},{17,1},{... | collective-permute-start | bytes 393224 | tf_op jit(solution)/shard_map/ppermute | solution.py:484
  49.3 15.0 %collective-permute-start.20 = (bf16[256,256]{1,0:T(8,128)(2,1)S(1)}, bf16[256,256]{1,0:T(8,128)(2,1)S(1)}, u32[]{:S(2)}, u32[]{:S(2)}) collective-permute-start(bf16[256,256]{1,0:T(8,128)(2,1)S(1)} %get-tuple-element.62), channel_id=1, source_target_pairs={{8,0},{12,4},{16,8},{20,12},{24,16},{28,20},{0,24},{4,28},{9,1},{1... | collective-permute-start | bytes 393224 | tf_op jit(solution)/shard_map/ppermute | solution.py:484
  55.8 9.3 %collective-permute-start.8 = (bf16[128,1024]{1,0:T(8,128)(2,1)S(1)}, bf16[128,1024]{1,0:T(8,128)(2,1)S(1)}, u32[]{:S(2)}, u32[]{:S(2)}) collective-permute-start(bf16[128,1024]{1,0:T(8,128)(2,1)S(1)} %shard_map.103), channel_id=1, source_target_pairs={{1,0},{0,1},{3,2},{2,3},{5,4},{4,5},{7,6},{6,7},{9,8},{8,9},{11,10... | collective-permute-start | bytes 786440 | tf_op jit(solution)/shard_map/ppermute | solution.py:477
  60.5 7.5 %collective-permute-start.11 = (bf16[128,1024]{1,0:T(8,128)(2,1)S(1)}, bf16[128,1024]{1,0:T(8,128)(2,1)S(1)}, u32[]{:S(2)}, u32[]{:S(2)}) collective-permute-start(bf16[128,1024]{1,0:T(8,128)(2,1)S(1)} %shard_map.104), channel_id=1, source_target_pairs={{1,0},{0,1},{3,2},{2,3},{5,4},{4,5},{7,6},{6,7},{9,8},{8,9},{11,10... | collective-permute-start | bytes 786440 | tf_op jit(solution)/shard_map/ppermute | solution.py:477
  60.6 9.2 %collective-permute-start.14 = (bf16[128,1024]{1,0:T(8,128)(2,1)S(1)}, bf16[128,1024]{1,0:T(8,128)(2,1)S(1)}, u32[]{:S(2)}, u32[]{:S(2)}) collective-permute-start(bf16[128,1024]{1,0:T(8,128)(2,1)S(1)} %add.34), channel_id=1, source_target_pairs={{1,2},{2,1},{0,4},{3,7},{5,6},{6,5},{4,0},{7,3},{9,10},{10,9},{8,1... | collective-permute-start | bytes 786440 | tf_op jit(solution)/shard_map/ppermute | solution.py:480
  63.9 9.9 %collective-permute-start.17 = (bf16[128,1024]{1,0:T(8,128)(2,1)S(1)}, bf16[128,1024]{1,0:T(8,128)(2,1)S(1)}, u32[]{:S(2)}, u32[]{:S(2)}) collective-permute-start(bf16[128,1024]{1,0:T(8,128)(2,1)S(1)} %add.35), channel_id=1, source_target_pairs={{1,2},{2,1},{0,4},{3,7},{5,6},{6,5},{4,0},{7,3},{9,10},{10,9},{8,1... | collective-permute-start | bytes 786440 | tf_op jit(solution)/shard_map/ppermute | solution.py:480

commit v4 on v3

--- a/solution.py
+++ b/solution.py
@@ -100,19 +100,39 @@
     )(*[main(array) for array in (key_vectors, values, queries, windows, slab_order)])
 
 
-def forward_kernel(limits, query, proj, *refs, reach, groups):
+def bring_kernel(source, out, sem):
+    copy = pltpu.make_async_copy(source, out, sem)
+    copy.start()
+    copy.wait()
+
+
+def bring(array):
+    return pl.pallas_call(
+        bring_kernel,
+        in_specs=[MAIN],
+        out_specs=WHOLE,
+        out_shape=pltpu.VMEM(array.shape, array.dtype),
+        scratch_shapes=[pltpu.SemaphoreType.DMA],
+        compiler_params=PARAMS,
+        cost_estimate=estimate(array.size, 4 * array.size),
+        name="bring",
+    )(main(array))
+
+
+def forward_kernel(limits, query, proj, *refs, part, reach, groups):
     blocks = refs[: reach + 1]
-    attention, turned, probs, local = refs[reach + 1 : reach + 5]
-    leads, sem = refs[reach + 5 : -1], refs[-1]
-    rows, width = query.shape
+    attention, turned, probs, lead = refs[reach + 1 : reach + 5]
+    keys = blocks[0].shape[0]
+    width = query.shape[1]
+    rows = attention.shape[0]
     heads = width // HEAD_DIM
     size = lax.axis_size("head")
     place = size - 1 - lax.axis_index("head")
-    copy = pltpu.make_async_copy(proj, local, sem)
-    copy.start()
     scale = HEAD_DIM ** (-0.5) * LOG2_E
-    offset = lax.broadcasted_iota(jnp.int32, (rows, rows), 1) - lax.broadcasted_iota(
-        jnp.int32, (rows, rows), 0
+    offset = (
+        lax.broadcasted_iota(jnp.int32, (keys, rows), 1)
+        - lax.broadcasted_iota(jnp.int32, (keys, rows), 0)
+        + part * rows
     )
     turned_values = [
         [head_of(blocks[step], groups + group).T for step in range(reach + 1)]
@@ -121,9 +141,10 @@
 
     def head_scores(head):
         scores = []
+        picked = query[pl.ds(part * rows, rows), pl.ds(head * HEAD_DIM, HEAD_DIM)]
         for step in range(reach + 1):
-            score = dot(head_of(blocks[step], head * groups // heads), head_of(query, head), NT)
-            mask = offset < limits[pl.ds(head * (reach + 1) + step, 1), :]
+            score = dot(head_of(blocks[step], head * groups // heads), picked, NT)
+            mask = offset < limits[pl.ds(head * (reach + 1) + step, 1), pl.ds(0, rows)]
             if step == 0:
                 mask = mask & (offset >= 0)
             scores.append(jnp.where(mask, score, LOWEST))
@@ -140,38 +161,37 @@
         mixed = jnp.zeros((HEAD_DIM, rows), F32)
         for step in range(reach + 1):
             prob = (powers[step] * inverse).astype(BF16)
-            probs[pl.ds(step * rows, rows), pl.ds(head * rows, rows)] = prob
+            probs[pl.ds(step * keys, keys), pl.ds(head * rows, rows)] = prob
             mixed = mixed + dot(turned_values[head * groups // heads][step], prob)
         turned[pl.ds(head * HEAD_DIM, HEAD_DIM), :] = mixed.astype(BF16)
         attention[:, pl.ds(head * HEAD_DIM, HEAD_DIM)] = mixed.T.astype(BF16)
         scores = following
-    copy.wait()
-    in_parts(leads, dot(attention[...], columns_at(local, place, leads[0].shape[1])[...]))
-
-
-def forward(limits, query, out_proj, blocks, groups, size):
+    lead[...] = dot(attention[...], columns_at(proj, place, lead.shape[1])[...]).astype(BF16)
+
+
+def forward(limits, query, proj, blocks, part, groups, size):
     rows, width = query.shape
     heads = width // HEAD_DIM
     reach = len(blocks) - 1
-    share = out_proj.shape[1] // size
     span = (reach + 1) * rows
-    outs = pl.pallas_call(
-        functools.partial(forward_kernel, reach=reach, groups=groups),
-        in_specs=[WHOLE, WHOLE, MAIN] + [WHOLE] * (reach + 1),
-        out_specs=[WHOLE] * (4 + PARTS),
+    rows = rows // PARTS
+    return pl.pallas_call(
+        functools.partial(forward_kernel, part=part, reach=reach, groups=groups),
+        in_specs=[WHOLE] * (reach + 4),
+        out_specs=[WHOLE] * 4,
         out_shape=[
             pltpu.VMEM((rows, width), BF16),
             pltpu.VMEM((width, rows), BF16),
             pltpu.VMEM((span, heads * rows), BF16),
-            pltpu.VMEM(out_proj.shape, BF16),
-        ]
-        + parts_of(rows, share),
-        scratch_shapes=[pltpu.SemaphoreType.DMA],
+            pltpu.VMEM((rows, proj.shape[1] // size), BF16),
+        ],
         compiler_params=PARAMS,
         cost_estimate=estimate(4 * rows * span * width, 8 * rows * span),
-        name="forward",
-    )(limits, query, main(out_proj), *blocks)
-    return outs[:4], outs[4:]
+    )(limits, query, proj, *blocks)
+
+
+def side_by_side(parts, spot, columns):
+    return jnp.concatenate([part[spot, columns] for part in parts], 1)
 
 
 def at_end():
@@ -179,32 +199,25 @@
     return (z == 0) | (z == lax.axis_size("head") - 1)
 
 
-def either_kernel(*refs):
-    count = (len(refs) - 1) // 2
-    ends, inner, outs = refs[:count], refs[count], refs[count + 1 :]
-    rows = outs[0].shape[0]
-    for index, out in enumerate(outs):
-
-        @pl.when(at_end())
-        def _():
-            out[...] = ends[index][...]
-
-        @pl.when(jnp.logical_not(at_end()))
-        def _():
-            out[...] = inner[pl.ds(index * rows, rows), :]
-
-
-def either(ends, inner):
-    rows, width = inner.shape
-    count = len(ends)
-    return pl.pallas_call(
-        either_kernel,
-        in_specs=[WHOLE] * (count + 1),
-        out_specs=[WHOLE] * count,
-        out_shape=[pltpu.VMEM((rows // count, width), BF16)] * count,
-        compiler_params=PARAMS,
-        cost_estimate=estimate(inner.size, 6 * inner.size),
-    )(*ends, inner)
+def either_kernel(ends, inner, out, *, first):
+    @pl.when(at_end())
+    def _():
+        out[...] = ends[...]
+
+    @pl.when(jnp.logical_not(at_end()))
+    def _():
+        out[...] = inner[pl.ds(first, out.shape[0]), :]
+
+
+def either(ends, inner, first):
+    return pl.pallas_call(
+        functools.partial(either_kernel, first=first),
+        in_specs=[WHOLE] * 2,
+        out_specs=WHOLE,
+        out_shape=pltpu.VMEM(ends.shape, BF16),
+        compiler_params=PARAMS,
+        cost_estimate=estimate(ends.size, 6 * ends.size),
+    )(ends, inner)
 
 
 def carry_kernel(share, passed, out):
@@ -279,30 +292,33 @@
     )(own, *parts)
 
 
-def middle_kernel(attention, own, paired, proj, own_share, partial, *refs):
-    far_shares, pair_shares, extra, sem = refs[:PARTS], refs[PARTS:-2], refs[-2], refs[-1]
+def middle_kernel(own, paired, proj, *refs):
+    attention = jnp.concatenate([part[...] for part in refs[:PARTS]], 0)
+    own_share, partial = refs[PARTS : PARTS + 2]
+    far_shares, pair_shares = refs[PARTS + 2 : 2 * PARTS + 2], refs[2 * PARTS + 2 : -2]
+    extra, sem = refs[-2:]
     size = lax.axis_size("head")
     z = lax.axis_index("head")
     share = extra.shape[1]
     copy = pltpu.make_async_copy(own, extra, sem)
     copy.start()
     block = columns_at(proj, lax.rem(z + size // 2, size), share)
-    in_parts(far_shares, dot(attention[...], block[...]))
+    in_parts(far_shares, dot(attention, block[...]))
     block = columns_at(proj, z + 1 - 2 * lax.rem(z, 2), share)
-    in_parts(pair_shares, dot(attention[...], block[...]))
+    in_parts(pair_shares, dot(attention, block[...]))
     total = dot(block[...], paired[...], NT)
     block = columns_at(proj, z, share)
-    own_share[...] = dot(attention[...], block[...]).astype(BF16)
+    own_share[...] = dot(attention, block[...]).astype(BF16)
     copy.wait()
     partial[...] = total + dot(block[...], extra[...], NT)
 
 
 def middle(attention, own, paired, out_proj):
-    rows, width = attention.shape
-    share = own.shape[1]
+    rows, share = own.shape
+    width = attention[0].shape[1]
     outs = pl.pallas_call(
         middle_kernel,
-        in_specs=[WHOLE, MAIN, WHOLE, WHOLE],
+        in_specs=[MAIN, WHOLE, WHOLE] + [WHOLE] * PARTS,
         out_specs=[WHOLE] * (2 + 2 * PARTS),
         out_shape=[pltpu.VMEM(own.shape, BF16), pltpu.VMEM((width, rows), F32)]
         + parts_of(rows, share) * 2,
@@ -310,7 +326,7 @@
         compiler_params=PARAMS,
         cost_estimate=estimate(10 * own.size * width, 8 * own.size),
         name="middle",
-    )(attention, main(own), paired, out_proj)
+    )(main(own), paired, out_proj, *attention)
     return outs[0], outs[1], outs[2 : 2 + PARTS], outs[2 + PARTS :]
 
 
@@ -349,7 +365,17 @@
     )(partial, out_proj, *ends, *inner)
 
 
-def backward_kernel(partial, inner, query, turned, probs, proj, *refs, reach, groups):
+def value_grad(probs, spot, ups, group, ratio, rows):
+    picked = range(group * ratio, (group + 1) * ratio)
+    part = rows // PARTS
+    wide = jnp.concatenate(
+        [side_by_side(probs, spot, pl.ds(head * part, part)) for head in picked], 1
+    )
+    return dot(wide, ups[pl.ds(group * ratio * rows, ratio * rows), :])
+
+
+def backward_kernel(partial, inner, query, proj, *refs, reach, groups):
+    turned, probs, refs = refs[:PARTS], refs[PARTS : 2 * PARTS], refs[2 * PARTS :]
     ends, refs = refs[:PARTS], refs[PARTS:]
     blocks = refs[: reach + 1]
     grads = refs[reach + 1 : 2 * reach + 1]
@@ -372,15 +398,15 @@
     for head in range(heads):
         up = upstream[pl.ds(head * HEAD_DIM, HEAD_DIM), :]
         ups[pl.ds(head * rows, rows), :] = up.T
-        wide = up.astype(F32) * turned[pl.ds(head * HEAD_DIM, HEAD_DIM), :].astype(F32)
+        mixed = side_by_side(turned, pl.ds(head * HEAD_DIM, HEAD_DIM), slice(None))
+        wide = up.astype(F32) * mixed.astype(F32)
         delta = jnp.sum(wide, 0, keepdims=True)
         columns = pl.ds(head * rows, rows)
         for step in range(reach + 1):
             spot = pl.ds(step * rows, rows)
             grad_prob = dot(head_of(blocks[step], groups + head // ratio), up)
-            scores[spot, columns] = (
-                probs[spot, columns].astype(F32) * (grad_prob - delta)
-            ).astype(BF16)
+            prob = side_by_side(probs, spot, pl.ds(head * rows // PARTS, rows // PARTS))
+            scores[spot, columns] = (prob.astype(F32) * (grad_prob - delta)).astype(BF16)
     for group in range(groups):
         tall_query = jnp.concatenate(
             [head_of(query, head) for head in range(group * ratio, (group + 1) * ratio)], 0
@@ -391,8 +417,8 @@
             grads[step - 1][:, pl.ds(group * HEAD_DIM, HEAD_DIM)] = (
                 dot(scores[spot, columns], tall_query) * scale
             ).astype(BF16)
-            grads[step - 1][:, pl.ds((groups + group) * HEAD_DIM, HEAD_DIM)] = dot(
-                probs[spot, columns], ups[columns, :]
+            grads[step - 1][:, pl.ds((groups + group) * HEAD_DIM, HEAD_DIM)] = value_grad(
+                probs, spot, ups, group, ratio, rows
             ).astype(BF16)
 
 
@@ -403,22 +429,23 @@
     span = (reach + 1) * rows
     outs = pl.pallas_call(
         functools.partial(backward_kernel, reach=reach, groups=groups),
-        in_specs=[WHOLE] * (reach + 7 + PARTS),
+        in_specs=[WHOLE] * (reach + 5 + 3 * PARTS),
         out_specs=[WHOLE] * (reach + 2),
         out_shape=[pltpu.VMEM((rows, 2 * groups * HEAD_DIM), BF16)] * reach
         + [
-            pltpu.VMEM(probs.shape, BF16),
+            pltpu.VMEM((span, heads * rows), BF16),
             pltpu.VMEM((heads * rows, HEAD_DIM), BF16),
         ],
         scratch_shapes=[pltpu.VMEM((width, rows), BF16)],
         compiler_params=PARAMS,
         cost_estimate=estimate(8 * rows * span * width, 8 * rows * span),
         name="backward",
-    )(partial, inner, query, turned, probs, out_proj, *ends, *blocks)
+    )(partial, inner, query, out_proj, *turned, *probs, *ends, *blocks)
     return outs[:reach], outs[reach], outs[reach + 1]
 
 
-def finish_kernel(scores, ups, query, probs, *refs, reach, groups):
+def finish_kernel(scores, ups, query, *refs, reach, groups):
+    probs, refs = refs[:PARTS], refs[PARTS:]
     blocks = refs[: reach + 1]
     grad_query, grad = refs[reach + 1 :]
     rows, width = query.shape
@@ -431,8 +458,8 @@
         tall_query = jnp.concatenate([head_of(query, head) for head in picked], 0)
         columns = pl.ds(group * ratio * rows, ratio * rows)
         grad[:, pl.ds(group * HEAD_DIM, HEAD_DIM)] = dot(scores[spot, columns], tall_query) * scale
-        grad[:, pl.ds((groups + group) * HEAD_DIM, HEAD_DIM)] = dot(
-            probs[spot, columns], ups[columns, :]
+        grad[:, pl.ds((groups + group) * HEAD_DIM, HEAD_DIM)] = value_grad(
+            probs, spot, ups, group, ratio, rows
         )
         keys = jnp.concatenate([head_of(blocks[step], group) for step in range(reach + 1)], 0).T
         for head in picked:
@@ -446,7 +473,7 @@
     span = (reach + 1) * rows
     return pl.pallas_call(
         functools.partial(finish_kernel, reach=reach, groups=groups),
-        in_specs=[WHOLE] * (reach + 5),
+        in_specs=[WHOLE] * (reach + 4 + PARTS),
         out_specs=[WHOLE] * 2,
         out_shape=[
             jax.ShapeDtypeStruct((rows, width), BF16),
@@ -455,7 +482,7 @@
         compiler_params=PARAMS,
         cost_estimate=estimate(2 * rows * span * width, 4 * rows * span),
         name="finish",
-    )(scores, ups, query, probs, *blocks)
+    )(scores, ups, query, *probs, *blocks)
 
 
 def body(queries, key_vectors, values, out_proj, grad_out, windows, slab_order):
@@ -497,15 +524,17 @@
 
     both = range(PARTS)
     outer1, inner1 = outer(grad_out), inner(grad_out)
-    (attention, turned, probs, proj), lead = forward(
-        limits, query, out_proj, blocks, groups, size
+    proj = bring(out_proj)
+    attention, turned, probs, lead = zip(
+        *[forward(limits, query, proj, blocks, part, groups, size) for part in both]
     )
     split1 = split(outer1)
     inner2 = [inner(split1[i]) for i in both]
-    send2 = either(lead, inner1)
+    rows = lead[0].shape[0]
+    send2 = [either(lead[i], inner1, i * rows) for i in both]
     outer2 = [outer(send2[i]) for i in both]
     own_share, partial, far_share, pair_share = middle(attention, grad_out, outer1, proj)
-    send3 = [either([far_share[i]], inner2[i])[0] for i in both]
+    send3 = [either(far_share[i], inner2[i], 0) for i in both]
     outer3 = [outer(send3[i]) for i in both]
     inner3 = [inner(far_share[i] + outer2[i]) for i in both]
     partial = far(partial, outer2, inner2, proj)

time: 75 us -> 76.6 us (1.021)
  the two profiles are of different devices: /device:TPU:12 before, /device:TPU:16 now
where the time goes in v4:
time: 76.6 us; the launch traced here: 76.3 us
  waiting for transfers between devices  42.2 us (55%)
  starting transfers between devices  17.1 us (22%)
  Pallas kernels  15.2 us (20%)
  between operations  0.84 us (1%)
    ppermute x7, waiting for transfers between devices, inner(): return lax.ppermute(array, ('seq', 'head'), across)  20.5 us
    ppermute x7, waiting for transfers between devices, outer(): return lax.ppermute(array, 'head', [(i ^ 1, i) for i in range(size)])  16.9 us
    ppermute x7, starting transfers between devices, inner(): return lax.ppermute(array, ('seq', 'head'), across)  6.34 us
    ppermute x4, starting transfers between devices, shifted(): return lax.ppermute(array, 'seq', pairs)  5.54 us
    ppermute x4, waiting for transfers between devices, shifted(): return lax.ppermute(array, 'seq', pairs)  4.77 us
    ppermute x7, starting transfers between devices, outer(): return lax.ppermute(array, 'head', [(i ^ 1, i) for i in range(size)])  4.06 us
    pallas_call x2, Pallas kernels, forward(): pl.pallas_call(functools.partial(forward_kernel, part=part, reach=reach,...  4.03 us
    pallas_call x1, Pallas kernels, backward(): pl.pallas_call(functools.partial(backward_kernel, reach=reach, groups=gro...  2.46 us
  transfers between devices with their start and end apart: 22, of which 13 were waited for; matrix products, arithmetic and copies ran while one was open for 1% of the time, Pallas kernels for 15%

profile of v4, /device:TPU:16, one launch (start us, length us, event | category | flops | bytes accessed | tf_op | source)
XLA Modules:
  0.0 76.3 jit_solution(2714961497082582297)
XLA Ops:
  0.6 1.6 %collective-permute-start = (bf16[256,1024]{1,0:T(8,128)(2,1)}, bf16[256,1024]{1,0:T(8,128)(2,1)S(1)}, u32[]{:S(2)}, u32[]{:S(2)}) collective-permute-start(bf16[256,1024]{1,0:T(8,128)(2,1)} %own.1), channel_id=1, source_target_pairs={{1,0},{0,1},{3,2},{2,3},{5,4},{4,5},{7,6},{6,7},{9,8},{8,9},{11,10... | collective-permute-start | bytes 1572872 | tf_op jit(solution)/shard_map/ppermute | solution.py:504
  2.3 1.1 %stage.1 = (bf16[256,256]{1,0:T(8,128)(2,1)S(1)}, bf16[256,512]{1,0:T(8,128)(2,1)S(1)}, s32[20,256]{1,0:T(8,128)S(1)}) custom-call(bf16[256,128]{1,0:T(8,128)(2,1)} %keys.1, bf16[256,128]{1,0:T(8,128)(2,1)} %values.1, bf16[256,512]{1,0:T(8,128)(2,1)} %queries.1, s32[4]{0:T(128)} %windows.1, s32[8]{0:T(128)} %order.1), custom_call_target="tpu_custom_call" | custom-call | flops 32768 | bytes 262144 | tf_op jit(solution)/shard_map/stage/pallas_call | solution.py:83
  3.4 1.6 %collective-permute-start.3 = (bf16[256,256]{1,0:T(8,128)(2,1)S(1)}, bf16[256,256]{1,0:T(8,128)(2,1)S(1)}, u32[]{:S(2)}, u32[]{:S(2)}) collective-permute-start(bf16[256,256]{1,0:T(8,128)(2,1)S(1)} %get-tuple-element.33.refs_0_.refs_6_.refs_2_), channel_id=1, source_target_pairs={{16,0},{20,4},{24,8},{28,12},{0,16},{4,20},{8,24},{12,28},{17,1},{... | collective-permute-start | bytes 393224 | tf_op jit(solution)/shard_map/ppermute | solution.py:511
  4.9 1.5 %collective-permute-start.1 = (bf16[256,256]{1,0:T(8,128)(2,1)S(1)}, bf16[256,256]{1,0:T(8,128)(2,1)S(1)}, u32[]{:S(2)}, u32[]{:S(2)}) collective-permute-start(bf16[256,256]{1,0:T(8,128)(2,1)S(1)} %get-tuple-element.33.refs_0_.refs_6_.refs_2_), channel_id=1, source_target_pairs={{24,0},{28,4},{0,8},{4,12},{8,16},{12,20},{16,24},{20,28},{25,1},{... | collective-permute-start | bytes 393224 | tf_op jit(solution)/shard_map/ppermute | solution.py:511
  6.4 0.0 collective-permute-start.5
  6.4 4.8 %collective-permute-done.3.refs_4_.refs_10_.refs_6_ = bf16[256,256]{1,0:T(8,128)(2,1)S(1)} collective-permute-done((bf16[256,256]{1,0:T(8,128)(2,1)S(1)}, bf16[256,256]{1,0:T(8,128)(2,1)S(1)}, u32[]{:S(2)}, u32[]{:S(2)}) %collective-permute-start.3) | collective-permute-done | bytes 131104 | tf_op jit(solution)/shard_map/ppermute | solution.py:511
  11.2 0.1 collective-permute-start.4
  11.3 0.0 collective-permute-done.1.refs_2_.refs_8_.refs_4_
  11.3 0.5 collective-permute-start.2
  11.8 2.2 %bring.1.proj = bf16[512,4096]{1,0:T(8,128)(2,1)S(1)} custom-call(bf16[512,4096]{1,0:T(8,128)(2,1)} %source.1), custom_call_target="tpu_custom_call" | custom-call | flops 2097152 | bytes 8388608 | tf_op jit(solution)/shard_map/bring/pallas_call | solution.py:110
  14.0 0.6 collective-permute-done.paired.whole
  14.6 0.5 collective-permute-start.12
  15.1 1.6 %collective-permute-start.15 = (bf16[128,1024]{1,0:T(8,128)(2,1)S(1)}, bf16[128,1024]{1,0:T(8,128)(2,1)S(1)}, u32[]{:S(2)}, u32[]{:S(2)}) collective-permute-start(bf16[128,1024]{1,0:T(8,128)(2,1)S(1)} %get-tuple-element.44), channel_id=1, source_target_pairs={{1,2},{2,1},{0,4},{3,7},{5,6},{6,5},{4,0},{7,3},{9,10},{10,9},{8,1... | collective-permute-start | bytes 786440 | tf_op jit(solution)/shard_map/ppermute | solution.py:507
  16.7 0.0 collective-permute-done.4
  16.7 0.0 collective-permute-done.2
  16.7 1.9 %shard_map.102 = (bf16[128,512]{1,0:T(8,128)(2,1)S(1)}, bf16[512,128]{1,0:T(8,128)(2,1)S(1)}, bf16[1280,512]{1,0:T(8,128)(2,1)S(1)}, bf16[128,1024]{1,0:T(8,128)(2,1)S(1)}) custom-call(s32[20,256]{1,0:T(8,128)S(1)} %get-tuple-element.31.limits, bf16[256,512]{1,0:T(8,128)(2,1)S(1)} %get-tuple-element.32.query, bf16[512,4096]{1,0:T(8,128)(2,1)S(1)} %bring.1.proj, ...), custom_call_target="tpu_custom_call" | custom-call | flops 335544320 | bytes 1310720 | tf_op jit(solution)/shard_map/pallas_call | solution.py:178
  18.7 2.1 %shard_map.103 = (bf16[128,512]{1,0:T(8,128)(2,1)S(1)}, bf16[512,128]{1,0:T(8,128)(2,1)S(1)}, bf16[1280,512]{1,0:T(8,128)(2,1)S(1)}, bf16[128,1024]{1,0:T(8,128)(2,1)S(1)}) custom-call(s32[20,256]{1,0:T(8,128)S(1)} %get-tuple-element.31.limits, bf16[256,512]{1,0:T(8,128)(2,1)S(1)} %get-tuple-element.32.query, bf16[512,4096]{1,0:T(8,128)(2,1)S(1)} %bring.1.proj, ...), custom_call_target="tpu_custom_call" | custom-call | flops 335544320 | bytes 1310720 | tf_op jit(solution)/shard_map/pallas_call | solution.py:178
  20.8 0.7 collective-permute-done.5.inner
  21.5 0.1 collective-permute-start.6
  21.6 2.1 %collective-permute-start.9 = (bf16[128,1024]{1,0:T(8,128)(2,1)S(1)}, bf16[128,1024]{1,0:T(8,128)(2,1)S(1)}, u32[]{:S(2)}, u32[]{:S(2)}) collective-permute-start(bf16[128,1024]{1,0:T(8,128)(2,1)S(1)} %shard_map.106), channel_id=1, source_target_pairs={{1,0},{0,1},{3,2},{2,3},{5,4},{4,5},{7,6},{6,7},{9,8},{8,9},{11,10... | collective-permute-start | bytes 786440 | tf_op jit(solution)/shard_map/ppermute | solution.py:504
  23.6 2.0 %middle.1 = (bf16[256,1024]{1,0:T(8,128)(2,1)S(1)}, f32[512,256]{1,0:T(8,128)S(1)}, bf16[128,1024]{1,0:T(8,128)(2,1)S(1)}, bf16[128,1024]{1,0:T(8,128)(2,1)S(1)}...) custom-call(bf16[256,1024]{1,0:T(8,128)(2,1)} %own.1, ...), custom_call_target="tpu_custom_call" | custom-call | flops 1342177280 | bytes 2097152 | tf_op jit(solution)/shard_map/middle/pallas_call | solution.py:319
  25.7 1.4 %collective-permute-done.12.inner.refs_2_ = bf16[128,1024]{1,0:T(8,128)(2,1)S(1)} collective-permute-done((bf16[128,1024]{1,0:T(8,128)(2,1)S(1)}, bf16[128,1024]{1,0:T(8,128)(2,1)S(1)}, u32[]{:S(2)}, u32[]{:S(2)}) %collective-permute-start.12) | collective-permute-done | bytes 262176 | tf_op jit(solution)/shard_map/ppermute | solution.py:507
  27.1 0.1 collective-permute-start.13
  27.2 3.5 %collective-permute-done.15.inner.refs_3_ = bf16[128,1024]{1,0:T(8,128)(2,1)S(1)} collective-permute-done((bf16[128,1024]{1,0:T(8,128)(2,1)S(1)}, bf16[128,1024]{1,0:T(8,128)(2,1)S(1)}, u32[]{:S(2)}, u32[]{:S(2)}) %collective-permute-start.15) | collective-permute-done | bytes 262176 | tf_op jit(solution)/shard_map/ppermute | solution.py:507
  30.7 0.1 collective-permute-start.16
  30.8 0.0 collective-permute-done.6.refs_0_
  30.8 5.5 %collective-permute-done.9.refs_1_ = bf16[128,1024]{1,0:T(8,128)(2,1)S(1)} collective-permute-done((bf16[128,1024]{1,0:T(8,128)(2,1)S(1)}, bf16[128,1024]{1,0:T(8,128)(2,1)S(1)}, u32[]{:S(2)}, u32[]{:S(2)}) %collective-permute-start.9) | collective-permute-done | bytes 262176 | tf_op jit(solution)/shard_map/ppermute | solution.py:504
  36.3 0.7 far.1.partial
  37.0 4.9 %collective-permute-done.13.refs_4_ = bf16[128,1024]{1,0:T(8,128)(2,1)S(1)} collective-permute-done((bf16[128,1024]{1,0:T(8,128)(2,1)S(1)}, bf16[128,1024]{1,0:T(8,128)(2,1)S(1)}, u32[]{:S(2)}, u32[]{:S(2)}) %collective-permute-start.13) | collective-permute-done | bytes 262176 | tf_op jit(solution)/shard_map/ppermute | solution.py:504
  41.9 3.0 %collective-permute-done.16.refs_5_ = bf16[128,1024]{1,0:T(8,128)(2,1)S(1)} collective-permute-done((bf16[128,1024]{1,0:T(8,128)(2,1)S(1)}, bf16[128,1024]{1,0:T(8,128)(2,1)S(1)}, u32[]{:S(2)}, u32[]{:S(2)}) %collective-permute-start.16) | collective-permute-done | bytes 262176 | tf_op jit(solution)/shard_map/ppermute | solution.py:504
  44.9 2.5 %backward.1 = (bf16[256,256]{1,0:T(8,128)(2,1)S(1)}, bf16[256,256]{1,0:T(8,128)(2,1)S(1)}, bf16[256,256]{1,0:T(8,128)(2,1)S(1)}, bf16[256,256]{1,0:T(8,128)(2,1)...) custom-call(f32[512,256]{1,0:T(8,128)S(1)} %far.1.partial, ...), custom_call_target="tpu_custom_call" | custom-call | flops 1342177280 | bytes 2621440 | tf_op jit(solution)/shard_map/backward/pallas_call | solution.py:430
  47.4 0.1 collective-permute-start.19
  47.5 0.5 collective-permute-start.18
  48.0 0.1 add.32
  48.1 0.4 collective-permute-start.7
  48.5 0.1 add.33
  48.5 1.7 %collective-permute-start.10 = (bf16[128,1024]{1,0:T(8,128)(2,1)S(1)}, bf16[128,1024]{1,0:T(8,128)(2,1)S(1)}, u32[]{:S(2)}, u32[]{:S(2)}) collective-permute-start(bf16[128,1024]{1,0:T(8,128)(2,1)S(1)} %add.33), channel_id=1, source_target_pairs={{1,2},{2,1},{0,4},{3,7},{5,6},{6,5},{4,0},{7,3},{9,10},{10,9},{8,1... | collective-permute-start | bytes 786440 | tf_op jit(solution)/shard_map/ppermute | solution.py:507
  50.3 0.0 collective-permute-done.19
  50.3 0.0 collective-permute-done.18
  50.3 1.6 %collective-permute-start.21 = (bf16[256,256]{1,0:T(8,128)(2,1)S(1)}, bf16[256,256]{1,0:T(8,128)(2,1)S(1)}, u32[]{:S(2)}, u32[]{:S(2)}) collective-permute-start(bf16[256,256]{1,0:T(8,128)(2,1)S(1)} %get-tuple-element.63), channel_id=1, source_target_pairs={{16,0},{20,4},{24,8},{28,12},{0,16},{4,20},{8,24},{12,28},{17,1},{... | collective-permute-start | bytes 393224 | tf_op jit(solution)/shard_map/ppermute | solution.py:511
  51.9 0.9 %collective-permute-start.20 = (bf16[256,256]{1,0:T(8,128)(2,1)S(1)}, bf16[256,256]{1,0:T(8,128)(2,1)S(1)}, u32[]{:S(2)}, u32[]{:S(2)}) collective-permute-start(bf16[256,256]{1,0:T(8,128)(2,1)S(1)} %get-tuple-element.62), channel_id=1, source_target_pairs={{8,0},{12,4},{16,8},{20,12},{24,16},{28,20},{0,24},{4,28},{9,1},{1... | collective-permute-start | bytes 393224 | tf_op jit(solution)/shard_map/ppermute | solution.py:511
  52.8 4.5 %collective-permute-done.7.passed = bf16[128,1024]{1,0:T(8,128)(2,1)S(1)} collective-permute-done((bf16[128,1024]{1,0:T(8,128)(2,1)S(1)}, bf16[128,1024]{1,0:T(8,128)(2,1)S(1)}, u32[]{:S(2)}, u32[]{:S(2)}) %collective-permute-start.7) | collective-permute-done | bytes 262176 | tf_op jit(solution)/shard_map/ppermute | solution.py:507
  57.3 0.1 collective-permute-start.8
  57.4 4.6 %collective-permute-done.10.passed = bf16[128,1024]{1,0:T(8,128)(2,1)S(1)} collective-permute-done((bf16[128,1024]{1,0:T(8,128)(2,1)S(1)}, bf16[128,1024]{1,0:T(8,128)(2,1)S(1)}, u32[]{:S(2)}, u32[]{:S(2)}) %collective-permute-start.10) | collective-permute-done | bytes 262176 | tf_op jit(solution)/shard_map/ppermute | solution.py:507
  62.1 0.1 collective-permute-start.11
  62.1 0.1 add.34
  62.2 0.4 collective-permute-start.14
  62.6 0.1 add.35
  62.7 1.5 %finish.1 = (bf16[256,512]{1,0:T(8,128)(2,1)}, f32[256,256]{1,0:T(8,128)S(1)}) custom-call(bf16[1280,1024]{1,0:T(8,128)(2,1)S(1)} %get-tuple-element.50.scores, bf16[1024,128]{1,0:T(8,128)(2,1)S(1)} %get-tuple-element.51.ups, bf16[256,512]{1,0:T(8,128)(2,1)S(1)} %get-tuple-element.32.query, bf16[1280,512]{1,0:T(8,128)(2,1)S(1)} %get-tuple-element.48.refs_2_.refs_0_, ...), custom_call_target="tpu_custom_call" | custom-call | flops 335544320 | bytes 1310720 | tf_op jit(solution)/shard_map/finish/pallas_call | solution.py:474
  64.2 0.0 collective-permute-done.21
  64.3 1.7 %collective-permute-start.17 = (bf16[128,1024]{1,0:T(8,128)(2,1)S(1)}, bf16[128,1024]{1,0:T(8,128)(2,1)S(1)}, u32[]{:S(2)}, u32[]{:S(2)}) collective-permute-start(bf16[128,1024]{1,0:T(8,128)(2,1)S(1)} %add.35), channel_id=1, source_target_pairs={{1,2},{2,1},{0,4},{3,7},{5,6},{6,5},{4,0},{7,3},{9,10},{10,9},{8,1... | collective-permute-start | bytes 786440 | tf_op jit(solution)/shard_map/ppermute | solution.py:507
  65.9 0.0 collective-permute-done.20
  65.9 0.1 add_convert_fusion
  66.0 0.7 fusion
  66.7 0.0 collective-permute-done.8.refs_0_
  66.7 2.9 %collective-permute-done.11.refs_1_ = bf16[128,1024]{1,0:T(8,128)(2,1)S(1)} collective-permute-done((bf16[128,1024]{1,0:T(8,128)(2,1)S(1)}, bf16[128,1024]{1,0:T(8,128)(2,1)S(1)}, u32[]{:S(2)}, u32[]{:S(2)}) %collective-permute-start.11) | collective-permute-done | bytes 262176 | tf_op jit(solution)/shard_map/ppermute | solution.py:504
  69.6 1.9 %collective-permute-done.14.refs_2_ = bf16[128,1024]{1,0:T(8,128)(2,1)S(1)} collective-permute-done((bf16[128,1024]{1,0:T(8,128)(2,1)S(1)}, bf16[128,1024]{1,0:T(8,128)(2,1)S(1)}, u32[]{:S(2)}, u32[]{:S(2)}) %collective-permute-start.14) | collective-permute-done | bytes 262176 | tf_op jit(solution)/shard_map/ppermute | solution.py:507
  71.5 3.9 %collective-permute-done.17.refs_3_ = bf16[128,1024]{1,0:T(8,128)(2,1)S(1)} collective-permute-done((bf16[128,1024]{1,0:T(8,128)(2,1)S(1)}, bf16[128,1024]{1,0:T(8,128)(2,1)S(1)}, u32[]{:S(2)}, u32[]{:S(2)}) %collective-permute-start.17) | collective-permute-done | bytes 262176 | tf_op jit(solution)/shard_map/ppermute | solution.py:507
  75.3 1.0 %total.1 = bf16[256,1024]{1,0:T(8,128)(2,1)} custom-call(bf16[256,1024]{1,0:T(8,128)(2,1)S(1)} %get-tuple-element.36.own, bf16[128,1024]{1,0:T(8,128)(2,1)S(1)} %collective-permute-done.8.refs_0_, bf16[128,1024]{1,0:T(8,128)(2,1)S(1)} %collective-permute-done.11.refs_1_, bf16[128,1024]{1,0:T(8,128)(2,1)S(1)} %collective-permute-done.14.refs_2_, ...), custom_call_target="tpu_custom_call" | custom-call | flops 786432 | bytes 2097152 | tf_op jit(solution)/shard_map/total/pallas_call | solution.py:283
  (10 shorter events, 0.2 us)
Async XLA Ops:
  0.6 13.9 %collective-permute-start = (bf16[256,1024]{1,0:T(8,128)(2,1)}, bf16[256,1024]{1,0:T(8,128)(2,1)S(1)}, u32[]{:S(2)}, u32[]{:S(2)}) collective-permute-start(bf16[256,1024]{1,0:T(8,128)(2,1)} %own.1), channel_id=1, source_target_pairs={{1,0},{0,1},{3,2},{2,3},{5,4},{4,5},{7,6},{6,7},{9,8},{8,9},{11,10... | collective-permute-start | bytes 1572872 | tf_op jit(solution)/shard_map/ppermute | solution.py:504
  3.4 7.8 %collective-permute-start.3 = (bf16[256,256]{1,0:T(8,128)(2,1)S(1)}, bf16[256,256]{1,0:T(8,128)(2,1)S(1)}, u32[]{:S(2)}, u32[]{:S(2)}) collective-permute-start(bf16[256,256]{1,0:T(8,128)(2,1)S(1)} %get-tuple-element.33.refs_0_.refs_6_.refs_2_), channel_id=1, source_target_pairs={{16,0},{20,4},{24,8},{28,12},{0,16},{4,20},{8,24},{12,28},{17,1},{... | collective-permute-start | bytes 393224 | tf_op jit(solution)/shard_map/ppermute | solution.py:511
  4.9 6.4 %collective-permute-start.1 = (bf16[256,256]{1,0:T(8,128)(2,1)S(1)}, bf16[256,256]{1,0:T(8,128)(2,1)S(1)}, u32[]{:S(2)}, u32[]{:S(2)}) collective-permute-start(bf16[256,256]{1,0:T(8,128)(2,1)S(1)} %get-tuple-element.33.refs_0_.refs_6_.refs_2_), channel_id=1, source_target_pairs={{24,0},{28,4},{0,8},{4,12},{8,16},{12,20},{16,24},{20,28},{25,1},{... | collective-permute-start | bytes 393224 | tf_op jit(solution)/shard_map/ppermute | solution.py:511
  6.4 15.0 %collective-permute-start.5 = (bf16[256,1024]{1,0:T(8,128)(2,1)}, bf16[256,1024]{1,0:T(8,128)(2,1)S(1)}, u32[]{:S(2)}, u32[]{:S(2)}) collective-permute-start(bf16[256,1024]{1,0:T(8,128)(2,1)} %own.1), channel_id=1, source_target_pairs={{1,2},{2,1},{0,4},{3,7},{5,6},{6,5},{4,0},{7,3},{9,10},{10,9},{8,1... | collective-permute-start | bytes 1572872 | tf_op jit(solution)/shard_map/ppermute | solution.py:507
  11.2 5.5 %collective-permute-start.4 = (bf16[256,256]{1,0:T(8,128)(2,1)S(1)}, bf16[256,256]{1,0:T(8,128)(2,1)S(1)}, u32[]{:S(2)}, u32[]{:S(2)}) collective-permute-start(bf16[256,256]{1,0:T(8,128)(2,1)S(1)} %broadcast_select_fusion.2), channel_id=1, source_target_pairs={{4,0},{0,4},{12,8},{8,12},{20,16},{16,20},{28,24},{24,28},{5,1},{1... | collective-permute-start | bytes 393224 | tf_op jit(solution)/shard_map/ppermute | solution.py:514
  11.3 5.4 %collective-permute-start.2 = (bf16[256,256]{1,0:T(8,128)(2,1)S(1)}, bf16[256,256]{1,0:T(8,128)(2,1)S(1)}, u32[]{:S(2)}, u32[]{:S(2)}) collective-permute-start(bf16[256,256]{1,0:T(8,128)(2,1)S(1)} %collective-permute-done.1.refs_2_.refs_8_.refs_4_), channel_id=1, source_target_pairs={{4,0},{0,4},{12,8},{8,12},{20,16},{16,20},{28,24},{24,28},{5,1},{1... | collective-permute-start | bytes 393224 | tf_op jit(solution)/shard_map/ppermute | solution.py:514
  14.6 12.4 %collective-permute-start.12 = (bf16[128,1024]{1,0:T(8,128)(2,1)S(1)}, bf16[128,1024]{1,0:T(8,128)(2,1)S(1)}, u32[]{:S(2)}, u32[]{:S(2)}) collective-permute-start(bf16[128,1024]{1,0:T(8,128)(2,1)S(1)} %get-tuple-element.43), channel_id=1, source_target_pairs={{1,2},{2,1},{0,4},{3,7},{5,6},{6,5},{4,0},{7,3},{9,10},{10,9},{8,1... | collective-permute-start | bytes 786440 | tf_op jit(solution)/shard_map/ppermute | solution.py:507
  15.1 15.6 %collective-permute-start.15 = (bf16[128,1024]{1,0:T(8,128)(2,1)S(1)}, bf16[128,1024]{1,0:T(8,128)(2,1)S(1)}, u32[]{:S(2)}, u32[]{:S(2)}) collective-permute-start(bf16[128,1024]{1,0:T(8,128)(2,1)S(1)} %get-tuple-element.44), channel_id=1, source_target_pairs={{1,2},{2,1},{0,4},{3,7},{5,6},{6,5},{4,0},{7,3},{9,10},{10,9},{8,1... | collective-permute-start | bytes 786440 | tf_op jit(solution)/shard_map/ppermute | solution.py:507
  21.5 9.3 %collective-permute-start.6 = (bf16[128,1024]{1,0:T(8,128)(2,1)S(1)}, bf16[128,1024]{1,0:T(8,128)(2,1)S(1)}, u32[]{:S(2)}, u32[]{:S(2)}) collective-permute-start(bf16[128,1024]{1,0:T(8,128)(2,1)S(1)} %shard_map.104), channel_id=1, source_target_pairs={{1,0},{0,1},{3,2},{2,3},{5,4},{4,5},{7,6},{6,7},{9,8},{8,9},{11,10... | collective-permute-start | bytes 786440 | tf_op jit(solution)/shard_map/ppermute | solution.py:504
  21.6 14.7 %collective-permute-start.9 = (bf16[128,1024]{1,0:T(8,128)(2,1)S(1)}, bf16[128,1024]{1,0:T(8,128)(2,1)S(1)}, u32[]{:S(2)}, u32[]{:S(2)}) collective-permute-start(bf16[128,1024]{1,0:T(8,128)(2,1)S(1)} %shard_map.106), channel_id=1, source_target_pairs={{1,0},{0,1},{3,2},{2,3},{5,4},{4,5},{7,6},{6,7},{9,8},{8,9},{11,10... | collective-permute-start | bytes 786440 | tf_op jit(solution)/shard_map/ppermute | solution.py:504
  27.1 14.9 %collective-permute-start.13 = (bf16[128,1024]{1,0:T(8,128)(2,1)S(1)}, bf16[128,1024]{1,0:T(8,128)(2,1)S(1)}, u32[]{:S(2)}, u32[]{:S(2)}) collective-permute-start(bf16[128,1024]{1,0:T(8,128)(2,1)S(1)} %shard_map.108), channel_id=1, source_target_pairs={{1,0},{0,1},{3,2},{2,3},{5,4},{4,5},{7,6},{6,7},{9,8},{8,9},{11,10... | collective-permute-start | bytes 786440 | tf_op jit(solution)/shard_map/ppermute | solution.py:504
  30.7 14.2 %collective-permute-start.16 = (bf16[128,1024]{1,0:T(8,128)(2,1)S(1)}, bf16[128,1024]{1,0:T(8,128)(2,1)S(1)}, u32[]{:S(2)}, u32[]{:S(2)}) collective-permute-start(bf16[128,1024]{1,0:T(8,128)(2,1)S(1)} %shard_map.109), channel_id=1, source_target_pairs={{1,0},{0,1},{3,2},{2,3},{5,4},{4,5},{7,6},{6,7},{9,8},{8,9},{11,10... | collective-permute-start | bytes 786440 | tf_op jit(solution)/shard_map/ppermute | solution.py:504
  47.4 2.9 %collective-permute-start.19 = (bf16[256,256]{1,0:T(8,128)(2,1)S(1)}, bf16[256,256]{1,0:T(8,128)(2,1)S(1)}, u32[]{:S(2)}, u32[]{:S(2)}) collective-permute-start(bf16[256,256]{1,0:T(8,128)(2,1)S(1)} %get-tuple-element.56), channel_id=1, source_target_pairs={{4,0},{0,4},{12,8},{8,12},{20,16},{16,20},{28,24},{24,28},{5,1},{1... | collective-permute-start | bytes 393224 | tf_op jit(solution)/shard_map/ppermute | solution.py:514
  47.5 2.8 %collective-permute-start.18 = (bf16[256,256]{1,0:T(8,128)(2,1)S(1)}, bf16[256,256]{1,0:T(8,128)(2,1)S(1)}, u32[]{:S(2)}, u32[]{:S(2)}) collective-permute-start(bf16[256,256]{1,0:T(8,128)(2,1)S(1)} %get-tuple-element.54), channel_id=1, source_target_pairs={{4,0},{0,4},{12,8},{8,12},{20,16},{16,20},{28,24},{24,28},{5,1},{1... | collective-permute-start | bytes 393224 | tf_op jit(solution)/shard_map/ppermute | solution.py:514
  48.1 9.2 %collective-permute-start.7 = (bf16[128,1024]{1,0:T(8,128)(2,1)S(1)}, bf16[128,1024]{1,0:T(8,128)(2,1)S(1)}, u32[]{:S(2)}, u32[]{:S(2)}) collective-permute-start(bf16[128,1024]{1,0:T(8,128)(2,1)S(1)} %add.32), channel_id=1, source_target_pairs={{1,2},{2,1},{0,4},{3,7},{5,6},{6,5},{4,0},{7,3},{9,10},{10,9},{8,1... | collective-permute-start | bytes 786440 | tf_op jit(solution)/shard_map/ppermute | solution.py:507
  48.5 13.5 %collective-permute-start.10 = (bf16[128,1024]{1,0:T(8,128)(2,1)S(1)}, bf16[128,1024]{1,0:T(8,128)(2,1)S(1)}, u32[]{:S(2)}, u32[]{:S(2)}) collective-permute-start(bf16[128,1024]{1,0:T(8,128)(2,1)S(1)} %add.33), channel_id=1, source_target_pairs={{1,2},{2,1},{0,4},{3,7},{5,6},{6,5},{4,0},{7,3},{9,10},{10,9},{8,1... | collective-permute-start | bytes 786440 | tf_op jit(solution)/shard_map/ppermute | solution.py:507
  50.3 13.9 %collective-permute-start.21 = (bf16[256,256]{1,0:T(8,128)(2,1)S(1)}, bf16[256,256]{1,0:T(8,128)(2,1)S(1)}, u32[]{:S(2)}, u32[]{:S(2)}) collective-permute-start(bf16[256,256]{1,0:T(8,128)(2,1)S(1)} %get-tuple-element.63), channel_id=1, source_target_pairs={{16,0},{20,4},{24,8},{28,12},{0,16},{4,20},{8,24},{12,28},{17,1},{... | collective-permute-start | bytes 393224 | tf_op jit(solution)/shard_map/ppermute | solution.py:511
  51.9 14.0 %collective-permute-start.20 = (bf16[256,256]{1,0:T(8,128)(2,1)S(1)}, bf16[256,256]{1,0:T(8,128)(2,1)S(1)}, u32[]{:S(2)}, u32[]{:S(2)}) collective-permute-start(bf16[256,256]{1,0:T(8,128)(2,1)S(1)} %get-tuple-element.62), channel_id=1, source_target_pairs={{8,0},{12,4},{16,8},{20,12},{24,16},{28,20},{0,24},{4,28},{9,1},{1... | collective-permute-start | bytes 393224 | tf_op jit(solution)/shard_map/ppermute | solution.py:511
  57.3 9.3 %collective-permute-start.8 = (bf16[128,1024]{1,0:T(8,128)(2,1)S(1)}, bf16[128,1024]{1,0:T(8,128)(2,1)S(1)}, u32[]{:S(2)}, u32[]{:S(2)}) collective-permute-start(bf16[128,1024]{1,0:T(8,128)(2,1)S(1)} %shard_map.105), channel_id=1, source_target_pairs={{1,0},{0,1},{3,2},{2,3},{5,4},{4,5},{7,6},{6,7},{9,8},{8,9},{11,10... | collective-permute-start | bytes 786440 | tf_op jit(solution)/shard_map/ppermute | solution.py:504
  62.1 7.5 %collective-permute-start.11 = (bf16[128,1024]{1,0:T(8,128)(2,1)S(1)}, bf16[128,1024]{1,0:T(8,128)(2,1)S(1)}, u32[]{:S(2)}, u32[]{:S(2)}) collective-permute-start(bf16[128,1024]{1,0:T(8,128)(2,1)S(1)} %shard_map.107), channel_id=1, source_target_pairs={{1,0},{0,1},{3,2},{2,3},{5,4},{4,5},{7,6},{6,7},{9,8},{8,9},{11,10... | collective-permute-start | bytes 786440 | tf_op jit(solution)/shard_map/ppermute | solution.py:504
  62.2 9.2 %collective-permute-start.14 = (bf16[128,1024]{1,0:T(8,128)(2,1)S(1)}, bf16[128,1024]{1,0:T(8,128)(2,1)S(1)}, u32[]{:S(2)}, u32[]{:S(2)}) collective-permute-start(bf16[128,1024]{1,0:T(8,128)(2,1)S(1)} %add.34), channel_id=1, source_target_pairs={{1,2},{2,1},{0,4},{3,7},{5,6},{6,5},{4,0},{7,3},{9,10},{10,9},{8,1... | collective-permute-start | bytes 786440 | tf_op jit(solution)/shard_map/ppermute | solution.py:507
  64.3 11.1 %collective-permute-start.17 = (bf16[128,1024]{1,0:T(8,128)(2,1)S(1)}, bf16[128,1024]{1,0:T(8,128)(2,1)S(1)}, u32[]{:S(2)}, u32[]{:S(2)}) collective-permute-start(bf16[128,1024]{1,0:T(8,128)(2,1)S(1)} %add.35), channel_id=1, source_target_pairs={{1,2},{2,1},{0,4},{3,7},{5,6},{6,5},{4,0},{7,3},{9,10},{10,9},{8,1... | collective-permute-start | bytes 786440 | tf_op jit(solution)/shard_map/ppermute | solution.py:507
